TPU v7x, 128 devices: a whole 4x4x4 slice. The times are simulated.
128 devices in a mesh: cp: 32 (over y, z, core), ep: 4 (over x).
Axes of the slice: x: 4, y: 4, z: 4, core: 2. Of those that a mesh axis runs over, the one named last changes fastest.
Arguments:
- residual: bfloat16 [4096, 6144], P('cp'), may hold values from -90 to 90
- queries: bfloat16 [4096, 3072], P('cp', 'ep'), may hold values from -256 to 256
- key_proj: bfloat16 [4096, 512], P('cp', 'ep'), may hold values from -8 to 8
- value_proj: bfloat16 [4096, 512], P('cp', 'ep'), may hold values from -12 to 12
- out_weight: bfloat16 [3072, 6144], P('ep'), may hold values from -0.109375 to 0.109375
- norm_gain: float32 [6144], replicated, may hold values from 0.1 to 1.9
- doc_ids: int32 [4096], replicated, may hold values from 0 to 11, never falling along the last dimension, each value on 1 to 1024 neighbouring positions
- block_order: int32 [32], replicated, may hold values from 0 to 31, each once
- expert_ids: int32 [4096, 2], P('cp'), may hold values from 0 to 7, as said below
- route_logits: float32 [4096, 2], P('cp'), may hold values from -12 to 12
- gate_weight: bfloat16 [4, 6144, 8192], P('ep', None, 'cp'), may hold values from -0.078125 to 0.078125
- up_weight: bfloat16 [4, 6144, 8192], P('ep', None, 'cp'), may hold values from -0.078125 to 0.078125
- down_weight: bfloat16 [4, 8192, 6144], P('ep', 'cp'), may hold values from -0.0625 to 0.0625
Outputs:
- hidden_state: bfloat16 [4096, 6144], P('cp', 'ep')
- expert_mix: bfloat16 [4096, 6144], P('cp', 'ep')
Inputs may be any that keep to these rules, and one draw needn't show every extreme that they name: `expert_ids`: each row names two different experts; within the 128 rows of one cp index no expert is named by more than 40 rows. `doc_ids`: document numbers never fall along the sequence. `block_order`: each block number appears once.
All inputs are finite; a program needn't handle non-finite values.
Results may differ from a plain program's by a relative error of at most 0.02.
Values may be sent and summed in bfloat16 or wider, within the bound.
No kernel may reach another device: no remote copies, remote signals or barrier semaphores. Data moves between devices by JAX's collectives and lax.ppermute only.
A program may use at most 128 MiB of HBM per device.

v0:
```python
import math

import jax
import jax.numpy as jnp
from jax import lax
from jax.experimental import pallas as pl
from jax.experimental.pallas import tpu as pltpu
from jax.sharding import PartitionSpec as P


HD = 128
CAP = 40
EPS = 1e-05
NEG = -1e30
SIDE = 4
WINDOW = 9


def device_at(y, z, core):
    return ((y % SIDE) * SIDE + z % SIDE) * 2 + core % 2


def shifted(array, dy, dz, dcore=0):
    pairs = [
        (device_at(y, z, c), device_at(y + dy, z + dz, c + dcore))
        for y in range(SIDE)
        for z in range(SIDE)
        for c in range(2)
    ]
    return lax.ppermute(array, "cp", pairs)


def along(array, dim, step):
    return shifted(array, step, 0) if dim == "y" else shifted(array, 0, step)


def gather_line(array, dim):
    return [array] + [along(array, dim, step) for step in (1, 2, 3)]


def attention_kernel(
    rank_ref, order_ref, q_ref, own_ref, other_ref, docs_ref, weight_hbm, out_ref,
    kv_ref, bias_ref, attended_ref, weight_ref, sems,
):
    tokens = q_ref.shape[0]
    heads = q_ref.shape[1] // HD
    quarters, _, quarter = out_ref.shape

    def fetch(j):
        return pltpu.make_async_copy(
            weight_hbm.at[:, pl.ds(j * quarter, quarter)], weight_ref.at[j], sems.at[j]
        )

    for j in range(quarters):
        fetch(j).start()

    rank = rank_ref[0]
    core = rank % 2
    z = (rank // 2) % SIDE
    y = rank // (2 * SIDE)
    placed = order_ref[rank]
    first_block = placed - (WINDOW - 1)

    def place_from(source, slot_core):
        def place(in_half, carry):
            slot_y = (y + SIDE - in_half % SIDE) % SIDE
            slot_z = (z + SIDE - in_half // SIDE) % SIDE
            at = order_ref[(slot_y * SIDE + slot_z) * 2 + slot_core] - first_block

            @pl.when((at >= 0) & (at < WINDOW))
            def _():
                kv_ref[pl.ds(pl.multiple_of(at * tokens, tokens), tokens), :] = source[
                    pl.ds(pl.multiple_of(in_half * tokens, tokens), tokens), :
                ]

            return carry

        lax.fori_loop(0, SIDE * SIDE, place, 0)

    place_from(own_ref, core)
    place_from(other_ref, 1 - core)

    row_at = lax.broadcasted_iota(jnp.int32, (tokens, tokens), 0)
    key_at = lax.broadcasted_iota(jnp.int32, (tokens, tokens), 1)
    own_docs = docs_ref[pl.ds(placed, 1), :]
    row_docs = jnp.sum(jnp.where(row_at == key_at, own_docs, 0), axis=1, keepdims=True)

    def mask(w, carry):
        block = first_block + w
        at = pl.ds(pl.multiple_of(w * tokens, tokens), tokens)

        @pl.when(block < 0)
        def _():
            kv_ref[at, :] = jnp.zeros((tokens, 2 * HD), jnp.bfloat16)

        allowed = docs_ref[pl.ds(jnp.maximum(block, 0), 1), :] == row_docs
        reach = jnp.where(block < 0, -2 * WINDOW * tokens, (WINDOW - 1 - w) * tokens)
        allowed = allowed & (key_at <= row_at + reach)
        bias_ref[:, at] = jnp.where(allowed, 0.0, NEG)
        return carry

    lax.fori_loop(0, WINDOW, mask, 0)

    def head(h, carry):
        at = pl.ds(pl.multiple_of(h * HD, HD), HD)
        scores = lax.dot_general(
            q_ref[:, at], kv_ref[:, :HD], (((1,), (1,)), ((), ())), preferred_element_type=jnp.float32
        )
        scores = scores * (1.0 / math.sqrt(HD)) + bias_ref[...]
        weights = jnp.exp(scores - jnp.max(scores, axis=1, keepdims=True))
        total = jnp.sum(weights, axis=1, keepdims=True)
        mix = jnp.dot(
            weights.astype(jnp.bfloat16), kv_ref[:, HD:], preferred_element_type=jnp.float32
        )
        attended_ref[:, at] = (mix / total).astype(jnp.bfloat16)
        return carry

    lax.fori_loop(0, heads, head, 0)
    for j in range(quarters):
        fetch(j).wait()
        out_ref[j] = jnp.dot(
            attended_ref[...], weight_ref[j], preferred_element_type=jnp.float32
        ).astype(jnp.bfloat16)


def attend_and_project(rank, order, queries, own, other, docs, out_weight):
    tokens, inner = queries.shape
    quarter = out_weight.shape[1] // SIDE
    smem = pl.BlockSpec(memory_space=pltpu.SMEM)
    vmem = pl.BlockSpec(memory_space=pltpu.VMEM)
    return pl.pallas_call(
        attention_kernel,
        out_shape=jax.ShapeDtypeStruct((SIDE, tokens, quarter), jnp.bfloat16),
        in_specs=[smem, smem, vmem, vmem, vmem, vmem, pl.BlockSpec(memory_space=pltpu.HBM)],
        out_specs=vmem,
        scratch_shapes=[
            pltpu.VMEM((WINDOW * tokens, 2 * HD), jnp.bfloat16),
            pltpu.VMEM((tokens, WINDOW * tokens), jnp.float32),
            pltpu.VMEM((tokens, inner), jnp.bfloat16),
            pltpu.VMEM((SIDE, inner, quarter), jnp.bfloat16),
            pltpu.SemaphoreType.DMA((SIDE,)),
        ],
        compiler_params=pltpu.CompilerParams(vmem_limit_bytes=48 * 1024 * 1024),
        name="attention",
    )(rank, order, queries, own, other, docs, out_weight)


TILE = 256


def tiles(width, body):
    def step(n, carry):
        body(pl.ds(pl.multiple_of(n * TILE, TILE), TILE), n)
        return carry

    lax.fori_loop(0, width // TILE, step, 0)


def lift_groups(groups, weight_ref, sums_ref, lanes):
    rows = 2 * groups[0][1].shape[0]
    inner = groups[0][1].shape[1]

    def body(cols, n):
        for lane, (d, near_ref, far_ref) in zip(lanes, groups):
            x = jnp.concatenate([near_ref[...], far_ref[...]], axis=0)
            sums_ref[lane, d * rows : (d + 1) * rows, cols] = jnp.dot(
                x,
                weight_ref[lane * inner : (lane + 1) * inner, cols],
                preferred_element_type=jnp.float32,
            )

    tiles(weight_ref.shape[1], body)


EARLY = (0, 1, 3)
LAST = 2


def early_kernel(*refs):
    *pieces, weight_ref, sums_ref = refs
    groups, lanes = [], []
    for lane in range(2):
        for k, d in enumerate(EARLY):
            at = 2 * (lane * len(EARLY) + k)
            groups.append((d, pieces[at], pieces[at + 1]))
            lanes.append(lane)
    lift_groups(groups, weight_ref, sums_ref, lanes)


def lower_groups(hidden_refs, down_ref, outs):
    rows = hidden_refs[0].shape[0] // SIDE
    half = outs[0][2].shape[1]

    def body(cols, n):
        for lane, d, near_ref, far_ref in outs:
            x = hidden_refs[lane][d * rows : (d + 1) * rows, :].astype(jnp.bfloat16)
            w = down_ref[:, pl.ds(pl.multiple_of(lane * half + n * TILE, TILE), TILE)]
            y = jnp.dot(x, w, preferred_element_type=jnp.float32).astype(jnp.bfloat16)
            near_ref[:, cols] = y[: rows // 2]
            far_ref[:, cols] = y[rows // 2 :]

    tiles(half, body)


def last_kernel(
    a_near, a_far, b_near, b_far, weight_ref, early_ref, down_ref,
    hidden_a, hidden_b, a_out_near, a_out_far, b_out_near, b_out_far, late_ref,
):
    rows = 2 * a_near.shape[0]
    units = down_ref.shape[0]
    slots = rows // SIDE
    lift_groups(
        [(0, a_near, a_far), (0, b_near, b_far)], weight_ref, late_ref, (0, 1)
    )

    def combine(a_ref, a_base, b_ref, b_base, a_group, b_group):
        a_at = pl.ds(pl.multiple_of(a_base + b_group * slots, 8), slots)
        b_at = pl.ds(pl.multiple_of(b_base + a_group * slots, 8), slots)
        gate = a_ref[0, a_at, :units] + b_ref[1, b_at, :units]
        up = a_ref[0, a_at, units:] + b_ref[1, b_at, units:]
        value = gate / (1.0 + jnp.exp(-gate)) * up
        hidden_a[pl.ds(pl.multiple_of(a_group * rows + b_group * slots, 8), slots), :] = value
        hidden_b[pl.ds(pl.multiple_of(b_group * rows + a_group * slots, 8), slots), :] = value

    combine(late_ref, 0, late_ref, 0, LAST, LAST)

    def each(k, carry):
        d = jnp.where(k == LAST, SIDE - 1, k)
        combine(late_ref, 0, early_ref, d * rows, LAST, d)
        combine(early_ref, d * rows, late_ref, 0, d, LAST)

        def other(m, inner):
            e = jnp.where(m == LAST, SIDE - 1, m)
            combine(early_ref, d * rows, early_ref, e * rows, d, e)
            return inner

        return lax.fori_loop(0, SIDE - 1, other, carry)

    lax.fori_loop(0, SIDE - 1, each, 0)
    lower_groups(
        (hidden_a, hidden_b),
        down_ref,
        [(0, LAST, a_out_near, a_out_far), (1, LAST, b_out_near, b_out_far)],
    )


def rest_kernel(hidden_a, hidden_b, down_ref, *outs):
    groups = []
    for lane in range(2):
        for k, d in enumerate(EARLY):
            at = 2 * (lane * len(EARLY) + k)
            groups.append((lane, d, outs[at], outs[at + 1]))
    lower_groups((hidden_a, hidden_b), down_ref, groups)


def in_vmem(kernel, out_shapes, operands, scratch=()):
    vmem = pl.BlockSpec(memory_space=pltpu.VMEM)
    return pl.pallas_call(
        kernel,
        out_shape=out_shapes,
        in_specs=[vmem] * len(operands),
        out_specs=[vmem] * len(out_shapes),
        scratch_shapes=list(scratch),
        compiler_params=pltpu.CompilerParams(vmem_limit_bytes=12 * 1024 * 1024),
    )(*operands)


def expert_parts(a_groups, b_groups, gate_up, down):
    piece = a_groups[0][0]
    rows = 2 * piece.shape[0]
    units, _ = down.shape
    early = [p for groups in (a_groups, b_groups) for d in EARLY for p in groups[d]]
    sums = jax.ShapeDtypeStruct((2, SIDE * rows, gate_up.shape[1]), jnp.float32)
    (early_sums,) = in_vmem(early_kernel, [sums], [*early, gate_up])
    hidden = jax.ShapeDtypeStruct((SIDE * rows, units), jnp.float32)
    part = jax.ShapeDtypeStruct(piece.shape, jnp.bfloat16)
    hidden_a, hidden_b, *first = in_vmem(
        last_kernel,
        [hidden, hidden] + [part] * 4,
        [*a_groups[LAST], *b_groups[LAST], gate_up, early_sums, down],
        [pltpu.VMEM((2, rows, gate_up.shape[1]), jnp.float32)],
    )
    rest = in_vmem(rest_kernel, [part] * (4 * len(EARLY)), [hidden_a, hidden_b, down])
    pieces = [[None] * SIDE, [None] * SIDE]
    for lane in range(2):
        pieces[lane][LAST] = (first[2 * lane], first[2 * lane + 1])
        for k, d in enumerate(EARLY):
            at = 2 * (lane * len(EARLY) + k)
            pieces[lane][d] = (rest[at], rest[at + 1])
    return pieces


def gather_ring(near, far, dim):
    up_near = along(near, dim, 1)
    down_far = along(far, dim, -1)
    up_far = along(far, dim, 1)
    down_near = along(near, dim, -1)
    two_near = along(up_near, dim, 1)
    two_far = along(down_far, dim, -1)
    return [(near, far), (up_near, up_far), (two_near, two_far), (down_near, down_far)]


def plus(*arrays):
    total = arrays[0].astype(jnp.float32)
    for a in arrays[1:]:
        total = total + a.astype(jnp.float32)
    return total.astype(jnp.bfloat16)


def scatter_ring(pieces, dim):
    near2 = along(pieces[2][0], dim, -1)
    far2 = along(pieces[2][1], dim, 1)
    far1 = along(pieces[1][1], dim, -1)
    near3 = along(pieces[3][0], dim, 1)
    near1 = along(plus(pieces[1][0], near2), dim, -1)
    far3 = along(plus(pieces[3][1], far2), dim, 1)
    near = plus(pieces[0][0], near3, near1)
    far = plus(pieces[0][1], far1, far3)
    return near, far


def scatter_line(near, far, dim):
    rows = near.shape[0] // 2
    pieces = [near[:rows], near[rows:], far[:rows], far[rows:]]
    moved = [along(pieces[step], dim, -step) for step in (1, 2, 3)]
    return plus(pieces[0], *moved)


def local(
    residual,
    queries,
    key_proj,
    value_proj,
    out_weight,
    norm_gain,
    doc_ids,
    block_order,
    expert_ids,
    route_logits,
    gate_weight,
    up_weight,
    down_weight,
):
    tokens, width = residual.shape
    quarter = width // SIDE
    cp_rank = lax.axis_index("cp")
    ep_rank = lax.axis_index("ep")

    gate_other = shifted(gate_weight[0], 0, 0, 1)
    up_other = shifted(up_weight[0], 0, 0, 1)
    down_other = shifted(down_weight[0], 0, 0, 1)

    kv = jnp.concatenate([key_proj, value_proj], axis=1)
    kv_line = jnp.concatenate(gather_line(kv, "y"), axis=0)
    kv_own = jnp.concatenate(gather_line(kv_line, "z"), axis=0)
    kv_other = shifted(kv_own, 0, 0, 1)

    projected = attend_and_project(
        cp_rank.reshape(1).astype(jnp.int32),
        block_order,
        queries,
        kv_own,
        kv_other,
        doc_ids.reshape(-1, tokens),
        out_weight,
    )
    gate_up = jnp.concatenate([gate_weight[0], gate_other, up_weight[0], up_other], axis=1)
    down = jnp.concatenate([down_weight[0], down_other], axis=0)
    arrived = lax.all_to_all(projected, "ep", split_axis=0, concat_axis=0, tiled=True)
    arrived, gate_up, down = lax.optimization_barrier((arrived, gate_up, down))
    own_residual = lax.dynamic_slice_in_dim(residual, ep_rank * quarter, quarter, 1)
    hidden_state = (
        own_residual.astype(jnp.float32) + arrived.astype(jnp.float32).sum(axis=0)
    ).astype(jnp.bfloat16)

    experts = jnp.arange(SIDE, dtype=jnp.int32)
    logit_gap = route_logits[:, 1] - route_logits[:, 0]
    first_share = 1.0 / (1.0 + jnp.exp(logit_gap))
    second_share = 1.0 / (1.0 + jnp.exp(-logit_gap))
    names_first = expert_ids[:, 0][:, None] == experts[None, :]
    names_second = expert_ids[:, 1][:, None] == experts[None, :]
    member = (names_first | names_second).astype(jnp.int32)
    slot_index = jnp.cumsum(member, axis=0) - member
    share = jnp.where(names_first, first_share[:, None], 0.0) + jnp.where(
        names_second, second_share[:, None], 0.0
    )
    slot_ids = jnp.arange(CAP, dtype=jnp.int32)
    placed_at = (slot_index[:, :, None] == slot_ids[None, None, :]) & (member[:, :, None] == 1)
    selector = placed_at.astype(jnp.bfloat16).reshape(tokens, SIDE * CAP)
    mix_weight = jnp.where(placed_at, share[:, :, None], 0.0).reshape(tokens, SIDE * CAP)

    rows = lax.dot_general(
        selector, hidden_state, (((0,), (0,)), ((), ())), preferred_element_type=jnp.float32
    ).astype(jnp.bfloat16)
    rows = lax.all_to_all(
        rows.reshape(SIDE, CAP, quarter), "ep", split_axis=0, concat_axis=0, tiled=True
    )
    wide = rows.astype(jnp.float32)
    mean_square = jnp.sum(wide * wide, axis=(0, 2), keepdims=True) / width
    gain = norm_gain.reshape(SIDE, 1, quarter)
    packed = (wide * lax.rsqrt(mean_square + EPS) * gain).astype(jnp.bfloat16)
    first = jnp.concatenate([packed[0], packed[1]], axis=1)
    second = jnp.concatenate([packed[2], packed[3]], axis=1)

    first_line = gather_line(first, "y")
    second_line = gather_line(second, "z")
    first_all = gather_ring(
        jnp.concatenate(first_line[:2], axis=0), jnp.concatenate(first_line[2:], axis=0), "z"
    )
    second_all = gather_ring(
        jnp.concatenate(second_line[:2], axis=0), jnp.concatenate(second_line[2:], axis=0), "y"
    )

    a_parts, b_parts = expert_parts(first_all, second_all, gate_up, down)
    sum_first = scatter_line(*scatter_ring(a_parts, "z"), "y")
    sum_second = scatter_line(*scatter_ring(b_parts, "y"), "z")
    back = jnp.stack(
        [sum_first[:, :quarter], sum_first[:, quarter:], sum_second[:, :quarter], sum_second[:, quarter:]]
    )
    back = lax.all_to_all(back, "ep", split_axis=0, concat_axis=0, tiled=True)
    back = back.reshape(SIDE * CAP, quarter)
    high = mix_weight.astype(jnp.bfloat16)
    low = (mix_weight - high.astype(jnp.float32)).astype(jnp.bfloat16)
    mixed = jnp.dot(high, back, preferred_element_type=jnp.float32) + jnp.dot(
        low, back, preferred_element_type=jnp.float32
    )
    return (hidden_state, mixed.astype(jnp.bfloat16))


def solution(mesh):
    return jax.shard_map(
        local,
        mesh=mesh,
        in_specs=(
            P("cp", None),
            P("cp", "ep"),
            P("cp", "ep"),
            P("cp", "ep"),
            P("ep", None),
            P(),
            P(),
            P(),
            P("cp", None),
            P("cp", None),
            P("ep", None, "cp"),
            P("ep", None, "cp"),
            P("ep", "cp", None),
        ),
        out_specs=(P("cp", "ep"), P("cp", "ep")),
        check_vma=False,
    )
```

profile of v0, /device:TPU:0, one launch (start us, length us, event | category | flops | bytes accessed | tf_op | source)
XLA Modules:
  0.0 247.6 jit_solution(12473411008275063204)
XLA Ops:
  2.9 1.8 collective-permute-start
  4.6 2.9 %collective-permute-start.1 = (bf16[128,256]{1,0:T(8,128)(2,1)S(1)}, bf16[128,256]{1,0:T(8,128)(2,1)S(1)}, u32[]{:S(2)}, u32[]{:S(2)}) collective-permute-start(bf16[128,256]{1,0:T(8,128)(2,1)S(1)} %get-tuple-element.56), channel_id=1, source_target_pairs={{0,64},{4,68},{8,72},{12,76},{16,80},{20,84},{24,88},{28,92},{32,9... | collective-permute-start | bytes 196616 | tf_op jit(solution)/shard_map/ppermute | solution.py:30
  7.5 1.2 collective-permute-done
  8.7 2.3 collective-permute-start.2
  11.3 1.7 collective-permute-done.2
  13.0 2.0 collective-permute-start.3
  15.0 3.6 %collective-permute-start.4 = (bf16[512,256]{1,0:T(8,128)(2,1)S(1)}, bf16[512,256]{1,0:T(8,128)(2,1)S(1)}, u32[]{:S(2)}, u32[]{:S(2)}) collective-permute-start(bf16[512,256]{1,0:T(8,128)(2,1)S(1)} %pad_maximum_fusion.5), channel_id=1, source_target_pairs={{0,16},{4,20},{8,24},{12,28},{16,0},{20,4},{24,8},{28,12},{32,48},... | collective-permute-start | bytes 786440 | tf_op jit(solution)/shard_map/ppermute | solution.py:30
  18.6 4.8 %collective-permute-done.3 = bf16[512,256]{1,0:T(8,128)(2,1)S(1)} collective-permute-done((bf16[512,256]{1,0:T(8,128)(2,1)S(1)}, bf16[512,256]{1,0:T(8,128)(2,1)S(1)}, u32[]{:S(2)}, u32[]{:S(2)}) %collective-permute-start.3) | collective-permute-done | bytes 262176 | tf_op jit(solution)/shard_map/ppermute | solution.py:30
  23.4 2.9 %collective-permute-start.5 = (bf16[512,256]{1,0:T(8,128)(2,1)S(1)}, bf16[512,256]{1,0:T(8,128)(2,1)S(1)}, u32[]{:S(2)}, u32[]{:S(2)}) collective-permute-start(bf16[512,256]{1,0:T(8,128)(2,1)S(1)} %pad_maximum_fusion.5), channel_id=1, source_target_pairs={{0,24},{4,28},{8,0},{12,4},{16,8},{20,12},{24,16},{28,20},{32,56},... | collective-permute-start | bytes 786440 | tf_op jit(solution)/shard_map/ppermute | solution.py:30
  26.3 2.5 %collective-permute-done.4 = bf16[512,256]{1,0:T(8,128)(2,1)S(1)} collective-permute-done((bf16[512,256]{1,0:T(8,128)(2,1)S(1)}, bf16[512,256]{1,0:T(8,128)(2,1)S(1)}, u32[]{:S(2)}, u32[]{:S(2)}) %collective-permute-start.4) | collective-permute-done | bytes 262176 | tf_op jit(solution)/shard_map/ppermute | solution.py:30
  28.9 2.2 collective-permute-done.5
  32.8 1.1 collective-permute-done.6.other_ref
  33.9 0.9 copy-done.3
  36.2 8.6 %attention.1 = bf16[4,128,1536]{2,1,0:T(8,128)(2,1)} custom-call(s32[1]{0:T(128)} %bitcast.rank_ref, s32[32]{0:T(128)S(1)} %copy-done.5, bf16[128,768]{1,0:T(8,128)(2,1)S(1)} %copy-done.3, bf16[2048,256]{1,0:T(8,128)(2,1)S(1)} %constant_dynamic-update-slice_fusion.2.own_ref, bf16[2048,256]{1,0:T(8,128)(2,1)S(1)} %collective-permute-done.6.other_ref, ...), custom_call_target="tpu_custom_call" | custom-call | tf_op jit(solution)/shard_map/attention/pallas_call | solution.py:131
  44.8 4.3 %all-to-all-start = ((bf16[4,128,1536]{2,1,0:T(8,128)(2,1)}), bf16[4,128,1536]{2,1,0:T(8,128)(2,1)S(1)}, u32[]{:S(2)}, u32[]{:S(2)}) async-start(bf16[4,128,1536]{2,1,0:T(8,128)(2,1)} %attention.1), calls=%async_computation | async-start | bytes 3145728 | tf_op jit(solution)/shard_map/all_to_all | solution.py:369
  49.1 6.3 %pad_maximum_fusion.1.down_ref = bf16[512,6144]{1,0:T(8,128)(2,1)} fusion(bf16[256,6144]{1,0:T(8,128)(2,1)} %collective-permute-done.9, bf16[256,6144]{1,0:T(8,128)(2,1)} %bitcast.54), kind=kLoop, calls=%fused_computation.1 | loop fusion | flops 12582912 | bytes 12582912 | tf_op jit(solution)/shard_map/concatenate | solution.py:368
  55.4 8.6 %pad_maximum_fusion.refs_12_.weight_ref = bf16[6144,1024]{1,0:T(8,128)(2,1)} fusion(bf16[6144,256]{1,0:T(8,128)(2,1)} %collective-permute-done.8, bf16[6144,256]{1,0:T(8,128)(2,1)S(1)} %bitcast.50, bf16[6144,256]{1,0:T(8,128)(2,1)} %collective-permute-done.7, bf16[6144,256]{1,0:T(8,128)(2,1)S(1)} %bitcast.52), kind=kLoop, calls=%fused_computation | loop fusion | flops 50331648 | bytes 25165824 | tf_op jit(solution)/shard_map/concatenate | solution.py:367
  64.1 6.0 %all-to-all-done = bf16[4,128,1536]{2,1,0:T(8,128)(2,1)S(1)} async-done(((bf16[4,128,1536]{2,1,0:T(8,128)(2,1)}), bf16[4,128,1536]{2,1,0:T(8,128)(2,1)S(1)}, u32[]{:S(2)}, u32[]{:S(2)}) %all-to-all-start) | async-done | bytes 1572896 | tf_op jit(solution)/shard_map/all_to_all | solution.py:369
  70.3 1.1 add_convert_fusion.8
  71.4 1.1 convolution_convert_fusion
  72.5 3.5 %all-to-all-start.1 = ((bf16[4,40,1536]{2,1,0:T(8,128)(2,1)}), bf16[4,40,1536]{2,1,0:T(8,128)(2,1)S(1)}, u32[]{:S(2)}, u32[]{:S(2)}) async-start(bf16[4,40,1536]{2,1,0:T(8,128)(2,1)} %bitcast.11), calls=%async_computation.1 | async-start | bytes 983040 | tf_op jit(solution)/shard_map/all_to_all | solution.py:395
  76.0 8.5 %all-to-all-done.1 = bf16[4,40,1536]{2,1,0:T(8,128)(2,1)S(1)} async-done(((bf16[4,40,1536]{2,1,0:T(8,128)(2,1)}), bf16[4,40,1536]{2,1,0:T(8,128)(2,1)S(1)}, u32[]{:S(2)}, u32[]{:S(2)}) %all-to-all-start.1) | async-done | bytes 491552 | tf_op jit(solution)/shard_map/all_to_all | solution.py:395
  85.0 4.6 %collective-permute-start.20 = (bf16[40,3072]{1,0:T(8,128)(2,1)S(1)}, bf16[40,3072]{1,0:T(8,128)(2,1)S(1)}, u32[]{:S(2)}, u32[]{:S(2)}) collective-permute-start(bf16[40,3072]{1,0:T(8,128)(2,1)S(1)} %pad_maximum_fusion.7), channel_id=1, source_target_pairs={{0,16},{4,20},{8,24},{12,28},{16,0},{20,4},{24,8},{28,12},{32,48},... | collective-permute-start | bytes 737288 | tf_op jit(solution)/shard_map/ppermute | solution.py:30
  90.2 1.4 collective-permute-start.17
  91.6 2.0 collective-permute-start.13
  93.7 1.7 collective-permute-start.14
  95.3 1.0 collective-permute-done.20
  96.3 0.9 collective-permute-start.10
  97.7 3.2 %collective-permute-start.22 = (bf16[80,3072]{1,0:T(8,128)(2,1)S(1)}, bf16[80,3072]{1,0:T(8,128)(2,1)S(1)}, u32[]{:S(2)}, u32[]{:S(2)}) collective-permute-start(bf16[80,3072]{1,0:T(8,128)(2,1)S(1)} %constant_dynamic-update-slice_fusion.12.refs_7_), channel_id=1, source_target_pairs={{0,96},{4,100},{8,104},{12,108},{16,112},{20,116},{24,120},{28,124... | collective-permute-start | bytes 1474568 | tf_op jit(solution)/shard_map/ppermute | solution.py:30
  101.1 1.9 collective-permute-start.18
  103.0 4.7 %collective-permute-done.14 = bf16[40,3072]{1,0:T(8,128)(2,1)S(1)} collective-permute-done((bf16[40,3072]{1,0:T(8,128)(2,1)S(1)}, bf16[40,3072]{1,0:T(8,128)(2,1)S(1)}, u32[]{:S(2)}, u32[]{:S(2)}) %collective-permute-start.14) | collective-permute-done | bytes 245792 | tf_op jit(solution)/shard_map/ppermute | solution.py:30
  107.9 1.9 collective-permute-start.15
  109.8 8.4 %collective-permute-done.22.refs_11_ = bf16[80,3072]{1,0:T(8,128)(2,1)S(1)} collective-permute-done((bf16[80,3072]{1,0:T(8,128)(2,1)S(1)}, bf16[80,3072]{1,0:T(8,128)(2,1)S(1)}, u32[]{:S(2)}, u32[]{:S(2)}) %collective-permute-start.22) | collective-permute-done | bytes 491552 | tf_op jit(solution)/shard_map/ppermute | solution.py:30
  118.3 6.6 %collective-permute-done.18.refs_8_ = bf16[80,3072]{1,0:T(8,128)(2,1)S(1)} collective-permute-done((bf16[80,3072]{1,0:T(8,128)(2,1)S(1)}, bf16[80,3072]{1,0:T(8,128)(2,1)S(1)}, u32[]{:S(2)}, u32[]{:S(2)}) %collective-permute-start.18) | collective-permute-done | bytes 491552 | tf_op jit(solution)/shard_map/ppermute | solution.py:30
  124.8 2.0 collective-permute-start.25
  126.9 1.3 collective-permute-start.23
  128.9 2.6 %collective-permute-done.24.refs_3_ = bf16[80,3072]{1,0:T(8,128)(2,1)S(1)} collective-permute-done((bf16[80,3072]{1,0:T(8,128)(2,1)S(1)}, bf16[80,3072]{1,0:T(8,128)(2,1)S(1)}, u32[]{:S(2)}, u32[]{:S(2)}) %collective-permute-start.24) | collective-permute-done | bytes 491552 | tf_op jit(solution)/shard_map/ppermute | solution.py:30
  132.1 8.1 %collective-permute-done.11.refs_2_ = bf16[80,3072]{1,0:T(8,128)(2,1)S(1)} collective-permute-done((bf16[80,3072]{1,0:T(8,128)(2,1)S(1)}, bf16[80,3072]{1,0:T(8,128)(2,1)S(1)}, u32[]{:S(2)}, u32[]{:S(2)}) %collective-permute-start.11) | collective-permute-done | bytes 491552 | tf_op jit(solution)/shard_map/ppermute | solution.py:30
  140.2 4.6 %copy-done = bf16[6144,1024]{1,0:T(8,128)(2,1)S(1)} copy-done((bf16[6144,1024]{1,0:T(8,128)(2,1)S(1)}, bf16[6144,1024]{1,0:T(8,128)(2,1)}, u32[]{:S(2)}) %copy-start) | copy-done | bytes 12582936
  144.8 7.1 %shard_map.140.early_ref = f32[2,640,1024]{2,1,0:T(8,128)S(1)} custom-call(bf16[80,3072]{1,0:T(8,128)(2,1)S(1)} %pad_maximum_fusion.2.refs_0_, bf16[80,3072]{1,0:T(8,128)(2,1)S(1)} %constant_dynamic-update-slice_fusion.10.refs_1_, bf16[80,3072]{1,0:T(8,128)(2,1)S(1)} %collective-permute-done.11.refs_2_, ...), custom_call_target="tpu_custom_call" | custom-call | tf_op jit(solution)/shard_map/pallas_call | solution.py:258
  151.9 6.8 %shard_map.141 = (f32[640,512]{1,0:T(8,128)S(1)}, f32[640,512]{1,0:T(8,128)S(1)}, bf16[80,3072]{1,0:T(8,128)(2,1)S(1)}, bf16[80,3072]{1,0:T(8,128)(2,1)S(1)}, bf...) custom-call(bf16[80,3072]{1,0:T(8,128)(2,1)S(1)} %collective-permute-done.12.a_near, ...), custom_call_target="tpu_custom_call" | custom-call | tf_op jit(solution)/shard_map/pallas_call | solution.py:258
  158.7 3.3 %collective-permute-start.29 = (bf16[80,3072]{1,0:T(8,128)(2,1)S(1)}, bf16[80,3072]{1,0:T(8,128)(2,1)S(1)}, u32[]{:S(2)}, u32[]{:S(2)}) collective-permute-start(bf16[80,3072]{1,0:T(8,128)(2,1)S(1)} %get-tuple-element.31), channel_id=1, source_target_pairs={{0,24},{4,28},{8,0},{12,4},{16,8},{20,12},{24,16},{28,20},{32,56},... | collective-permute-start | bytes 1474568 | tf_op jit(solution)/shard_map/ppermute | solution.py:30
  162.0 5.5 %shard_map.142 = (bf16[80,3072]{1,0:T(8,128)(2,1)S(1)}, bf16[80,3072]{1,0:T(8,128)(2,1)S(1)}, bf16[80,3072]{1,0:T(8,128)(2,1)S(1)}, bf16[80,3072]{1,0:T(8,128)(2...) custom-call(f32[640,512]{1,0:T(8,128)S(1)} %get-tuple-element.26.hid, ...), custom_call_target="tpu_custom_call" | custom-call | tf_op jit(solution)/shard_map/pallas_call | solution.py:258
  167.7 3.2 %collective-permute-start.32 = (bf16[80,3072]{1,0:T(8,128)(2,1)S(1)}, bf16[80,3072]{1,0:T(8,128)(2,1)S(1)}, u32[]{:S(2)}, u32[]{:S(2)}) collective-permute-start(bf16[80,3072]{1,0:T(8,128)(2,1)S(1)} %get-tuple-element.33), channel_id=1, source_target_pairs={{0,24},{4,28},{8,0},{12,4},{16,8},{20,12},{24,16},{28,20},{32,56},... | collective-permute-start | bytes 1474568 | tf_op jit(solution)/shard_map/ppermute | solution.py:30
  171.2 1.8 collective-permute-done.29
  173.1 11.1 %collective-permute-done.33 = bf16[80,3072]{1,0:T(8,128)(2,1)S(1)} collective-permute-done((bf16[80,3072]{1,0:T(8,128)(2,1)S(1)}, bf16[80,3072]{1,0:T(8,128)(2,1)S(1)}, u32[]{:S(2)}, u32[]{:S(2)}) %collective-permute-start.33) | collective-permute-done | bytes 491552 | tf_op jit(solution)/shard_map/ppermute | solution.py:30
  184.2 1.9 collective-permute-start.42
  186.2 2.5 %collective-permute-start.41 = (bf16[80,3072]{1,0:T(8,128)(2,1)S(1)}, bf16[80,3072]{1,0:T(8,128)(2,1)S(1)}, u32[]{:S(2)}, u32[]{:S(2)}) collective-permute-start(bf16[80,3072]{1,0:T(8,128)(2,1)S(1)} %get-tuple-element.41), channel_id=1, source_target_pairs={{0,96},{4,100},{8,104},{12,108},{16,112},{20,116},{24,120},{28,124... | collective-permute-start | bytes 1474568 | tf_op jit(solution)/shard_map/ppermute | solution.py:30
  188.8 6.5 %collective-permute-done.42 = bf16[80,3072]{1,0:T(8,128)(2,1)S(1)} collective-permute-done((bf16[80,3072]{1,0:T(8,128)(2,1)S(1)}, bf16[80,3072]{1,0:T(8,128)(2,1)S(1)}, u32[]{:S(2)}, u32[]{:S(2)}) %collective-permute-start.42) | collective-permute-done | bytes 491552 | tf_op jit(solution)/shard_map/ppermute | solution.py:30
  195.3 2.0 collective-permute-start.30
  197.5 7.3 %collective-permute-done.30 = bf16[80,3072]{1,0:T(8,128)(2,1)S(1)} collective-permute-done((bf16[80,3072]{1,0:T(8,128)(2,1)S(1)}, bf16[80,3072]{1,0:T(8,128)(2,1)S(1)}, u32[]{:S(2)}, u32[]{:S(2)}) %collective-permute-start.30) | collective-permute-done | bytes 491552 | tf_op jit(solution)/shard_map/ppermute | solution.py:30
  204.8 1.4 collective-permute-start.39
  207.1 1.3 collective-permute-done.34
  208.4 1.3 collective-permute-start.31
  210.0 8.9 %collective-permute-done.39 = bf16[80,3072]{1,0:T(8,128)(2,1)S(1)} collective-permute-done((bf16[80,3072]{1,0:T(8,128)(2,1)S(1)}, bf16[80,3072]{1,0:T(8,128)(2,1)S(1)}, u32[]{:S(2)}, u32[]{:S(2)}) %collective-permute-start.39) | collective-permute-done | bytes 491552 | tf_op jit(solution)/shard_map/ppermute | solution.py:30
  219.1 3.8 %collective-permute-start.40 = (bf16[40,3072]{1,0:T(8,128)(2,1)S(1)}, bf16[40,3072]{1,0:T(8,128)(2,1)S(1)}, u32[]{:S(2)}, u32[]{:S(2)}) collective-permute-start(bf16[40,3072]{1,0:T(8,128)(2,1)S(1)} %slice.97), channel_id=1, source_target_pairs={{0,24},{4,28},{8,0},{12,4},{16,8},{20,12},{24,16},{28,20},{32,56},... | collective-permute-start | bytes 737288 | tf_op jit(solution)/shard_map/ppermute | solution.py:30
  223.5 2.6 %collective-permute-start.44 = (bf16[40,3072]{1,0:T(8,128)(2,1)S(1)}, bf16[40,3072]{1,0:T(8,128)(2,1)S(1)}, u32[]{:S(2)}, u32[]{:S(2)}) collective-permute-start(bf16[40,3072]{1,0:T(8,128)(2,1)S(1)} %get-tuple-element.46), channel_id=1, source_target_pairs={{0,16},{4,20},{8,24},{12,28},{16,0},{20,4},{24,8},{28,12},{32,48},... | collective-permute-start | bytes 737288 | tf_op jit(solution)/shard_map/ppermute | solution.py:30
  226.1 2.1 collective-permute-start.45
  228.3 3.0 %collective-permute-done.44 = bf16[40,3072]{1,0:T(8,128)(2,1)S(1)} collective-permute-done((bf16[40,3072]{1,0:T(8,128)(2,1)S(1)}, bf16[40,3072]{1,0:T(8,128)(2,1)S(1)}, u32[]{:S(2)}, u32[]{:S(2)}) %collective-permute-start.44) | collective-permute-done | bytes 245792 | tf_op jit(solution)/shard_map/ppermute | solution.py:30
  231.3 2.6 %collective-permute-done.45 = bf16[40,3072]{1,0:T(8,128)(2,1)S(1)} collective-permute-done((bf16[40,3072]{1,0:T(8,128)(2,1)S(1)}, bf16[40,3072]{1,0:T(8,128)(2,1)S(1)}, u32[]{:S(2)}, u32[]{:S(2)}) %collective-permute-start.45) | collective-permute-done | bytes 245792 | tf_op jit(solution)/shard_map/ppermute | solution.py:30
  234.1 0.9 pad_maximum_fusion.4
  235.0 3.5 %all-to-all-start.2 = ((bf16[4,40,1536]{2,1,0:T(8,128)(2,1)}), bf16[4,40,1536]{2,1,0:T(8,128)(2,1)S(1)}, u32[]{:S(2)}, u32[]{:S(2)}) async-start(bf16[4,40,1536]{2,1,0:T(8,128)(2,1)} %pad_maximum_fusion.4), calls=%async_computation.2 | async-start | bytes 983040 | tf_op jit(solution)/shard_map/all_to_all | solution.py:420
  238.7 7.6 %all-to-all-done.2 = bf16[4,40,1536]{2,1,0:T(8,128)(2,1)S(1)} async-done(((bf16[4,40,1536]{2,1,0:T(8,128)(2,1)}), bf16[4,40,1536]{2,1,0:T(8,128)(2,1)S(1)}, u32[]{:S(2)}, u32[]{:S(2)}) %all-to-all-start.2) | async-done | bytes 491552 | tf_op jit(solution)/shard_map/all_to_all | solution.py:420
  246.6 1.0 fusion.1
  (118 shorter events, 13.1 us)
Async XLA Ops:
  0.6 48.5 %collective-permute-start.9 = (bf16[256,6144]{1,0:T(8,128)(2,1)}, bf16[256,6144]{1,0:T(8,128)(2,1)}, u32[]{:S(2)}, u32[]{:S(2)}) collective-permute-start(bf16[256,6144]{1,0:T(8,128)(2,1)} %bitcast.53), channel_id=1, source_target_pairs={{0,4},{4,0},{8,12},{12,8},{16,20},{20,16},{24,28},{28,24},{32,36},... | collective-permute-start | bytes 9437192 | tf_op jit(solution)/shard_map/ppermute | solution.py:30
  0.7 54.7 %collective-permute-start.7 = (bf16[6144,256]{1,0:T(8,128)(2,1)}, bf16[6144,256]{1,0:T(8,128)(2,1)}, u32[]{:S(2)}, u32[]{:S(2)}) collective-permute-start(bf16[6144,256]{1,0:T(8,128)(2,1)} %bitcast.51), channel_id=1, source_target_pairs={{0,4},{4,0},{8,12},{12,8},{16,20},{20,16},{24,28},{28,24},{32,36},... | collective-permute-start | bytes 9437192 | tf_op jit(solution)/shard_map/ppermute | solution.py:30
  1.2 54.2 %collective-permute-start.8 = (bf16[6144,256]{1,0:T(8,128)(2,1)}, bf16[6144,256]{1,0:T(8,128)(2,1)}, u32[]{:S(2)}, u32[]{:S(2)}) collective-permute-start(bf16[6144,256]{1,0:T(8,128)(2,1)} %bitcast.49), channel_id=1, source_target_pairs={{0,4},{4,0},{8,12},{12,8},{16,20},{20,16},{24,28},{28,24},{32,36},... | collective-permute-start | bytes 9437192 | tf_op jit(solution)/shard_map/ppermute | solution.py:30
  2.9 5.9 %collective-permute-start = (bf16[128,256]{1,0:T(8,128)(2,1)S(1)}, bf16[128,256]{1,0:T(8,128)(2,1)S(1)}, u32[]{:S(2)}, u32[]{:S(2)}) collective-permute-start(bf16[128,256]{1,0:T(8,128)(2,1)S(1)} %get-tuple-element.56), channel_id=1, source_target_pairs={{0,32},{4,36},{8,40},{12,44},{16,48},{20,52},{24,56},{28,60},{32,6... | collective-permute-start | bytes 196616 | tf_op jit(solution)/shard_map/ppermute | solution.py:30
  4.6 6.7 %collective-permute-start.1 = (bf16[128,256]{1,0:T(8,128)(2,1)S(1)}, bf16[128,256]{1,0:T(8,128)(2,1)S(1)}, u32[]{:S(2)}, u32[]{:S(2)}) collective-permute-start(bf16[128,256]{1,0:T(8,128)(2,1)S(1)} %get-tuple-element.56), channel_id=1, source_target_pairs={{0,64},{4,68},{8,72},{12,76},{16,80},{20,84},{24,88},{28,92},{32,9... | collective-permute-start | bytes 196616 | tf_op jit(solution)/shard_map/ppermute | solution.py:30
  8.7 4.3 %collective-permute-start.2 = (bf16[128,256]{1,0:T(8,128)(2,1)S(1)}, bf16[128,256]{1,0:T(8,128)(2,1)S(1)}, u32[]{:S(2)}, u32[]{:S(2)}) collective-permute-start(bf16[128,256]{1,0:T(8,128)(2,1)S(1)} %get-tuple-element.56), channel_id=1, source_target_pairs={{0,96},{4,100},{8,104},{12,108},{16,112},{20,116},{24,120},{28,124... | collective-permute-start | bytes 196616 | tf_op jit(solution)/shard_map/ppermute | solution.py:30
  13.0 10.4 %collective-permute-start.3 = (bf16[512,256]{1,0:T(8,128)(2,1)S(1)}, bf16[512,256]{1,0:T(8,128)(2,1)S(1)}, u32[]{:S(2)}, u32[]{:S(2)}) collective-permute-start(bf16[512,256]{1,0:T(8,128)(2,1)S(1)} %pad_maximum_fusion.5), channel_id=1, source_target_pairs={{0,8},{4,12},{8,16},{12,20},{16,24},{20,28},{24,0},{28,4},{32,40},... | collective-permute-start | bytes 786440 | tf_op jit(solution)/shard_map/ppermute | solution.py:30
  15.0 13.9 %collective-permute-start.4 = (bf16[512,256]{1,0:T(8,128)(2,1)S(1)}, bf16[512,256]{1,0:T(8,128)(2,1)S(1)}, u32[]{:S(2)}, u32[]{:S(2)}) collective-permute-start(bf16[512,256]{1,0:T(8,128)(2,1)S(1)} %pad_maximum_fusion.5), channel_id=1, source_target_pairs={{0,16},{4,20},{8,24},{12,28},{16,0},{20,4},{24,8},{28,12},{32,48},... | collective-permute-start | bytes 786440 | tf_op jit(solution)/shard_map/ppermute | solution.py:30
  23.4 7.7 %collective-permute-start.5 = (bf16[512,256]{1,0:T(8,128)(2,1)S(1)}, bf16[512,256]{1,0:T(8,128)(2,1)S(1)}, u32[]{:S(2)}, u32[]{:S(2)}) collective-permute-start(bf16[512,256]{1,0:T(8,128)(2,1)S(1)} %pad_maximum_fusion.5), channel_id=1, source_target_pairs={{0,24},{4,28},{8,0},{12,4},{16,8},{20,12},{24,16},{28,20},{32,56},... | collective-permute-start | bytes 786440 | tf_op jit(solution)/shard_map/ppermute | solution.py:30
  31.2 2.7 %collective-permute-start.6 = (bf16[2048,256]{1,0:T(8,128)(2,1)S(1)}, bf16[2048,256]{1,0:T(8,128)(2,1)S(1)}, u32[]{:S(2)}, u32[]{:S(2)}) collective-permute-start(bf16[2048,256]{1,0:T(8,128)(2,1)S(1)} %constant_dynamic-update-slice_fusion.2.own_ref), channel_id=1, source_target_pairs={{0,4},{4,0},{8,12},{12,8},{16,20},{20,16},{24,28},{28,24},{32,36},... | collective-permute-start | bytes 3145736 | tf_op jit(solution)/shard_map/ppermute | solution.py:30
  33.9 0.9 copy-start.3
  34.8 0.7 copy-start.4
  35.5 0.7 copy-start.5
  44.8 25.3 %all-to-all-start = ((bf16[4,128,1536]{2,1,0:T(8,128)(2,1)}), bf16[4,128,1536]{2,1,0:T(8,128)(2,1)S(1)}, u32[]{:S(2)}, u32[]{:S(2)}) async-start(bf16[4,128,1536]{2,1,0:T(8,128)(2,1)} %attention.1), calls=%async_computation | async-start | bytes 3145728 | tf_op jit(solution)/shard_map/all_to_all | solution.py:369
  49.1 6.3 %copy-start.6 = (bf16[1,6144,256]{2,1,0:T(8,128)(2,1)S(1)}, bf16[1,6144,256]{2,1,0:T(8,128)(2,1)}, u32[]{:S(2)}) copy-start(bf16[1,6144,256]{2,1,0:T(8,128)(2,1)} %param.24) | copy-start | bytes 9437188
  49.1 6.4 %copy-start.7 = (bf16[1,6144,256]{2,1,0:T(8,128)(2,1)S(1)}, bf16[1,6144,256]{2,1,0:T(8,128)(2,1)}, u32[]{:S(2)}) copy-start(bf16[1,6144,256]{2,1,0:T(8,128)(2,1)} %param.23) | copy-start | bytes 9437188
  55.4 20.6 %copy-start.9 = (f32[6144]{0:T(1024)S(1)}, f32[6144]{0:T(1024)}, u32[]{:S(2)}) copy-start(f32[6144]{0:T(1024)} %param.18) | copy-start | bytes 73732
  71.4 80.4 %copy-start.8 = (bf16[128,1536]{1,0:T(8,128)(2,1)}, bf16[128,1536]{1,0:T(8,128)(2,1)S(1)}, u32[]{:S(2)}) copy-start(bf16[128,1536]{1,0:T(8,128)(2,1)S(1)} %add_convert_fusion.8) | copy-start | bytes 1179652
  72.5 12.0 %all-to-all-start.1 = ((bf16[4,40,1536]{2,1,0:T(8,128)(2,1)}), bf16[4,40,1536]{2,1,0:T(8,128)(2,1)S(1)}, u32[]{:S(2)}, u32[]{:S(2)}) async-start(bf16[4,40,1536]{2,1,0:T(8,128)(2,1)} %bitcast.11), calls=%async_computation.1 | async-start | bytes 983040 | tf_op jit(solution)/shard_map/all_to_all | solution.py:395
  85.0 11.3 %collective-permute-start.20 = (bf16[40,3072]{1,0:T(8,128)(2,1)S(1)}, bf16[40,3072]{1,0:T(8,128)(2,1)S(1)}, u32[]{:S(2)}, u32[]{:S(2)}) collective-permute-start(bf16[40,3072]{1,0:T(8,128)(2,1)S(1)} %pad_maximum_fusion.7), channel_id=1, source_target_pairs={{0,16},{4,20},{8,24},{12,28},{16,0},{20,4},{24,8},{28,12},{32,48},... | collective-permute-start | bytes 737288 | tf_op jit(solution)/shard_map/ppermute | solution.py:30
  89.6 8.1 %collective-permute-start.21 = (bf16[40,3072]{1,0:T(8,128)(2,1)S(1)}, bf16[40,3072]{1,0:T(8,128)(2,1)S(1)}, u32[]{:S(2)}, u32[]{:S(2)}) collective-permute-start(bf16[40,3072]{1,0:T(8,128)(2,1)S(1)} %pad_maximum_fusion.7), channel_id=1, source_target_pairs={{0,24},{4,28},{8,0},{12,4},{16,8},{20,12},{24,16},{28,20},{32,56},... | collective-permute-start | bytes 737288 | tf_op jit(solution)/shard_map/ppermute | solution.py:30
  90.2 10.7 %collective-permute-start.17 = (bf16[40,3072]{1,0:T(8,128)(2,1)S(1)}, bf16[40,3072]{1,0:T(8,128)(2,1)S(1)}, u32[]{:S(2)}, u32[]{:S(2)}) collective-permute-start(bf16[40,3072]{1,0:T(8,128)(2,1)S(1)} %pad_maximum_fusion.7), channel_id=1, source_target_pairs={{0,8},{4,12},{8,16},{12,20},{16,24},{20,28},{24,0},{28,4},{32,40},... | collective-permute-start | bytes 737288 | tf_op jit(solution)/shard_map/ppermute | solution.py:30
  91.6 9.5 %collective-permute-start.13 = (bf16[40,3072]{1,0:T(8,128)(2,1)S(1)}, bf16[40,3072]{1,0:T(8,128)(2,1)S(1)}, u32[]{:S(2)}, u32[]{:S(2)}) collective-permute-start(bf16[40,3072]{1,0:T(8,128)(2,1)S(1)} %pad_maximum_fusion.6), channel_id=1, source_target_pairs={{0,64},{4,68},{8,72},{12,76},{16,80},{20,84},{24,88},{28,92},{32,9... | collective-permute-start | bytes 737288 | tf_op jit(solution)/shard_map/ppermute | solution.py:30
  93.7 14.0 %collective-permute-start.14 = (bf16[40,3072]{1,0:T(8,128)(2,1)S(1)}, bf16[40,3072]{1,0:T(8,128)(2,1)S(1)}, u32[]{:S(2)}, u32[]{:S(2)}) collective-permute-start(bf16[40,3072]{1,0:T(8,128)(2,1)S(1)} %pad_maximum_fusion.6), channel_id=1, source_target_pairs={{0,96},{4,100},{8,104},{12,108},{16,112},{20,116},{24,120},{28,124... | collective-permute-start | bytes 737288 | tf_op jit(solution)/shard_map/ppermute | solution.py:30
  96.3 11.6 %collective-permute-start.10 = (bf16[40,3072]{1,0:T(8,128)(2,1)S(1)}, bf16[40,3072]{1,0:T(8,128)(2,1)S(1)}, u32[]{:S(2)}, u32[]{:S(2)}) collective-permute-start(bf16[40,3072]{1,0:T(8,128)(2,1)S(1)} %pad_maximum_fusion.6), channel_id=1, source_target_pairs={{0,32},{4,36},{8,40},{12,44},{16,48},{20,52},{24,56},{28,60},{32,6... | collective-permute-start | bytes 737288 | tf_op jit(solution)/shard_map/ppermute | solution.py:30
  97.7 20.5 %collective-permute-start.22 = (bf16[80,3072]{1,0:T(8,128)(2,1)S(1)}, bf16[80,3072]{1,0:T(8,128)(2,1)S(1)}, u32[]{:S(2)}, u32[]{:S(2)}) collective-permute-start(bf16[80,3072]{1,0:T(8,128)(2,1)S(1)} %constant_dynamic-update-slice_fusion.12.refs_7_), channel_id=1, source_target_pairs={{0,96},{4,100},{8,104},{12,108},{16,112},{20,116},{24,120},{28,124... | collective-permute-start | bytes 1474568 | tf_op jit(solution)/shard_map/ppermute | solution.py:30
  100.9 17.3 %collective-permute-start.26 = (bf16[80,3072]{1,0:T(8,128)(2,1)S(1)}, bf16[80,3072]{1,0:T(8,128)(2,1)S(1)}, u32[]{:S(2)}, u32[]{:S(2)}) collective-permute-start(bf16[80,3072]{1,0:T(8,128)(2,1)S(1)} %constant_dynamic-update-slice_fusion.12.refs_7_), channel_id=1, source_target_pairs={{0,32},{4,36},{8,40},{12,44},{16,48},{20,52},{24,56},{28,60},{32,6... | collective-permute-start | bytes 1474568 | tf_op jit(solution)/shard_map/ppermute | solution.py:30
  101.1 23.7 %collective-permute-start.18 = (bf16[80,3072]{1,0:T(8,128)(2,1)S(1)}, bf16[80,3072]{1,0:T(8,128)(2,1)S(1)}, u32[]{:S(2)}, u32[]{:S(2)}) collective-permute-start(bf16[80,3072]{1,0:T(8,128)(2,1)S(1)} %pad_maximum_fusion.3.refs_6_), channel_id=1, source_target_pairs={{0,32},{4,36},{8,40},{12,44},{16,48},{20,52},{24,56},{28,60},{32,6... | collective-permute-start | bytes 1474568 | tf_op jit(solution)/shard_map/ppermute | solution.py:30
  107.7 19.1 %collective-permute-start.27 = (bf16[80,3072]{1,0:T(8,128)(2,1)S(1)}, bf16[80,3072]{1,0:T(8,128)(2,1)S(1)}, u32[]{:S(2)}, u32[]{:S(2)}) collective-permute-start(bf16[80,3072]{1,0:T(8,128)(2,1)S(1)} %pad_maximum_fusion.3.refs_6_), channel_id=1, source_target_pairs={{0,96},{4,100},{8,104},{12,108},{16,112},{20,116},{24,120},{28,124... | collective-permute-start | bytes 1474568 | tf_op jit(solution)/shard_map/ppermute | solution.py:30
  107.9 20.2 %collective-permute-start.15 = (bf16[80,3072]{1,0:T(8,128)(2,1)S(1)}, bf16[80,3072]{1,0:T(8,128)(2,1)S(1)}, u32[]{:S(2)}, u32[]{:S(2)}) collective-permute-start(bf16[80,3072]{1,0:T(8,128)(2,1)S(1)} %constant_dynamic-update-slice_fusion.10.refs_1_), channel_id=1, source_target_pairs={{0,24},{4,28},{8,0},{12,4},{16,8},{20,12},{24,16},{28,20},{32,56},... | collective-permute-start | bytes 1474568 | tf_op jit(solution)/shard_map/ppermute | solution.py:30
  118.2 13.2 %collective-permute-start.24 = (bf16[80,3072]{1,0:T(8,128)(2,1)S(1)}, bf16[80,3072]{1,0:T(8,128)(2,1)S(1)}, u32[]{:S(2)}, u32[]{:S(2)}) collective-permute-start(bf16[80,3072]{1,0:T(8,128)(2,1)S(1)} %constant_dynamic-update-slice_fusion.10.refs_1_), channel_id=1, source_target_pairs={{0,8},{4,12},{8,16},{12,20},{16,24},{20,28},{24,0},{28,4},{32,40},... | collective-permute-start | bytes 1474568 | tf_op jit(solution)/shard_map/ppermute | solution.py:30
  118.3 21.9 %collective-permute-start.11 = (bf16[80,3072]{1,0:T(8,128)(2,1)S(1)}, bf16[80,3072]{1,0:T(8,128)(2,1)S(1)}, u32[]{:S(2)}, u32[]{:S(2)}) collective-permute-start(bf16[80,3072]{1,0:T(8,128)(2,1)S(1)} %pad_maximum_fusion.2.refs_0_), channel_id=1, source_target_pairs={{0,8},{4,12},{8,16},{12,20},{16,24},{20,28},{24,0},{28,4},{32,40},... | collective-permute-start | bytes 1474568 | tf_op jit(solution)/shard_map/ppermute | solution.py:30
  124.8 15.4 %collective-permute-start.25 = (bf16[80,3072]{1,0:T(8,128)(2,1)S(1)}, bf16[80,3072]{1,0:T(8,128)(2,1)S(1)}, u32[]{:S(2)}, u32[]{:S(2)}) collective-permute-start(bf16[80,3072]{1,0:T(8,128)(2,1)S(1)} %pad_maximum_fusion.2.refs_0_), channel_id=1, source_target_pairs={{0,24},{4,28},{8,0},{12,4},{16,8},{20,12},{24,16},{28,20},{32,56},... | collective-permute-start | bytes 1474568 | tf_op jit(solution)/shard_map/ppermute | solution.py:30
  126.9 25.0 %collective-permute-start.23 = (bf16[80,3072]{1,0:T(8,128)(2,1)S(1)}, bf16[80,3072]{1,0:T(8,128)(2,1)S(1)}, u32[]{:S(2)}, u32[]{:S(2)}) collective-permute-start(bf16[80,3072]{1,0:T(8,128)(2,1)S(1)} %collective-permute-done.22.refs_11_), channel_id=1, source_target_pairs={{0,96},{4,100},{8,104},{12,108},{16,112},{20,116},{24,120},{28,124... | collective-permute-start | bytes 1474568 | tf_op jit(solution)/shard_map/ppermute | solution.py:30
  128.1 23.7 %collective-permute-start.19 = (bf16[80,3072]{1,0:T(8,128)(2,1)S(1)}, bf16[80,3072]{1,0:T(8,128)(2,1)S(1)}, u32[]{:S(2)}, u32[]{:S(2)}) collective-permute-start(bf16[80,3072]{1,0:T(8,128)(2,1)S(1)} %collective-permute-done.18.refs_8_), channel_id=1, source_target_pairs={{0,32},{4,36},{8,40},{12,44},{16,48},{20,52},{24,56},{28,60},{32,6... | collective-permute-start | bytes 1474568 | tf_op jit(solution)/shard_map/ppermute | solution.py:30
  131.5 20.4 %collective-permute-start.16 = (bf16[80,3072]{1,0:T(8,128)(2,1)S(1)}, bf16[80,3072]{1,0:T(8,128)(2,1)S(1)}, u32[]{:S(2)}, u32[]{:S(2)}) collective-permute-start(bf16[80,3072]{1,0:T(8,128)(2,1)S(1)} %collective-permute-done.15.refs_5_), channel_id=1, source_target_pairs={{0,24},{4,28},{8,0},{12,4},{16,8},{20,12},{24,16},{28,20},{32,56},... | collective-permute-start | bytes 1474568 | tf_op jit(solution)/shard_map/ppermute | solution.py:30
  140.2 11.7 %collective-permute-start.12 = (bf16[80,3072]{1,0:T(8,128)(2,1)S(1)}, bf16[80,3072]{1,0:T(8,128)(2,1)S(1)}, u32[]{:S(2)}, u32[]{:S(2)}) collective-permute-start(bf16[80,3072]{1,0:T(8,128)(2,1)S(1)} %collective-permute-done.11.refs_2_), channel_id=1, source_target_pairs={{0,8},{4,12},{8,16},{12,20},{16,24},{20,28},{24,0},{28,4},{32,40},... | collective-permute-start | bytes 1474568 | tf_op jit(solution)/shard_map/ppermute | solution.py:30
  140.2 4.6 %copy-start = (bf16[6144,1024]{1,0:T(8,128)(2,1)S(1)}, bf16[6144,1024]{1,0:T(8,128)(2,1)}, u32[]{:S(2)}) copy-start(bf16[6144,1024]{1,0:T(8,128)(2,1)} %pad_maximum_fusion.refs_12_.weight_ref) | copy-start | bytes 37748740
  144.8 7.1 %copy-start.1 = (bf16[6144,1024]{1,0:T(8,128)(2,1)S(1)}, bf16[6144,1024]{1,0:T(8,128)(2,1)}, u32[]{:S(2)}) copy-start(bf16[6144,1024]{1,0:T(8,128)(2,1)} %pad_maximum_fusion.refs_12_.weight_ref) | copy-start | bytes 37748740
  144.8 7.1 %copy-start.2 = (bf16[512,6144]{1,0:T(8,128)(2,1)S(1)}, bf16[512,6144]{1,0:T(8,128)(2,1)}, u32[]{:S(2)}) copy-start(bf16[512,6144]{1,0:T(8,128)(2,1)} %pad_maximum_fusion.1.down_ref) | copy-start | bytes 18874372
  158.7 14.2 %collective-permute-start.29 = (bf16[80,3072]{1,0:T(8,128)(2,1)S(1)}, bf16[80,3072]{1,0:T(8,128)(2,1)S(1)}, u32[]{:S(2)}, u32[]{:S(2)}) collective-permute-start(bf16[80,3072]{1,0:T(8,128)(2,1)S(1)} %get-tuple-element.31), channel_id=1, source_target_pairs={{0,24},{4,28},{8,0},{12,4},{16,8},{20,12},{24,16},{28,20},{32,56},... | collective-permute-start | bytes 1474568 | tf_op jit(solution)/shard_map/ppermute | solution.py:30
  167.5 29.8 %collective-permute-start.28 = (bf16[80,3072]{1,0:T(8,128)(2,1)S(1)}, bf16[80,3072]{1,0:T(8,128)(2,1)S(1)}, u32[]{:S(2)}, u32[]{:S(2)}) collective-permute-start(bf16[80,3072]{1,0:T(8,128)(2,1)S(1)} %get-tuple-element.29), channel_id=1, source_target_pairs={{0,8},{4,12},{8,16},{12,20},{16,24},{20,28},{24,0},{28,4},{32,40},... | collective-permute-start | bytes 1474568 | tf_op jit(solution)/shard_map/ppermute | solution.py:30
  167.6 16.5 %collective-permute-start.33 = (bf16[80,3072]{1,0:T(8,128)(2,1)S(1)}, bf16[80,3072]{1,0:T(8,128)(2,1)S(1)}, u32[]{:S(2)}, u32[]{:S(2)}) collective-permute-start(bf16[80,3072]{1,0:T(8,128)(2,1)S(1)} %get-tuple-element.35), channel_id=1, source_target_pairs={{0,8},{4,12},{8,16},{12,20},{16,24},{20,28},{24,0},{28,4},{32,40},... | collective-permute-start | bytes 1474568 | tf_op jit(solution)/shard_map/ppermute | solution.py:30
  167.7 38.6 %collective-permute-start.32 = (bf16[80,3072]{1,0:T(8,128)(2,1)S(1)}, bf16[80,3072]{1,0:T(8,128)(2,1)S(1)}, u32[]{:S(2)}, u32[]{:S(2)}) collective-permute-start(bf16[80,3072]{1,0:T(8,128)(2,1)S(1)} %get-tuple-element.33), channel_id=1, source_target_pairs={{0,24},{4,28},{8,0},{12,4},{16,8},{20,12},{24,16},{28,20},{32,56},... | collective-permute-start | bytes 1474568 | tf_op jit(solution)/shard_map/ppermute | solution.py:30
  170.9 15.2 %collective-permute-start.38 = (bf16[80,3072]{1,0:T(8,128)(2,1)S(1)}, bf16[80,3072]{1,0:T(8,128)(2,1)S(1)}, u32[]{:S(2)}, u32[]{:S(2)}) collective-permute-start(bf16[80,3072]{1,0:T(8,128)(2,1)S(1)} %get-tuple-element.39), channel_id=1, source_target_pairs={{0,96},{4,100},{8,104},{12,108},{16,112},{20,116},{24,120},{28,124... | collective-permute-start | bytes 1474568 | tf_op jit(solution)/shard_map/ppermute | solution.py:30
  173.0 36.9 %collective-permute-start.37 = (bf16[80,3072]{1,0:T(8,128)(2,1)S(1)}, bf16[80,3072]{1,0:T(8,128)(2,1)S(1)}, u32[]{:S(2)}, u32[]{:S(2)}) collective-permute-start(bf16[80,3072]{1,0:T(8,128)(2,1)S(1)} %get-tuple-element.37), channel_id=1, source_target_pairs={{0,32},{4,36},{8,40},{12,44},{16,48},{20,52},{24,56},{28,60},{32,6... | collective-permute-start | bytes 1474568 | tf_op jit(solution)/shard_map/ppermute | solution.py:30
  184.2 11.1 %collective-permute-start.42 = (bf16[80,3072]{1,0:T(8,128)(2,1)S(1)}, bf16[80,3072]{1,0:T(8,128)(2,1)S(1)}, u32[]{:S(2)}, u32[]{:S(2)}) collective-permute-start(bf16[80,3072]{1,0:T(8,128)(2,1)S(1)} %get-tuple-element.43), channel_id=1, source_target_pairs={{0,32},{4,36},{8,40},{12,44},{16,48},{20,52},{24,56},{28,60},{32,6... | collective-permute-start | bytes 1474568 | tf_op jit(solution)/shard_map/ppermute | solution.py:30
  186.2 32.9 %collective-permute-start.41 = (bf16[80,3072]{1,0:T(8,128)(2,1)S(1)}, bf16[80,3072]{1,0:T(8,128)(2,1)S(1)}, u32[]{:S(2)}, u32[]{:S(2)}) collective-permute-start(bf16[80,3072]{1,0:T(8,128)(2,1)S(1)} %get-tuple-element.41), channel_id=1, source_target_pairs={{0,96},{4,100},{8,104},{12,108},{16,112},{20,116},{24,120},{28,124... | collective-permute-start | bytes 1474568 | tf_op jit(solution)/shard_map/ppermute | solution.py:30
  195.3 9.5 %collective-permute-start.30 = (bf16[80,3072]{1,0:T(8,128)(2,1)S(1)}, bf16[80,3072]{1,0:T(8,128)(2,1)S(1)}, u32[]{:S(2)}, u32[]{:S(2)}) collective-permute-start(bf16[80,3072]{1,0:T(8,128)(2,1)S(1)} %add_convert_fusion.7), channel_id=1, source_target_pairs={{0,24},{4,28},{8,0},{12,4},{16,8},{20,12},{24,16},{28,20},{32,56},... | collective-permute-start | bytes 1474568 | tf_op jit(solution)/shard_map/ppermute | solution.py:30
  197.4 11.0 %collective-permute-start.34 = (bf16[80,3072]{1,0:T(8,128)(2,1)S(1)}, bf16[80,3072]{1,0:T(8,128)(2,1)S(1)}, u32[]{:S(2)}, u32[]{:S(2)}) collective-permute-start(bf16[80,3072]{1,0:T(8,128)(2,1)S(1)} %add_convert_fusion.5), channel_id=1, source_target_pairs={{0,8},{4,12},{8,16},{12,20},{16,24},{20,28},{24,0},{28,4},{32,40},... | collective-permute-start | bytes 1474568 | tf_op jit(solution)/shard_map/ppermute | solution.py:30
  204.8 14.1 %collective-permute-start.39 = (bf16[80,3072]{1,0:T(8,128)(2,1)S(1)}, bf16[80,3072]{1,0:T(8,128)(2,1)S(1)}, u32[]{:S(2)}, u32[]{:S(2)}) collective-permute-start(bf16[80,3072]{1,0:T(8,128)(2,1)S(1)} %add_convert_fusion.3), channel_id=1, source_target_pairs={{0,96},{4,100},{8,104},{12,108},{16,112},{20,116},{24,120},{28,124... | collective-permute-start | bytes 1474568 | tf_op jit(solution)/shard_map/ppermute | solution.py:30
  206.3 17.0 %collective-permute-start.43 = (bf16[80,3072]{1,0:T(8,128)(2,1)S(1)}, bf16[80,3072]{1,0:T(8,128)(2,1)S(1)}, u32[]{:S(2)}, u32[]{:S(2)}) collective-permute-start(bf16[80,3072]{1,0:T(8,128)(2,1)S(1)} %add_convert_fusion.1), channel_id=1, source_target_pairs={{0,32},{4,36},{8,40},{12,44},{16,48},{20,52},{24,56},{28,60},{32,6... | collective-permute-start | bytes 1474568 | tf_op jit(solution)/shard_map/ppermute | solution.py:30
  208.4 17.7 %collective-permute-start.31 = (bf16[40,3072]{1,0:T(8,128)(2,1)S(1)}, bf16[40,3072]{1,0:T(8,128)(2,1)S(1)}, u32[]{:S(2)}, u32[]{:S(2)}) collective-permute-start(bf16[40,3072]{1,0:T(8,128)(2,1)S(1)} %slice.91), channel_id=1, source_target_pairs={{0,96},{4,100},{8,104},{12,108},{16,112},{20,116},{24,120},{28,124... | collective-permute-start | bytes 737288 | tf_op jit(solution)/shard_map/ppermute | solution.py:30
  209.8 28.6 %copy-start.10 = (f32[128,2]{0,1:T(2,128)S(1)}, f32[128,2]{0,1:T(2,128)}, u32[]{:S(2)}) copy-start(f32[128,2]{0,1:T(2,128)} %param.22) | copy-start | bytes 3076
  209.9 18.3 %collective-permute-start.35 = (bf16[40,3072]{1,0:T(8,128)(2,1)S(1)}, bf16[40,3072]{1,0:T(8,128)(2,1)S(1)}, u32[]{:S(2)}, u32[]{:S(2)}) collective-permute-start(bf16[40,3072]{1,0:T(8,128)(2,1)S(1)} %get-tuple-element.44), channel_id=1, source_target_pairs={{0,64},{4,68},{8,72},{12,76},{16,80},{20,84},{24,88},{28,92},{32,9... | collective-permute-start | bytes 737288 | tf_op jit(solution)/shard_map/ppermute | solution.py:30
  218.8 9.3 %collective-permute-start.36 = (bf16[40,3072]{1,0:T(8,128)(2,1)S(1)}, bf16[40,3072]{1,0:T(8,128)(2,1)S(1)}, u32[]{:S(2)}, u32[]{:S(2)}) collective-permute-start(bf16[40,3072]{1,0:T(8,128)(2,1)S(1)} %get-tuple-element.45), channel_id=1, source_target_pairs={{0,32},{4,36},{8,40},{12,44},{16,48},{20,52},{24,56},{28,60},{32,6... | collective-permute-start | bytes 737288 | tf_op jit(solution)/shard_map/ppermute | solution.py:30
  219.1 9.2 %collective-permute-start.40 = (bf16[40,3072]{1,0:T(8,128)(2,1)S(1)}, bf16[40,3072]{1,0:T(8,128)(2,1)S(1)}, u32[]{:S(2)}, u32[]{:S(2)}) collective-permute-start(bf16[40,3072]{1,0:T(8,128)(2,1)S(1)} %slice.97), channel_id=1, source_target_pairs={{0,24},{4,28},{8,0},{12,4},{16,8},{20,12},{24,16},{28,20},{32,56},... | collective-permute-start | bytes 737288 | tf_op jit(solution)/shard_map/ppermute | solution.py:30
  223.5 7.8 %collective-permute-start.44 = (bf16[40,3072]{1,0:T(8,128)(2,1)S(1)}, bf16[40,3072]{1,0:T(8,128)(2,1)S(1)}, u32[]{:S(2)}, u32[]{:S(2)}) collective-permute-start(bf16[40,3072]{1,0:T(8,128)(2,1)S(1)} %get-tuple-element.46), channel_id=1, source_target_pairs={{0,16},{4,20},{8,24},{12,28},{16,0},{20,4},{24,8},{28,12},{32,48},... | collective-permute-start | bytes 737288 | tf_op jit(solution)/shard_map/ppermute | solution.py:30
  226.1 7.9 %collective-permute-start.45 = (bf16[40,3072]{1,0:T(8,128)(2,1)S(1)}, bf16[40,3072]{1,0:T(8,128)(2,1)S(1)}, u32[]{:S(2)}, u32[]{:S(2)}) collective-permute-start(bf16[40,3072]{1,0:T(8,128)(2,1)S(1)} %get-tuple-element.47), channel_id=1, source_target_pairs={{0,8},{4,12},{8,16},{12,20},{16,24},{20,28},{24,0},{28,4},{32,40},... | collective-permute-start | bytes 737288 | tf_op jit(solution)/shard_map/ppermute | solution.py:30
  235.0 11.3 %all-to-all-start.2 = ((bf16[4,40,1536]{2,1,0:T(8,128)(2,1)}), bf16[4,40,1536]{2,1,0:T(8,128)(2,1)S(1)}, u32[]{:S(2)}, u32[]{:S(2)}) async-start(bf16[4,40,1536]{2,1,0:T(8,128)(2,1)} %pad_maximum_fusion.4), calls=%async_computation.2 | async-start | bytes 983040 | tf_op jit(solution)/shard_map/all_to_all | solution.py:420
where the time goes:
time: 248 us
  waiting for transfers between devices  111 us (45%)
  starting transfers between devices  75.8 us (31%)
  Pallas kernels  27.9 us (11%)
  other arithmetic  19.7 us (8%)
  local copies, waits for them, and re-layouts  9.85 us (4%)
    ppermute x46, waiting for transfers between devices, shifted(): return lax.ppermute(array, 'cp', pairs)  88.6 us
    ppermute x46, starting transfers between devices, shifted(): return lax.ppermute(array, 'cp', pairs)  64.6 us
    pallas_call x3, Pallas kernels, in_vmem(): pl.pallas_call(kernel, out_shape=out_shapes, in_specs=[vmem] * len(operan...  19.4 us
    concatenate x1, other arithmetic, local(): jnp.concatenate([gate_weight[0], gate_other, up_weight[0], up_other], axi...  8.62 us
    pallas_call x1, Pallas kernels, attend_and_project(): pl.pallas_call(attention_kernel, out_shape=jax.ShapeDtypeStruct((SIDE, to...  8.57 us
    all_to_all x1, waiting for transfers between devices, local(): lax.all_to_all(rows.reshape(SIDE, CAP, quarter), 'ep', split_axis=0, conc...  8.51 us
    unnamed x30, local copies, waits for them, and re-layouts  7.76 us
    all_to_all x1, waiting for transfers between devices, local(): back = lax.all_to_all(back, 'ep', split_axis=0, concat_axis=0, tiled=True)  7.64 us
  transfers between devices with their start and end apart: 49, of which 27 were waited for; matrix products, arithmetic and copies ran while one was open for 8% of the time, Pallas kernels for 9%

commit v1 on v0

--- a/solution.py
+++ b/solution.py
@@ -31,6 +31,8 @@
 
 
 def along(array, dim, step):
+    if dim == "x":
+        return lax.ppermute(array, "ep", [(i, (i + step) % SIDE) for i in range(SIDE)])
     return shifted(array, step, 0) if dim == "y" else shifted(array, 0, step)
 
 
@@ -39,20 +41,25 @@
 
 
 def attention_kernel(
-    rank_ref, order_ref, q_ref, own_ref, other_ref, docs_ref, weight_hbm, out_ref,
-    kv_ref, bias_ref, attended_ref, weight_ref, sems,
+    rank_ref, order_ref, q_hbm, own_ref, other_ref, docs_hbm, weight_hbm, *rest
 ):
+    *outs, q_ref, docs_ref, kv_ref, bias_ref, attended_ref, weight_ref, sems = rest
     tokens = q_ref.shape[0]
     heads = q_ref.shape[1] // HD
-    quarters, _, quarter = out_ref.shape
-
-    def fetch(j):
+    quarter = weight_ref.shape[2]
+
+    def fetch(d):
+        at = ((rank_ref[1] + SIDE - d) % SIDE) * quarter
         return pltpu.make_async_copy(
-            weight_hbm.at[:, pl.ds(j * quarter, quarter)], weight_ref.at[j], sems.at[j]
+            weight_hbm.at[:, pl.ds(pl.multiple_of(at, HD), quarter)], weight_ref.at[d], sems.at[d]
         )
 
-    for j in range(quarters):
-        fetch(j).start()
+    docs_copy = pltpu.make_async_copy(docs_hbm, docs_ref, sems.at[SIDE])
+    q_copy = pltpu.make_async_copy(q_hbm, q_ref, sems.at[SIDE + 1])
+    docs_copy.start()
+    q_copy.start()
+    for d in range(SIDE):
+        fetch(d).start()
 
     rank = rank_ref[0]
     core = rank % 2
@@ -80,6 +87,7 @@
     place_from(own_ref, core)
     place_from(other_ref, 1 - core)
 
+    docs_copy.wait()
     row_at = lax.broadcasted_iota(jnp.int32, (tokens, tokens), 0)
     key_at = lax.broadcasted_iota(jnp.int32, (tokens, tokens), 1)
     own_docs = docs_ref[pl.ds(placed, 1), :]
@@ -100,6 +108,7 @@
         return carry
 
     lax.fori_loop(0, WINDOW, mask, 0)
+    q_copy.wait()
 
     def head(h, carry):
         at = pl.ds(pl.multiple_of(h * HD, HD), HD)
@@ -116,36 +125,43 @@
         return carry
 
     lax.fori_loop(0, heads, head, 0)
-    for j in range(quarters):
-        fetch(j).wait()
-        out_ref[j] = jnp.dot(
-            attended_ref[...], weight_ref[j], preferred_element_type=jnp.float32
-        ).astype(jnp.bfloat16)
-
-
-def attend_and_project(rank, order, queries, own, other, docs, out_weight):
+    for d in range(SIDE):
+        fetch(d).wait()
+        part = jnp.dot(attended_ref[...], weight_ref[d], preferred_element_type=jnp.float32)
+        part = part.astype(jnp.bfloat16)
+        outs[2 * d][...] = part[: tokens // 2]
+        outs[2 * d + 1][...] = part[tokens // 2 :]
+
+
+def attend_and_project(ranks, order, queries, own, other, docs, out_weight):
     tokens, inner = queries.shape
     quarter = out_weight.shape[1] // SIDE
     smem = pl.BlockSpec(memory_space=pltpu.SMEM)
     vmem = pl.BlockSpec(memory_space=pltpu.VMEM)
-    return pl.pallas_call(
+    far = pl.BlockSpec(memory_space=pltpu.HBM)
+    queries, docs, out_weight = in_hbm([queries, docs, out_weight])
+    outs = pl.pallas_call(
         attention_kernel,
-        out_shape=jax.ShapeDtypeStruct((SIDE, tokens, quarter), jnp.bfloat16),
-        in_specs=[smem, smem, vmem, vmem, vmem, vmem, pl.BlockSpec(memory_space=pltpu.HBM)],
-        out_specs=vmem,
+        out_shape=[jax.ShapeDtypeStruct((tokens // 2, quarter), jnp.bfloat16)] * (2 * SIDE),
+        in_specs=[smem, smem, far, vmem, vmem, far, far],
+        out_specs=[vmem] * (2 * SIDE),
         scratch_shapes=[
+            pltpu.VMEM(queries.shape, queries.dtype),
+            pltpu.VMEM(docs.shape, docs.dtype),
             pltpu.VMEM((WINDOW * tokens, 2 * HD), jnp.bfloat16),
             pltpu.VMEM((tokens, WINDOW * tokens), jnp.float32),
             pltpu.VMEM((tokens, inner), jnp.bfloat16),
             pltpu.VMEM((SIDE, inner, quarter), jnp.bfloat16),
-            pltpu.SemaphoreType.DMA((SIDE,)),
+            pltpu.SemaphoreType.DMA((SIDE + 2,)),
         ],
-        compiler_params=pltpu.CompilerParams(vmem_limit_bytes=48 * 1024 * 1024),
+        compiler_params=pltpu.CompilerParams(vmem_limit_bytes=20 * 1024 * 1024),
         name="attention",
-    )(rank, order, queries, own, other, docs, out_weight)
+    )(ranks, order, queries, own, other, docs, out_weight)
+    return [(outs[2 * d], outs[2 * d + 1]) for d in range(SIDE)]
 
 
 TILE = 256
+OWN_LIMIT = 12
 
 
 def tiles(width, body):
@@ -156,15 +172,16 @@
     lax.fori_loop(0, width // TILE, step, 0)
 
 
-def lift_groups(groups, weight_ref, sums_ref, lanes):
-    rows = 2 * groups[0][1].shape[0]
-    inner = groups[0][1].shape[1]
+def lift_groups(groups, weight_ref, sums_ref, arrive=None):
+    rows = 2 * groups[0][2].shape[0]
+    inner = groups[0][2].shape[1]
 
     def body(cols, n):
-        for lane, (d, near_ref, far_ref) in zip(lanes, groups):
-            x = jnp.concatenate([near_ref[...], far_ref[...]], axis=0)
-            sums_ref[lane, d * rows : (d + 1) * rows, cols] = jnp.dot(
-                x,
+        if arrive is not None:
+            arrive(n)
+        for lane, k, near_ref, far_ref in groups:
+            sums_ref[lane, k * rows : (k + 1) * rows, cols] = jnp.dot(
+                jnp.concatenate([near_ref[...], far_ref[...]], axis=0),
                 weight_ref[lane * inner : (lane + 1) * inner, cols],
                 preferred_element_type=jnp.float32,
             )
@@ -172,19 +189,79 @@
     tiles(weight_ref.shape[1], body)
 
 
-EARLY = (0, 1, 3)
+SIDES = (1, 3)
 LAST = 2
 
 
+def each_side(body):
+    def step(k, carry):
+        body(k, 2 * k + 1)
+        return carry
+
+    lax.fori_loop(0, len(SIDES), step, 0)
+
+
+def combine(a_ref, a_at, b_ref, b_at, a_group, b_group, hidden_a, hidden_b):
+    rows, units = hidden_a.shape[0] // SIDE, hidden_a.shape[1]
+    slots = rows // SIDE
+
+    def at(group, block):
+        start = group * rows + block * slots
+        return pl.ds(start if isinstance(start, int) else pl.multiple_of(start, 8), slots)
+
+    a_rows, b_rows = at(a_at, b_group), at(b_at, a_group)
+    gate = a_ref[0, a_rows, :units] + b_ref[1, b_rows, :units]
+    up = a_ref[0, a_rows, units:] + b_ref[1, b_rows, units:]
+    value = gate / (1.0 + jnp.exp(-gate)) * up
+    hidden_a[at(a_group, b_group), :] = value
+    hidden_b[at(b_group, a_group), :] = value
+
+
+def own_kernel(*refs):
+    pieces, lifts, downs = refs[:4], refs[4:8], refs[8:10]
+    own_ref, weight_ref, down_ref, lift_sems, down_sems = refs[10:]
+    units = downs[0].shape[0]
+
+    def lift_copy(source, n):
+        cols = pl.ds(pl.multiple_of(n * TILE, TILE), TILE)
+        return pltpu.make_async_copy(source, weight_ref.at[:, cols], lift_sems.at[n])
+
+    down_copies = [
+        pltpu.make_async_copy(ref, down_ref.at[i * units : (i + 1) * units, :], down_sems.at[i])
+        for i, ref in enumerate(downs)
+    ]
+    for n, ref in enumerate(lifts):
+        lift_copy(ref, n).start()
+    for copy in down_copies:
+        copy.start()
+    lift_groups(
+        [(0, 0, pieces[0], pieces[1]), (1, 0, pieces[2], pieces[3])],
+        weight_ref,
+        own_ref,
+        lambda n: lift_copy(lifts[0], n).wait(),
+    )
+    for copy in down_copies:
+        copy.wait()
+
+
 def early_kernel(*refs):
-    *pieces, weight_ref, sums_ref = refs
-    groups, lanes = [], []
+    pieces, own_ref, weight_ref, (sums_ref, hidden_a, hidden_b) = refs[:8], refs[8], refs[9], refs[10:]
+    groups = []
     for lane in range(2):
-        for k, d in enumerate(EARLY):
-            at = 2 * (lane * len(EARLY) + k)
-            groups.append((d, pieces[at], pieces[at + 1]))
-            lanes.append(lane)
-    lift_groups(groups, weight_ref, sums_ref, lanes)
+        for k in range(len(SIDES)):
+            at = 2 * (lane * len(SIDES) + k)
+            groups.append((lane, k, pieces[at], pieces[at + 1]))
+    lift_groups(groups, weight_ref, sums_ref)
+    combine(own_ref, 0, own_ref, 0, 0, 0, hidden_a, hidden_b)
+
+    def outer(k, d):
+        combine(own_ref, 0, sums_ref, k, 0, d, hidden_a, hidden_b)
+        combine(sums_ref, k, own_ref, 0, d, 0, hidden_a, hidden_b)
+        each_side(
+            lambda m, e: combine(sums_ref, k, sums_ref, m, d, e, hidden_a, hidden_b)
+        )
+
+    each_side(outer)
 
 
 def lower_groups(hidden_refs, down_ref, outs):
@@ -203,40 +280,19 @@
 
 
 def last_kernel(
-    a_near, a_far, b_near, b_far, weight_ref, early_ref, down_ref,
+    a_near, a_far, b_near, b_far, weight_ref, own_ref, sums_ref, down_ref, early_a, early_b,
     hidden_a, hidden_b, a_out_near, a_out_far, b_out_near, b_out_far, late_ref,
 ):
-    rows = 2 * a_near.shape[0]
-    units = down_ref.shape[0]
-    slots = rows // SIDE
-    lift_groups(
-        [(0, a_near, a_far), (0, b_near, b_far)], weight_ref, late_ref, (0, 1)
-    )
-
-    def combine(a_ref, a_base, b_ref, b_base, a_group, b_group):
-        a_at = pl.ds(pl.multiple_of(a_base + b_group * slots, 8), slots)
-        b_at = pl.ds(pl.multiple_of(b_base + a_group * slots, 8), slots)
-        gate = a_ref[0, a_at, :units] + b_ref[1, b_at, :units]
-        up = a_ref[0, a_at, units:] + b_ref[1, b_at, units:]
-        value = gate / (1.0 + jnp.exp(-gate)) * up
-        hidden_a[pl.ds(pl.multiple_of(a_group * rows + b_group * slots, 8), slots), :] = value
-        hidden_b[pl.ds(pl.multiple_of(b_group * rows + a_group * slots, 8), slots), :] = value
-
-    combine(late_ref, 0, late_ref, 0, LAST, LAST)
-
-    def each(k, carry):
-        d = jnp.where(k == LAST, SIDE - 1, k)
-        combine(late_ref, 0, early_ref, d * rows, LAST, d)
-        combine(early_ref, d * rows, late_ref, 0, d, LAST)
-
-        def other(m, inner):
-            e = jnp.where(m == LAST, SIDE - 1, m)
-            combine(early_ref, d * rows, early_ref, e * rows, d, e)
-            return inner
-
-        return lax.fori_loop(0, SIDE - 1, other, carry)
-
-    lax.fori_loop(0, SIDE - 1, each, 0)
+    lift_groups([(0, 0, a_near, a_far), (1, 0, b_near, b_far)], weight_ref, late_ref)
+    combine(late_ref, 0, late_ref, 0, LAST, LAST, hidden_a, hidden_b)
+    combine(late_ref, 0, own_ref, 0, LAST, 0, hidden_a, hidden_b)
+    combine(own_ref, 0, late_ref, 0, 0, LAST, hidden_a, hidden_b)
+
+    def crossing(k, d):
+        combine(late_ref, 0, sums_ref, k, LAST, d, hidden_a, hidden_b)
+        combine(sums_ref, k, late_ref, 0, d, LAST, hidden_a, hidden_b)
+
+    each_side(crossing)
     lower_groups(
         (hidden_a, hidden_b),
         down_ref,
@@ -244,48 +300,75 @@
     )
 
 
+REST = (1, 3, 0)
+
+
 def rest_kernel(hidden_a, hidden_b, down_ref, *outs):
     groups = []
     for lane in range(2):
-        for k, d in enumerate(EARLY):
-            at = 2 * (lane * len(EARLY) + k)
+        for k, d in enumerate(REST):
+            at = 2 * (lane * len(REST) + k)
             groups.append((lane, d, outs[at], outs[at + 1]))
     lower_groups((hidden_a, hidden_b), down_ref, groups)
 
 
-def in_vmem(kernel, out_shapes, operands, scratch=()):
+def in_hbm(arrays):
+    return [pltpu.with_memory_space_constraint(a, pltpu.HBM) for a in arrays]
+
+
+def in_vmem(kernel, out_shapes, operands, scratch=(), aliases=None, hbm=(), limit=12):
     vmem = pl.BlockSpec(memory_space=pltpu.VMEM)
+    far = pl.BlockSpec(memory_space=pltpu.HBM)
     return pl.pallas_call(
         kernel,
         out_shape=out_shapes,
-        in_specs=[vmem] * len(operands),
+        in_specs=[far if i in hbm else vmem for i in range(len(operands))],
         out_specs=[vmem] * len(out_shapes),
         scratch_shapes=list(scratch),
-        compiler_params=pltpu.CompilerParams(vmem_limit_bytes=12 * 1024 * 1024),
+        input_output_aliases=aliases or {},
+        compiler_params=pltpu.CompilerParams(vmem_limit_bytes=limit * 1024 * 1024),
     )(*operands)
 
 
-def expert_parts(a_groups, b_groups, gate_up, down):
+def expert_parts(a_groups, b_groups, lifts, downs):
     piece = a_groups[0][0]
     rows = 2 * piece.shape[0]
-    units, _ = down.shape
-    early = [p for groups in (a_groups, b_groups) for d in EARLY for p in groups[d]]
-    sums = jax.ShapeDtypeStruct((2, SIDE * rows, gate_up.shape[1]), jnp.float32)
-    (early_sums,) = in_vmem(early_kernel, [sums], [*early, gate_up])
+    units = 2 * downs[0].shape[0]
+    both = 2 * units
     hidden = jax.ShapeDtypeStruct((SIDE * rows, units), jnp.float32)
     part = jax.ShapeDtypeStruct(piece.shape, jnp.bfloat16)
+    own_sums, weight, down = in_vmem(
+        own_kernel,
+        [
+            jax.ShapeDtypeStruct((2, rows, both), jnp.float32),
+            jax.ShapeDtypeStruct((lifts[0].shape[0], both), piece.dtype),
+            jax.ShapeDtypeStruct((units, downs[0].shape[1]), piece.dtype),
+        ],
+        [*a_groups[0], *b_groups[0], *in_hbm(lifts), *in_hbm(downs)],
+        [pltpu.SemaphoreType.DMA((len(lifts),)), pltpu.SemaphoreType.DMA((len(downs),))],
+        hbm=range(4, 10),
+        limit=OWN_LIMIT,
+    )
+    sides = [p for groups in (a_groups, b_groups) for d in SIDES for p in groups[d]]
+    sums, early_a, early_b = in_vmem(
+        early_kernel,
+        [jax.ShapeDtypeStruct((2, len(SIDES) * rows, both), jnp.float32), hidden, hidden],
+        [*sides, own_sums, weight],
+    )
+    operands = [*a_groups[LAST], *b_groups[LAST], weight, own_sums, sums, down, early_a, early_b]
     hidden_a, hidden_b, *first = in_vmem(
         last_kernel,
         [hidden, hidden] + [part] * 4,
-        [*a_groups[LAST], *b_groups[LAST], gate_up, early_sums, down],
-        [pltpu.VMEM((2, rows, gate_up.shape[1]), jnp.float32)],
-    )
-    rest = in_vmem(rest_kernel, [part] * (4 * len(EARLY)), [hidden_a, hidden_b, down])
+        operands,
+        [pltpu.VMEM((2, rows, both), jnp.float32)],
+        {len(operands) - 2: 0, len(operands) - 1: 1},
+    )
+    rest = in_vmem(rest_kernel, [part] * (4 * len(REST)), [hidden_a, hidden_b, down])
     pieces = [[None] * SIDE, [None] * SIDE]
     for lane in range(2):
         pieces[lane][LAST] = (first[2 * lane], first[2 * lane + 1])
-        for k, d in enumerate(EARLY):
-            at = 2 * (lane * len(EARLY) + k)
+        for k, d in enumerate(REST):
+            at = 2 * (lane * len(REST) + k)
             pieces[lane][d] = (rest[at], rest[at + 1])
     return pieces
 
@@ -314,8 +397,13 @@
     near3 = along(pieces[3][0], dim, 1)
     near1 = along(plus(pieces[1][0], near2), dim, -1)
     far3 = along(plus(pieces[3][1], far2), dim, 1)
-    near = plus(pieces[0][0], near3, near1)
-    far = plus(pieces[0][1], far1, far3)
+    return (pieces[0][0], near3, near1), (pieces[0][1], far1, far3)
+
+
+def summed_ring(pieces, dim):
+    near, far = scatter_ring(pieces, dim)
+    near = plus(*near)
+    far = plus(*far)
     return near, far
 
 
@@ -356,7 +444,7 @@
     kv_other = shifted(kv_own, 0, 0, 1)
 
     projected = attend_and_project(
-        cp_rank.reshape(1).astype(jnp.int32),
+        jnp.stack([cp_rank, ep_rank]).astype(jnp.int32),
         block_order,
         queries,
         kv_own,
@@ -364,14 +452,12 @@
         doc_ids.reshape(-1, tokens),
         out_weight,
     )
-    gate_up = jnp.concatenate([gate_weight[0], gate_other, up_weight[0], up_other], axis=1)
-    down = jnp.concatenate([down_weight[0], down_other], axis=0)
-    arrived = lax.all_to_all(projected, "ep", split_axis=0, concat_axis=0, tiled=True)
-    arrived, gate_up, down = lax.optimization_barrier((arrived, gate_up, down))
+    near, far = scatter_ring(projected, "x")
     own_residual = lax.dynamic_slice_in_dim(residual, ep_rank * quarter, quarter, 1)
-    hidden_state = (
-        own_residual.astype(jnp.float32) + arrived.astype(jnp.float32).sum(axis=0)
-    ).astype(jnp.bfloat16)
+    cut = tokens // 2
+    hidden_near = plus(own_residual[:cut], *near)
+    hidden_far = plus(own_residual[cut:], *far)
+    hidden_state = jnp.concatenate([hidden_near, hidden_far], axis=0)
 
     experts = jnp.arange(SIDE, dtype=jnp.int32)
     logit_gap = route_logits[:, 1] - route_logits[:, 0]
@@ -411,9 +497,14 @@
         jnp.concatenate(second_line[:2], axis=0), jnp.concatenate(second_line[2:], axis=0), "y"
     )
 
-    a_parts, b_parts = expert_parts(first_all, second_all, gate_up, down)
-    sum_first = scatter_line(*scatter_ring(a_parts, "z"), "y")
-    sum_second = scatter_line(*scatter_ring(b_parts, "y"), "z")
+    a_parts, b_parts = expert_parts(
+        first_all,
+        second_all,
+        (gate_weight[0], gate_other, up_weight[0], up_other),
+        (down_weight[0], down_other),
+    )
+    sum_first = scatter_line(*summed_ring(a_parts, "z"), "y")
+    sum_second = scatter_line(*summed_ring(b_parts, "y"), "z")
     back = jnp.stack(
         [sum_first[:, :quarter], sum_first[:, quarter:], sum_second[:, :quarter], sum_second[:, quarter:]]
     )

time: 248 us -> 256 us (1.032)
  other arithmetic: 19.7 us -> 4.88 us
  waiting for transfers between devices: 111 us -> 125 us
  starting transfers between devices: 75.8 us -> 87.5 us
  local copies, waits for them, and re-layouts: 9.85 us -> 3.62 us
  Pallas kernels: 27.9 us -> 31.2 us
    concatenate x2 -> x1, other arithmetic: 14.9 us -> 0.03 us  [local(): hidden_state = jnp.concatenate([hidden_near, hidden_far], axis=0)]
    ppermute x46, waiting for transfers between devices: 88.6 us -> 103 us  [shifted(): return lax.ppermute(array, 'cp', pairs)]
    ppermute x0 -> x6, starting transfers between devices: none -> 9.46 us  [along(): lax.ppermute(array, 'ep', [(i, (i + step) % SIDE) for i in range(SIDE)])]
    ppermute x0 -> x6, waiting for transfers between devices: none -> 6.66 us  [along(): lax.ppermute(array, 'ep', [(i, (i + step) % SIDE) for i in range(SIDE)])]
    unnamed x30 -> x16, local copies, waits for them, and re-layouts: 7.76 us -> 1.53 us
    all_to_all x1 -> x0, waiting for transfers between devices: 6.04 us -> none  [local(): lax.all_to_all(projected, 'ep', split_axis=0, concat_axis=0, tiled=True)]
    ppermute x46, starting transfers between devices: 64.6 us -> 70.1 us  [shifted(): return lax.ppermute(array, 'cp', pairs)]
    all_to_all x1 -> x0, starting transfers between devices: 4.3 us -> none  [local(): lax.all_to_all(projected, 'ep', split_axis=0, concat_axis=0, tiled=True)]
  transfers between devices with their start and end apart: 49 -> 54, of which waited for: 27 -> 30; matrix products, arithmetic and copies ran while one was open for 8% -> 2% of each run, Pallas kernels for 9% -> 7%
where the time goes in v1:
time: 256 us
  waiting for transfers between devices  125 us (49%)
  starting transfers between devices  87.5 us (34%)
  Pallas kernels  31.2 us (12%)
  other arithmetic  4.88 us (2%)
  local copies, waits for them, and re-layouts  3.62 us (1%)
    ppermute x46, waiting for transfers between devices, shifted(): return lax.ppermute(array, 'cp', pairs)  103 us
    ppermute x46, starting transfers between devices, shifted(): return lax.ppermute(array, 'cp', pairs)  70.1 us
    pallas_call x4, Pallas kernels, in_vmem(): pl.pallas_call(kernel, out_shape=out_shapes, in_specs=[far if i in hbm el...  23.6 us
    ppermute x6, starting transfers between devices, along(): lax.ppermute(array, 'ep', [(i, (i + step) % SIDE) for i in range(SIDE)])  9.46 us
    all_to_all x1, waiting for transfers between devices, local(): back = lax.all_to_all(back, 'ep', split_axis=0, concat_axis=0, tiled=True)  7.68 us
    pallas_call x1, Pallas kernels, attend_and_project(): pl.pallas_call(attention_kernel, out_shape=[jax.ShapeDtypeStruct((tokens...  7.65 us
    all_to_all x1, waiting for transfers between devices, local(): lax.all_to_all(rows.reshape(SIDE, CAP, quarter), 'ep', split_axis=0, conc...  7.53 us
    ppermute x6, waiting for transfers between devices, along(): lax.ppermute(array, 'ep', [(i, (i + step) % SIDE) for i in range(SIDE)])  6.66 us
  transfers between devices with their start and end apart: 54, of which 30 were waited for; matrix products, arithmetic and copies ran while one was open for 2% of the time, Pallas kernels for 7%

profile of v1, /device:TPU:0, one launch (start us, length us, event | category | flops | bytes accessed | tf_op | source)
XLA Modules:
  0.0 255.8 jit_solution(1689224113417226756)
XLA Ops:
  2.2 1.8 collective-permute-start
  3.9 2.9 %collective-permute-start.1 = (bf16[128,256]{1,0:T(8,128)(2,1)S(1)}, bf16[128,256]{1,0:T(8,128)(2,1)S(1)}, u32[]{:S(2)}, u32[]{:S(2)}) collective-permute-start(bf16[128,256]{1,0:T(8,128)(2,1)S(1)} %get-tuple-element.80), channel_id=1, source_target_pairs={{0,64},{4,68},{8,72},{12,76},{16,80},{20,84},{24,88},{28,92},{32,9... | collective-permute-start | bytes 196616 | tf_op jit(solution)/shard_map/ppermute | solution.py:30
  6.8 1.3 collective-permute-start.2
  8.2 1.9 collective-permute-done.1
  11.1 2.0 collective-permute-start.3
  13.1 3.6 %collective-permute-start.4 = (bf16[512,256]{1,0:T(8,128)(2,1)S(1)}, bf16[512,256]{1,0:T(8,128)(2,1)S(1)}, u32[]{:S(2)}, u32[]{:S(2)}) collective-permute-start(bf16[512,256]{1,0:T(8,128)(2,1)S(1)} %pad_maximum_fusion.4), channel_id=1, source_target_pairs={{0,16},{4,20},{8,24},{12,28},{16,0},{20,4},{24,8},{28,12},{32,48},... | collective-permute-start | bytes 786440 | tf_op jit(solution)/shard_map/ppermute | solution.py:30
  17.7 3.8 %collective-permute-done.3 = bf16[512,256]{1,0:T(8,128)(2,1)S(1)} collective-permute-done((bf16[512,256]{1,0:T(8,128)(2,1)S(1)}, bf16[512,256]{1,0:T(8,128)(2,1)S(1)}, u32[]{:S(2)}, u32[]{:S(2)}) %collective-permute-start.3) | collective-permute-done | bytes 262176 | tf_op jit(solution)/shard_map/ppermute | solution.py:30
  21.5 5.4 %collective-permute-done.4 = bf16[512,256]{1,0:T(8,128)(2,1)S(1)} collective-permute-done((bf16[512,256]{1,0:T(8,128)(2,1)S(1)}, bf16[512,256]{1,0:T(8,128)(2,1)S(1)}, u32[]{:S(2)}, u32[]{:S(2)}) %collective-permute-start.4) | collective-permute-done | bytes 262176 | tf_op jit(solution)/shard_map/ppermute | solution.py:30
  27.9 1.8 collective-permute-done.6.other_ref
  30.4 7.6 %attention.1 = (bf16[64,1536]{1,0:T(8,128)(2,1)S(1)}, bf16[64,1536]{1,0:T(8,128)(2,1)S(1)}, bf16[64,1536]{1,0:T(8,128)(2,1)S(1)}, bf16[64,1536]{1,0:T(8,128)(2,1...) custom-call(s32[2]{0:T(128)S(1)} %pad_add_fusion.rank_ref, ...), custom_call_target="tpu_custom_call" | custom-call | tf_op jit(solution)/shard_map/attention/pallas_call | solution.py:143
  38.0 1.6 collective-permute-start.11
  39.9 1.8 collective-permute-start.8
  41.7 1.5 collective-permute-start.10
  43.7 2.9 %collective-permute-done.11 = bf16[64,1536]{1,0:T(8,128)(2,1)S(1)} collective-permute-done((bf16[64,1536]{1,0:T(8,128)(2,1)}, bf16[64,1536]{1,0:T(8,128)(2,1)S(1)}, u32[]{:S(2)}, u32[]{:S(2)}) %collective-permute-start.11) | collective-permute-done | bytes 196640 | tf_op jit(solution)/shard_map/ppermute | solution.py:35
  47.8 3.0 %collective-permute-start.9 = (bf16[64,1536]{1,0:T(8,128)(2,1)S(1)}, bf16[64,1536]{1,0:T(8,128)(2,1)S(1)}, u32[]{:S(2)}, u32[]{:S(2)}) collective-permute-start(bf16[64,1536]{1,0:T(8,128)(2,1)S(1)} %add_convert_fusion.13), channel_id=1, source_target_pairs={{0,3},{1,0},{2,1},{3,2},{4,7},{5,4},{6,5},{7,6},{8,11},{9,8},{10,9... | collective-permute-start | bytes 589832 | tf_op jit(solution)/shard_map/ppermute | solution.py:35
  51.9 3.0 %collective-permute-done.12 = bf16[64,1536]{1,0:T(8,128)(2,1)S(1)} collective-permute-done((bf16[64,1536]{1,0:T(8,128)(2,1)S(1)}, bf16[64,1536]{1,0:T(8,128)(2,1)S(1)}, u32[]{:S(2)}, u32[]{:S(2)}) %collective-permute-start.12) | collective-permute-done | bytes 196640 | tf_op jit(solution)/shard_map/ppermute | solution.py:35
  55.0 1.2 add_convert_fusion.12
  57.4 4.2 %all-to-all-start = ((bf16[4,40,1536]{2,1,0:T(8,128)(2,1)}), bf16[4,40,1536]{2,1,0:T(8,128)(2,1)S(1)}, u32[]{:S(2)}, u32[]{:S(2)}) async-start(bf16[4,40,1536]{2,1,0:T(8,128)(2,1)} %bitcast.9), calls=%async_computation | async-start | bytes 983040 | tf_op jit(solution)/shard_map/all_to_all | solution.py:481
  62.1 7.5 %all-to-all-done = bf16[4,40,1536]{2,1,0:T(8,128)(2,1)S(1)} async-done(((bf16[4,40,1536]{2,1,0:T(8,128)(2,1)}), bf16[4,40,1536]{2,1,0:T(8,128)(2,1)S(1)}, u32[]{:S(2)}, u32[]{:S(2)}) %all-to-all-start) | async-done | bytes 491552 | tf_op jit(solution)/shard_map/all_to_all | solution.py:481
  70.1 2.3 collective-permute-start.23
  72.4 1.7 collective-permute-start.24
  74.1 3.8 %collective-permute-done.23 = bf16[40,3072]{1,0:T(8,128)(2,1)S(1)} collective-permute-done((bf16[40,3072]{1,0:T(8,128)(2,1)S(1)}, bf16[40,3072]{1,0:T(8,128)(2,1)S(1)}, u32[]{:S(2)}, u32[]{:S(2)}) %collective-permute-start.23) | collective-permute-done | bytes 245792 | tf_op jit(solution)/shard_map/ppermute | solution.py:30
  77.9 3.0 %collective-permute-start.20 = (bf16[40,3072]{1,0:T(8,128)(2,1)S(1)}, bf16[40,3072]{1,0:T(8,128)(2,1)S(1)}, u32[]{:S(2)}, u32[]{:S(2)}) collective-permute-start(bf16[40,3072]{1,0:T(8,128)(2,1)S(1)} %pad_maximum_fusion.6), channel_id=1, source_target_pairs={{0,8},{4,12},{8,16},{12,20},{16,24},{20,28},{24,0},{28,4},{32,40},... | collective-permute-start | bytes 737288 | tf_op jit(solution)/shard_map/ppermute | solution.py:30
  81.6 1.5 collective-permute-start.16
  83.1 2.7 %collective-permute-done.20 = bf16[40,3072]{1,0:T(8,128)(2,1)S(1)} collective-permute-done((bf16[40,3072]{1,0:T(8,128)(2,1)S(1)}, bf16[40,3072]{1,0:T(8,128)(2,1)S(1)}, u32[]{:S(2)}, u32[]{:S(2)}) %collective-permute-start.20) | collective-permute-done | bytes 245792 | tf_op jit(solution)/shard_map/ppermute | solution.py:30
  85.8 2.4 collective-permute-start.17
  89.3 5.0 %collective-permute-start.25 = (bf16[80,3072]{1,0:T(8,128)(2,1)S(1)}, bf16[80,3072]{1,0:T(8,128)(2,1)S(1)}, u32[]{:S(2)}, u32[]{:S(2)}) collective-permute-start(bf16[80,3072]{1,0:T(8,128)(2,1)S(1)} %constant_dynamic-update-slice_fusion.12.refs_3_), channel_id=1, source_target_pairs={{0,96},{4,100},{8,104},{12,108},{16,112},{20,116},{24,120},{28,124... | collective-permute-start | bytes 1474568 | tf_op jit(solution)/shard_map/ppermute | solution.py:30
  94.3 2.6 %collective-permute-done.17 = bf16[40,3072]{1,0:T(8,128)(2,1)S(1)} collective-permute-done((bf16[40,3072]{1,0:T(8,128)(2,1)S(1)}, bf16[40,3072]{1,0:T(8,128)(2,1)S(1)}, u32[]{:S(2)}, u32[]{:S(2)}) %collective-permute-start.17) | collective-permute-done | bytes 245792 | tf_op jit(solution)/shard_map/ppermute | solution.py:30
  97.0 10.0 %collective-permute-done.13 = bf16[40,3072]{1,0:T(8,128)(2,1)S(1)} collective-permute-done((bf16[40,3072]{1,0:T(8,128)(2,1)S(1)}, bf16[40,3072]{1,0:T(8,128)(2,1)S(1)}, u32[]{:S(2)}, u32[]{:S(2)}) %collective-permute-start.13) | collective-permute-done | bytes 245792 | tf_op jit(solution)/shard_map/ppermute | solution.py:30
  107.0 10.9 %collective-permute-done.32.refs_5_ = bf16[80,3072]{1,0:T(8,128)(2,1)S(1)} collective-permute-done((bf16[80,3072]{1,0:T(8,128)(2,1)S(1)}, bf16[80,3072]{1,0:T(8,128)(2,1)S(1)}, u32[]{:S(2)}, u32[]{:S(2)}) %collective-permute-start.32) | collective-permute-done | bytes 491552 | tf_op jit(solution)/shard_map/ppermute | solution.py:30
  118.6 4.6 %collective-permute-done.21.refs_4_ = bf16[80,3072]{1,0:T(8,128)(2,1)S(1)} collective-permute-done((bf16[80,3072]{1,0:T(8,128)(2,1)S(1)}, bf16[80,3072]{1,0:T(8,128)(2,1)S(1)}, u32[]{:S(2)}, u32[]{:S(2)}) %collective-permute-start.21) | collective-permute-done | bytes 491552 | tf_op jit(solution)/shard_map/ppermute | solution.py:30
  123.2 4.9 %collective-permute-start.18 = (bf16[80,3072]{1,0:T(8,128)(2,1)S(1)}, bf16[80,3072]{1,0:T(8,128)(2,1)S(1)}, u32[]{:S(2)}, u32[]{:S(2)}) collective-permute-start(bf16[80,3072]{1,0:T(8,128)(2,1)S(1)} %constant_dynamic-update-slice_fusion.10.refs_1_), channel_id=1, source_target_pairs={{0,24},{4,28},{8,0},{12,4},{16,8},{20,12},{24,16},{28,20},{32,56},... | collective-permute-start | bytes 1474568 | tf_op jit(solution)/shard_map/ppermute | solution.py:30
  128.1 2.6 %collective-permute-start.30 = (bf16[80,3072]{1,0:T(8,128)(2,1)S(1)}, bf16[80,3072]{1,0:T(8,128)(2,1)S(1)}, u32[]{:S(2)}, u32[]{:S(2)}) collective-permute-start(bf16[80,3072]{1,0:T(8,128)(2,1)S(1)} %constant_dynamic-update-slice_fusion.10.refs_1_), channel_id=1, source_target_pairs={{0,8},{4,12},{8,16},{12,20},{16,24},{20,28},{24,0},{28,4},{32,40},... | collective-permute-start | bytes 1474568 | tf_op jit(solution)/shard_map/ppermute | solution.py:30
  130.7 7.3 %collective-permute-done.18.refs_3_ = bf16[80,3072]{1,0:T(8,128)(2,1)S(1)} collective-permute-done((bf16[80,3072]{1,0:T(8,128)(2,1)S(1)}, bf16[80,3072]{1,0:T(8,128)(2,1)S(1)}, u32[]{:S(2)}, u32[]{:S(2)}) %collective-permute-start.18) | collective-permute-done | bytes 491552 | tf_op jit(solution)/shard_map/ppermute | solution.py:30
  138.0 1.4 collective-permute-start.14
  139.4 2.6 %collective-permute-done.30.refs_1_ = bf16[80,3072]{1,0:T(8,128)(2,1)S(1)} collective-permute-done((bf16[80,3072]{1,0:T(8,128)(2,1)S(1)}, bf16[80,3072]{1,0:T(8,128)(2,1)S(1)}, u32[]{:S(2)}, u32[]{:S(2)}) %collective-permute-start.30) | collective-permute-done | bytes 491552 | tf_op jit(solution)/shard_map/ppermute | solution.py:30
  142.0 1.7 collective-permute-start.31
  143.7 4.9 %collective-permute-done.14.refs_0_ = bf16[80,3072]{1,0:T(8,128)(2,1)S(1)} collective-permute-done((bf16[80,3072]{1,0:T(8,128)(2,1)S(1)}, bf16[80,3072]{1,0:T(8,128)(2,1)S(1)}, u32[]{:S(2)}, u32[]{:S(2)}) %collective-permute-start.14) | collective-permute-done | bytes 491552 | tf_op jit(solution)/shard_map/ppermute | solution.py:30
  148.5 1.7 collective-permute-start.26
  150.6 5.0 %collective-permute-start.19 = (bf16[80,3072]{1,0:T(8,128)(2,1)S(1)}, bf16[80,3072]{1,0:T(8,128)(2,1)S(1)}, u32[]{:S(2)}, u32[]{:S(2)}) collective-permute-start(bf16[80,3072]{1,0:T(8,128)(2,1)S(1)} %collective-permute-done.18.refs_3_), channel_id=1, source_target_pairs={{0,24},{4,28},{8,0},{12,4},{16,8},{20,12},{24,16},{28,20},{32,56},... | collective-permute-start | bytes 1474568 | tf_op jit(solution)/shard_map/ppermute | solution.py:30
  155.6 6.5 %shard_map.140 = (f32[2,160,1024]{2,1,0:T(8,128)S(1)}, bf16[6144,1024]{1,0:T(8,128)(2,1)S(1)}, bf16[512,6144]{1,0:T(8,128)(2,1)S(1)}) custom-call(bf16[80,3072]{1,0:T(8,128)(2,1)S(1)} %pad_maximum_fusion.refs_0_, bf16[80,3072]{1,0:T(8,128)(2,1)S(1)} %constant_dynamic-update-slice_fusion.10.refs_1_, bf16[80,3072]{1,0:T(8,128)(2,1)S(1)} %pad_maximum_fusion.1.refs_2_, ...), custom_call_target="tpu_custom_call" | custom-call | tf_op jit(solution)/shard_map/pallas_call | solution.py:322
  162.1 5.2 %shard_map.141 = (f32[2,320,1024]{2,1,0:T(8,128)S(1)}, f32[640,512]{1,0:T(8,128)S(1)}, f32[640,512]{1,0:T(8,128)S(1)}) custom-call(bf16[80,3072]{1,0:T(8,128)(2,1)S(1)} %collective-permute-done.14.refs_0_, bf16[80,3072]{1,0:T(8,128)(2,1)S(1)} %collective-permute-done.30.refs_1_, bf16[80,3072]{1,0:T(8,128)(2,1)S(1)} %collective-permute-done.31.refs_2_, ...), custom_call_target="tpu_custom_call" | custom-call | tf_op jit(solution)/shard_map/pallas_call | solution.py:322
  167.3 6.4 %shard_map.142 = (f32[640,512]{1,0:T(8,128)S(1)}, f32[640,512]{1,0:T(8,128)S(1)}, bf16[80,3072]{1,0:T(8,128)(2,1)S(1)}, bf16[80,3072]{1,0:T(8,128)(2,1)S(1)}, bf...) custom-call(bf16[80,3072]{1,0:T(8,128)(2,1)S(1)} %collective-permute-done.1, ...), custom_call_target="tpu_custom_call", output_to_operand_aliasing={{0}: (8, {}), {1}: (9, {})} | custom-call | tf_op jit(solution)/shard_map/pallas_call | solution.py:322
  173.7 3.3 %collective-permute-start.35 = (bf16[80,3072]{1,0:T(8,128)(2,1)S(1)}, bf16[80,3072]{1,0:T(8,128)(2,1)S(1)}, u32[]{:S(2)}, u32[]{:S(2)}) collective-permute-start(bf16[80,3072]{1,0:T(8,128)(2,1)S(1)} %get-tuple-element.53), channel_id=1, source_target_pairs={{0,24},{4,28},{8,0},{12,4},{16,8},{20,12},{24,16},{28,20},{32,56},... | collective-permute-start | bytes 1474568 | tf_op jit(solution)/shard_map/ppermute | solution.py:30
  177.0 5.5 %shard_map.143 = (bf16[80,3072]{1,0:T(8,128)(2,1)S(1)}, bf16[80,3072]{1,0:T(8,128)(2,1)S(1)}, bf16[80,3072]{1,0:T(8,128)(2,1)S(1)}, bf16[80,3072]{1,0:T(8,128)(2...) custom-call(f32[640,512]{1,0:T(8,128)S(1)} %get-tuple-element.48.hid, ...), custom_call_target="tpu_custom_call" | custom-call | tf_op jit(solution)/shard_map/pallas_call | solution.py:322
  182.7 3.2 %collective-permute-start.38 = (bf16[80,3072]{1,0:T(8,128)(2,1)S(1)}, bf16[80,3072]{1,0:T(8,128)(2,1)S(1)}, u32[]{:S(2)}, u32[]{:S(2)}) collective-permute-start(bf16[80,3072]{1,0:T(8,128)(2,1)S(1)} %get-tuple-element.55), channel_id=1, source_target_pairs={{0,24},{4,28},{8,0},{12,4},{16,8},{20,12},{24,16},{28,20},{32,56},... | collective-permute-start | bytes 1474568 | tf_op jit(solution)/shard_map/ppermute | solution.py:30
  185.9 1.2 collective-permute-start.44
  188.1 9.8 %collective-permute-done.39 = bf16[80,3072]{1,0:T(8,128)(2,1)S(1)} collective-permute-done((bf16[80,3072]{1,0:T(8,128)(2,1)S(1)}, bf16[80,3072]{1,0:T(8,128)(2,1)S(1)}, u32[]{:S(2)}, u32[]{:S(2)}) %collective-permute-start.39) | collective-permute-done | bytes 491552 | tf_op jit(solution)/shard_map/ppermute | solution.py:30
  198.1 1.1 collective-permute-done.44
  199.2 2.6 %collective-permute-start.47 = (bf16[80,3072]{1,0:T(8,128)(2,1)S(1)}, bf16[80,3072]{1,0:T(8,128)(2,1)S(1)}, u32[]{:S(2)}, u32[]{:S(2)}) collective-permute-start(bf16[80,3072]{1,0:T(8,128)(2,1)S(1)} %get-tuple-element.63), channel_id=1, source_target_pairs={{0,96},{4,100},{8,104},{12,108},{16,112},{20,116},{24,120},{28,124... | collective-permute-start | bytes 1474568 | tf_op jit(solution)/shard_map/ppermute | solution.py:30
  202.0 6.0 %collective-permute-done.48 = bf16[80,3072]{1,0:T(8,128)(2,1)S(1)} collective-permute-done((bf16[80,3072]{1,0:T(8,128)(2,1)S(1)}, bf16[80,3072]{1,0:T(8,128)(2,1)S(1)}, u32[]{:S(2)}, u32[]{:S(2)}) %collective-permute-start.48) | collective-permute-done | bytes 491552 | tf_op jit(solution)/shard_map/ppermute | solution.py:30
  208.1 2.1 collective-permute-start.40
  210.2 6.6 %collective-permute-done.36 = bf16[80,3072]{1,0:T(8,128)(2,1)S(1)} collective-permute-done((bf16[80,3072]{1,0:T(8,128)(2,1)S(1)}, bf16[80,3072]{1,0:T(8,128)(2,1)S(1)}, u32[]{:S(2)}, u32[]{:S(2)}) %collective-permute-start.36) | collective-permute-done | bytes 491552 | tf_op jit(solution)/shard_map/ppermute | solution.py:30
  217.0 2.1 collective-permute-start.49
  219.1 1.2 collective-permute-start.37
  220.6 1.2 collective-permute-start.41
  221.8 3.8 %collective-permute-done.45 = bf16[80,3072]{1,0:T(8,128)(2,1)S(1)} collective-permute-done((bf16[80,3072]{1,0:T(8,128)(2,1)S(1)}, bf16[80,3072]{1,0:T(8,128)(2,1)S(1)}, u32[]{:S(2)}, u32[]{:S(2)}) %collective-permute-start.45) | collective-permute-done | bytes 491552 | tf_op jit(solution)/shard_map/ppermute | solution.py:30
  226.8 1.6 collective-permute-start.46
  228.3 2.9 %collective-permute-done.49 = bf16[80,3072]{1,0:T(8,128)(2,1)S(1)} collective-permute-done((bf16[80,3072]{1,0:T(8,128)(2,1)S(1)}, bf16[80,3072]{1,0:T(8,128)(2,1)S(1)}, u32[]{:S(2)}, u32[]{:S(2)}) %collective-permute-start.49) | collective-permute-done | bytes 491552 | tf_op jit(solution)/shard_map/ppermute | solution.py:30
  232.0 2.0 collective-permute-start.51
  234.1 5.3 %collective-permute-done.50 = bf16[40,3072]{1,0:T(8,128)(2,1)S(1)} collective-permute-done((bf16[40,3072]{1,0:T(8,128)(2,1)S(1)}, bf16[40,3072]{1,0:T(8,128)(2,1)S(1)}, u32[]{:S(2)}, u32[]{:S(2)}) %collective-permute-start.50) | collective-permute-done | bytes 245792 | tf_op jit(solution)/shard_map/ppermute | solution.py:30
  239.4 2.5 collective-permute-done.51
  242.9 3.7 %all-to-all-start.1 = ((bf16[4,40,1536]{2,1,0:T(8,128)(2,1)}), bf16[4,40,1536]{2,1,0:T(8,128)(2,1)S(1)}, u32[]{:S(2)}, u32[]{:S(2)}) async-start(bf16[4,40,1536]{2,1,0:T(8,128)(2,1)} %pad_maximum_fusion.2), calls=%async_computation.1 | async-start | bytes 983040 | tf_op jit(solution)/shard_map/all_to_all | solution.py:511
  246.8 7.7 %all-to-all-done.1 = bf16[4,40,1536]{2,1,0:T(8,128)(2,1)S(1)} async-done(((bf16[4,40,1536]{2,1,0:T(8,128)(2,1)}), bf16[4,40,1536]{2,1,0:T(8,128)(2,1)S(1)}, u32[]{:S(2)}, u32[]{:S(2)}) %all-to-all-start.1) | async-done | bytes 491552 | tf_op jit(solution)/shard_map/all_to_all | solution.py:511
  (116 shorter events, 19.9 us)
Async XLA Ops:
  2.2 6.0 %collective-permute-start = (bf16[128,256]{1,0:T(8,128)(2,1)S(1)}, bf16[128,256]{1,0:T(8,128)(2,1)S(1)}, u32[]{:S(2)}, u32[]{:S(2)}) collective-permute-start(bf16[128,256]{1,0:T(8,128)(2,1)S(1)} %get-tuple-element.80), channel_id=1, source_target_pairs={{0,32},{4,36},{8,40},{12,44},{16,48},{20,52},{24,56},{28,60},{32,6... | collective-permute-start | bytes 196616 | tf_op jit(solution)/shard_map/ppermute | solution.py:30
  3.9 6.1 %collective-permute-start.1 = (bf16[128,256]{1,0:T(8,128)(2,1)S(1)}, bf16[128,256]{1,0:T(8,128)(2,1)S(1)}, u32[]{:S(2)}, u32[]{:S(2)}) collective-permute-start(bf16[128,256]{1,0:T(8,128)(2,1)S(1)} %get-tuple-element.80), channel_id=1, source_target_pairs={{0,64},{4,68},{8,72},{12,76},{16,80},{20,84},{24,88},{28,92},{32,9... | collective-permute-start | bytes 196616 | tf_op jit(solution)/shard_map/ppermute | solution.py:30
  6.8 4.3 %collective-permute-start.2 = (bf16[128,256]{1,0:T(8,128)(2,1)S(1)}, bf16[128,256]{1,0:T(8,128)(2,1)S(1)}, u32[]{:S(2)}, u32[]{:S(2)}) collective-permute-start(bf16[128,256]{1,0:T(8,128)(2,1)S(1)} %get-tuple-element.80), channel_id=1, source_target_pairs={{0,96},{4,100},{8,104},{12,108},{16,112},{20,116},{24,120},{28,124... | collective-permute-start | bytes 196616 | tf_op jit(solution)/shard_map/ppermute | solution.py:30
  11.1 10.4 %collective-permute-start.3 = (bf16[512,256]{1,0:T(8,128)(2,1)S(1)}, bf16[512,256]{1,0:T(8,128)(2,1)S(1)}, u32[]{:S(2)}, u32[]{:S(2)}) collective-permute-start(bf16[512,256]{1,0:T(8,128)(2,1)S(1)} %pad_maximum_fusion.4), channel_id=1, source_target_pairs={{0,8},{4,12},{8,16},{12,20},{16,24},{20,28},{24,0},{28,4},{32,40},... | collective-permute-start | bytes 786440 | tf_op jit(solution)/shard_map/ppermute | solution.py:30
  13.1 13.8 %collective-permute-start.4 = (bf16[512,256]{1,0:T(8,128)(2,1)S(1)}, bf16[512,256]{1,0:T(8,128)(2,1)S(1)}, u32[]{:S(2)}, u32[]{:S(2)}) collective-permute-start(bf16[512,256]{1,0:T(8,128)(2,1)S(1)} %pad_maximum_fusion.4), channel_id=1, source_target_pairs={{0,16},{4,20},{8,24},{12,28},{16,0},{20,4},{24,8},{28,12},{32,48},... | collective-permute-start | bytes 786440 | tf_op jit(solution)/shard_map/ppermute | solution.py:30
  16.7 10.2 %collective-permute-start.5 = (bf16[512,256]{1,0:T(8,128)(2,1)S(1)}, bf16[512,256]{1,0:T(8,128)(2,1)S(1)}, u32[]{:S(2)}, u32[]{:S(2)}) collective-permute-start(bf16[512,256]{1,0:T(8,128)(2,1)S(1)} %pad_maximum_fusion.4), channel_id=1, source_target_pairs={{0,24},{4,28},{8,0},{12,4},{16,8},{20,12},{24,16},{28,20},{32,56},... | collective-permute-start | bytes 786440 | tf_op jit(solution)/shard_map/ppermute | solution.py:30
  27.0 2.7 %collective-permute-start.6 = (bf16[2048,256]{1,0:T(8,128)(2,1)S(1)}, bf16[2048,256]{1,0:T(8,128)(2,1)S(1)}, u32[]{:S(2)}, u32[]{:S(2)}) collective-permute-start(bf16[2048,256]{1,0:T(8,128)(2,1)S(1)} %constant_dynamic-update-slice_fusion.2.own_ref), channel_id=1, source_target_pairs={{0,4},{4,0},{8,12},{12,8},{16,20},{20,16},{24,28},{28,24},{32,36},... | collective-permute-start | bytes 3145736 | tf_op jit(solution)/shard_map/ppermute | solution.py:30
  29.7 0.7 copy-start
  38.0 8.6 %collective-permute-start.11 = (bf16[64,1536]{1,0:T(8,128)(2,1)}, bf16[64,1536]{1,0:T(8,128)(2,1)S(1)}, u32[]{:S(2)}, u32[]{:S(2)}) collective-permute-start(bf16[64,1536]{1,0:T(8,128)(2,1)} %get-tuple-element.41), channel_id=1, source_target_pairs={{0,1},{1,2},{2,3},{3,0},{4,5},{5,6},{6,7},{7,4},{8,9},{9,10},{10,1... | collective-permute-start | bytes 589832 | tf_op jit(solution)/shard_map/ppermute | solution.py:35
  39.6 22.5 %copy-start.2 = (f32[6144]{0:T(1024)S(1)}, f32[6144]{0:T(1024)}, u32[]{:S(2)}) copy-start(f32[6144]{0:T(1024)} %param.18) | copy-start | bytes 73732
  39.9 7.8 %collective-permute-start.8 = (bf16[64,1536]{1,0:T(8,128)(2,1)S(1)}, bf16[64,1536]{1,0:T(8,128)(2,1)S(1)}, u32[]{:S(2)}, u32[]{:S(2)}) collective-permute-start(bf16[64,1536]{1,0:T(8,128)(2,1)S(1)} %get-tuple-element.37), channel_id=1, source_target_pairs={{0,3},{1,0},{2,1},{3,2},{4,7},{5,4},{6,5},{7,6},{8,11},{9,8},{10,9... | collective-permute-start | bytes 589832 | tf_op jit(solution)/shard_map/ppermute | solution.py:35
  41.7 10.2 %collective-permute-start.10 = (bf16[64,1536]{1,0:T(8,128)(2,1)S(1)}, bf16[64,1536]{1,0:T(8,128)(2,1)S(1)}, u32[]{:S(2)}, u32[]{:S(2)}) collective-permute-start(bf16[64,1536]{1,0:T(8,128)(2,1)S(1)} %get-tuple-element.39), channel_id=1, source_target_pairs={{0,3},{1,0},{2,1},{3,2},{4,7},{5,4},{6,5},{7,6},{8,11},{9,8},{10,9... | collective-permute-start | bytes 589832 | tf_op jit(solution)/shard_map/ppermute | solution.py:35
  43.2 8.7 %collective-permute-start.7 = (bf16[64,1536]{1,0:T(8,128)(2,1)S(1)}, bf16[64,1536]{1,0:T(8,128)(2,1)S(1)}, u32[]{:S(2)}, u32[]{:S(2)}) collective-permute-start(bf16[64,1536]{1,0:T(8,128)(2,1)S(1)} %get-tuple-element.35), channel_id=1, source_target_pairs={{0,1},{1,2},{2,3},{3,0},{4,5},{5,6},{6,7},{7,4},{8,9},{9,10},{10,1... | collective-permute-start | bytes 589832 | tf_op jit(solution)/shard_map/ppermute | solution.py:35
  46.7 8.2 %collective-permute-start.12 = (bf16[64,1536]{1,0:T(8,128)(2,1)S(1)}, bf16[64,1536]{1,0:T(8,128)(2,1)S(1)}, u32[]{:S(2)}, u32[]{:S(2)}) collective-permute-start(bf16[64,1536]{1,0:T(8,128)(2,1)S(1)} %add_convert_fusion.11), channel_id=1, source_target_pairs={{0,1},{1,2},{2,3},{3,0},{4,5},{5,6},{6,7},{7,4},{8,9},{9,10},{10,1... | collective-permute-start | bytes 589832 | tf_op jit(solution)/shard_map/ppermute | solution.py:35
  47.8 7.3 %collective-permute-start.9 = (bf16[64,1536]{1,0:T(8,128)(2,1)S(1)}, bf16[64,1536]{1,0:T(8,128)(2,1)S(1)}, u32[]{:S(2)}, u32[]{:S(2)}) collective-permute-start(bf16[64,1536]{1,0:T(8,128)(2,1)S(1)} %add_convert_fusion.13), channel_id=1, source_target_pairs={{0,3},{1,0},{2,1},{3,2},{4,7},{5,4},{6,5},{7,6},{8,11},{9,8},{10,9... | collective-permute-start | bytes 589832 | tf_op jit(solution)/shard_map/ppermute | solution.py:35
  56.3 32.0 %copy-start.1 = (bf16[128,1536]{1,0:T(8,128)(2,1)}, bf16[128,1536]{1,0:T(8,128)(2,1)S(1)}, u32[]{:S(2)}) copy-start(bf16[128,1536]{1,0:T(8,128)(2,1)S(1)} %pad_maximum_fusion.3) | copy-start | bytes 1179652
  57.4 12.3 %all-to-all-start = ((bf16[4,40,1536]{2,1,0:T(8,128)(2,1)}), bf16[4,40,1536]{2,1,0:T(8,128)(2,1)S(1)}, u32[]{:S(2)}, u32[]{:S(2)}) async-start(bf16[4,40,1536]{2,1,0:T(8,128)(2,1)} %bitcast.9), calls=%async_computation | async-start | bytes 983040 | tf_op jit(solution)/shard_map/all_to_all | solution.py:481
  61.6 88.7 %collective-permute-start.27 = (bf16[6144,256]{1,0:T(8,128)(2,1)}, bf16[6144,256]{1,0:T(8,128)(2,1)}, u32[]{:S(2)}, u32[]{:S(2)}) collective-permute-start(bf16[6144,256]{1,0:T(8,128)(2,1)} %bitcast.49), channel_id=1, source_target_pairs={{0,4},{4,0},{8,12},{12,8},{16,20},{20,16},{24,28},{28,24},{32,36},... | collective-permute-start | bytes 9437192 | tf_op jit(solution)/shard_map/ppermute | solution.py:30
  61.6 89.0 %collective-permute-start.28 = (bf16[6144,256]{1,0:T(8,128)(2,1)}, bf16[6144,256]{1,0:T(8,128)(2,1)}, u32[]{:S(2)}, u32[]{:S(2)}) collective-permute-start(bf16[6144,256]{1,0:T(8,128)(2,1)} %bitcast.51), channel_id=1, source_target_pairs={{0,4},{4,0},{8,12},{12,8},{16,20},{20,16},{24,28},{28,24},{32,36},... | collective-permute-start | bytes 9437192 | tf_op jit(solution)/shard_map/ppermute | solution.py:30
  62.1 93.5 %collective-permute-start.29 = (bf16[256,6144]{1,0:T(8,128)(2,1)}, bf16[256,6144]{1,0:T(8,128)(2,1)}, u32[]{:S(2)}, u32[]{:S(2)}) collective-permute-start(bf16[256,6144]{1,0:T(8,128)(2,1)} %bitcast.53), channel_id=1, source_target_pairs={{0,4},{4,0},{8,12},{12,8},{16,20},{20,16},{24,28},{28,24},{32,36},... | collective-permute-start | bytes 9437192 | tf_op jit(solution)/shard_map/ppermute | solution.py:30
  70.1 7.8 %collective-permute-start.23 = (bf16[40,3072]{1,0:T(8,128)(2,1)S(1)}, bf16[40,3072]{1,0:T(8,128)(2,1)S(1)}, u32[]{:S(2)}, u32[]{:S(2)}) collective-permute-start(bf16[40,3072]{1,0:T(8,128)(2,1)S(1)} %pad_maximum_fusion.6), channel_id=1, source_target_pairs={{0,16},{4,20},{8,24},{12,28},{16,0},{20,4},{24,8},{28,12},{32,48},... | collective-permute-start | bytes 737288 | tf_op jit(solution)/shard_map/ppermute | solution.py:30
  72.4 9.2 %collective-permute-start.24 = (bf16[40,3072]{1,0:T(8,128)(2,1)S(1)}, bf16[40,3072]{1,0:T(8,128)(2,1)S(1)}, u32[]{:S(2)}, u32[]{:S(2)}) collective-permute-start(bf16[40,3072]{1,0:T(8,128)(2,1)S(1)} %pad_maximum_fusion.6), channel_id=1, source_target_pairs={{0,24},{4,28},{8,0},{12,4},{16,8},{20,12},{24,16},{28,20},{32,56},... | collective-permute-start | bytes 737288 | tf_op jit(solution)/shard_map/ppermute | solution.py:30
  77.9 7.9 %collective-permute-start.20 = (bf16[40,3072]{1,0:T(8,128)(2,1)S(1)}, bf16[40,3072]{1,0:T(8,128)(2,1)S(1)}, u32[]{:S(2)}, u32[]{:S(2)}) collective-permute-start(bf16[40,3072]{1,0:T(8,128)(2,1)S(1)} %pad_maximum_fusion.6), channel_id=1, source_target_pairs={{0,8},{4,12},{8,16},{12,20},{16,24},{20,28},{24,0},{28,4},{32,40},... | collective-permute-start | bytes 737288 | tf_op jit(solution)/shard_map/ppermute | solution.py:30
  81.6 7.7 %collective-permute-start.16 = (bf16[40,3072]{1,0:T(8,128)(2,1)S(1)}, bf16[40,3072]{1,0:T(8,128)(2,1)S(1)}, u32[]{:S(2)}, u32[]{:S(2)}) collective-permute-start(bf16[40,3072]{1,0:T(8,128)(2,1)S(1)} %pad_maximum_fusion.5), channel_id=1, source_target_pairs={{0,64},{4,68},{8,72},{12,76},{16,80},{20,84},{24,88},{28,92},{32,9... | collective-permute-start | bytes 737288 | tf_op jit(solution)/shard_map/ppermute | solution.py:30
  85.8 11.1 %collective-permute-start.17 = (bf16[40,3072]{1,0:T(8,128)(2,1)S(1)}, bf16[40,3072]{1,0:T(8,128)(2,1)S(1)}, u32[]{:S(2)}, u32[]{:S(2)}) collective-permute-start(bf16[40,3072]{1,0:T(8,128)(2,1)S(1)} %pad_maximum_fusion.5), channel_id=1, source_target_pairs={{0,96},{4,100},{8,104},{12,108},{16,112},{20,116},{24,120},{28,124... | collective-permute-start | bytes 737288 | tf_op jit(solution)/shard_map/ppermute | solution.py:30
  89.3 17.6 %collective-permute-start.25 = (bf16[80,3072]{1,0:T(8,128)(2,1)S(1)}, bf16[80,3072]{1,0:T(8,128)(2,1)S(1)}, u32[]{:S(2)}, u32[]{:S(2)}) collective-permute-start(bf16[80,3072]{1,0:T(8,128)(2,1)S(1)} %constant_dynamic-update-slice_fusion.12.refs_3_), channel_id=1, source_target_pairs={{0,96},{4,100},{8,104},{12,108},{16,112},{20,116},{24,120},{28,124... | collective-permute-start | bytes 1474568 | tf_op jit(solution)/shard_map/ppermute | solution.py:30
  96.9 10.0 %collective-permute-start.13 = (bf16[40,3072]{1,0:T(8,128)(2,1)S(1)}, bf16[40,3072]{1,0:T(8,128)(2,1)S(1)}, u32[]{:S(2)}, u32[]{:S(2)}) collective-permute-start(bf16[40,3072]{1,0:T(8,128)(2,1)S(1)} %pad_maximum_fusion.5), channel_id=1, source_target_pairs={{0,32},{4,36},{8,40},{12,44},{16,48},{20,52},{24,56},{28,60},{32,6... | collective-permute-start | bytes 737288 | tf_op jit(solution)/shard_map/ppermute | solution.py:30
  107.0 11.0 %collective-permute-start.32 = (bf16[80,3072]{1,0:T(8,128)(2,1)S(1)}, bf16[80,3072]{1,0:T(8,128)(2,1)S(1)}, u32[]{:S(2)}, u32[]{:S(2)}) collective-permute-start(bf16[80,3072]{1,0:T(8,128)(2,1)S(1)} %constant_dynamic-update-slice_fusion.12.refs_3_), channel_id=1, source_target_pairs={{0,32},{4,36},{8,40},{12,44},{16,48},{20,52},{24,56},{28,60},{32,6... | collective-permute-start | bytes 1474568 | tf_op jit(solution)/shard_map/ppermute | solution.py:30
  107.0 16.2 %collective-permute-start.21 = (bf16[80,3072]{1,0:T(8,128)(2,1)S(1)}, bf16[80,3072]{1,0:T(8,128)(2,1)S(1)}, u32[]{:S(2)}, u32[]{:S(2)}) collective-permute-start(bf16[80,3072]{1,0:T(8,128)(2,1)S(1)} %pad_maximum_fusion.1.refs_2_), channel_id=1, source_target_pairs={{0,32},{4,36},{8,40},{12,44},{16,48},{20,52},{24,56},{28,60},{32,6... | collective-permute-start | bytes 1474568 | tf_op jit(solution)/shard_map/ppermute | solution.py:30
  117.9 10.2 %collective-permute-start.33 = (bf16[80,3072]{1,0:T(8,128)(2,1)S(1)}, bf16[80,3072]{1,0:T(8,128)(2,1)S(1)}, u32[]{:S(2)}, u32[]{:S(2)}) collective-permute-start(bf16[80,3072]{1,0:T(8,128)(2,1)S(1)} %pad_maximum_fusion.1.refs_2_), channel_id=1, source_target_pairs={{0,96},{4,100},{8,104},{12,108},{16,112},{20,116},{24,120},{28,124... | collective-permute-start | bytes 1474568 | tf_op jit(solution)/shard_map/ppermute | solution.py:30
  123.2 14.8 %collective-permute-start.18 = (bf16[80,3072]{1,0:T(8,128)(2,1)S(1)}, bf16[80,3072]{1,0:T(8,128)(2,1)S(1)}, u32[]{:S(2)}, u32[]{:S(2)}) collective-permute-start(bf16[80,3072]{1,0:T(8,128)(2,1)S(1)} %constant_dynamic-update-slice_fusion.10.refs_1_), channel_id=1, source_target_pairs={{0,24},{4,28},{8,0},{12,4},{16,8},{20,12},{24,16},{28,20},{32,56},... | collective-permute-start | bytes 1474568 | tf_op jit(solution)/shard_map/ppermute | solution.py:30
  128.1 13.9 %collective-permute-start.30 = (bf16[80,3072]{1,0:T(8,128)(2,1)S(1)}, bf16[80,3072]{1,0:T(8,128)(2,1)S(1)}, u32[]{:S(2)}, u32[]{:S(2)}) collective-permute-start(bf16[80,3072]{1,0:T(8,128)(2,1)S(1)} %constant_dynamic-update-slice_fusion.10.refs_1_), channel_id=1, source_target_pairs={{0,8},{4,12},{8,16},{12,20},{16,24},{20,28},{24,0},{28,4},{32,40},... | collective-permute-start | bytes 1474568 | tf_op jit(solution)/shard_map/ppermute | solution.py:30
  138.0 10.5 %collective-permute-start.14 = (bf16[80,3072]{1,0:T(8,128)(2,1)S(1)}, bf16[80,3072]{1,0:T(8,128)(2,1)S(1)}, u32[]{:S(2)}, u32[]{:S(2)}) collective-permute-start(bf16[80,3072]{1,0:T(8,128)(2,1)S(1)} %pad_maximum_fusion.refs_0_), channel_id=1, source_target_pairs={{0,8},{4,12},{8,16},{12,20},{16,24},{20,28},{24,0},{28,4},{32,40},... | collective-permute-start | bytes 1474568 | tf_op jit(solution)/shard_map/ppermute | solution.py:30
  142.0 20.1 %collective-permute-start.31 = (bf16[80,3072]{1,0:T(8,128)(2,1)S(1)}, bf16[80,3072]{1,0:T(8,128)(2,1)S(1)}, u32[]{:S(2)}, u32[]{:S(2)}) collective-permute-start(bf16[80,3072]{1,0:T(8,128)(2,1)S(1)} %pad_maximum_fusion.refs_0_), channel_id=1, source_target_pairs={{0,24},{4,28},{8,0},{12,4},{16,8},{20,12},{24,16},{28,20},{32,56},... | collective-permute-start | bytes 1474568 | tf_op jit(solution)/shard_map/ppermute | solution.py:30
  148.5 18.7 %collective-permute-start.26 = (bf16[80,3072]{1,0:T(8,128)(2,1)S(1)}, bf16[80,3072]{1,0:T(8,128)(2,1)S(1)}, u32[]{:S(2)}, u32[]{:S(2)}) collective-permute-start(bf16[80,3072]{1,0:T(8,128)(2,1)S(1)} %collective-permute-done.25.refs_7_), channel_id=1, source_target_pairs={{0,96},{4,100},{8,104},{12,108},{16,112},{20,116},{24,120},{28,124... | collective-permute-start | bytes 1474568 | tf_op jit(solution)/shard_map/ppermute | solution.py:30
  150.3 17.0 %collective-permute-start.22 = (bf16[80,3072]{1,0:T(8,128)(2,1)S(1)}, bf16[80,3072]{1,0:T(8,128)(2,1)S(1)}, u32[]{:S(2)}, u32[]{:S(2)}) collective-permute-start(bf16[80,3072]{1,0:T(8,128)(2,1)S(1)} %collective-permute-done.21.refs_4_), channel_id=1, source_target_pairs={{0,32},{4,36},{8,40},{12,44},{16,48},{20,52},{24,56},{28,60},{32,6... | collective-permute-start | bytes 1474568 | tf_op jit(solution)/shard_map/ppermute | solution.py:30
  150.6 16.7 %collective-permute-start.19 = (bf16[80,3072]{1,0:T(8,128)(2,1)S(1)}, bf16[80,3072]{1,0:T(8,128)(2,1)S(1)}, u32[]{:S(2)}, u32[]{:S(2)}) collective-permute-start(bf16[80,3072]{1,0:T(8,128)(2,1)S(1)} %collective-permute-done.18.refs_3_), channel_id=1, source_target_pairs={{0,24},{4,28},{8,0},{12,4},{16,8},{20,12},{24,16},{28,20},{32,56},... | collective-permute-start | bytes 1474568 | tf_op jit(solution)/shard_map/ppermute | solution.py:30
  155.6 11.7 %collective-permute-start.15 = (bf16[80,3072]{1,0:T(8,128)(2,1)S(1)}, bf16[80,3072]{1,0:T(8,128)(2,1)S(1)}, u32[]{:S(2)}, u32[]{:S(2)}) collective-permute-start(bf16[80,3072]{1,0:T(8,128)(2,1)S(1)} %collective-permute-done.14.refs_0_), channel_id=1, source_target_pairs={{0,8},{4,12},{8,16},{12,20},{16,24},{20,28},{24,0},{28,4},{32,40},... | collective-permute-start | bytes 1474568 | tf_op jit(solution)/shard_map/ppermute | solution.py:30
  173.7 13.4 %collective-permute-start.35 = (bf16[80,3072]{1,0:T(8,128)(2,1)S(1)}, bf16[80,3072]{1,0:T(8,128)(2,1)S(1)}, u32[]{:S(2)}, u32[]{:S(2)}) collective-permute-start(bf16[80,3072]{1,0:T(8,128)(2,1)S(1)} %get-tuple-element.53), channel_id=1, source_target_pairs={{0,24},{4,28},{8,0},{12,4},{16,8},{20,12},{24,16},{28,20},{32,56},... | collective-permute-start | bytes 1474568 | tf_op jit(solution)/shard_map/ppermute | solution.py:30
  182.5 25.5 %collective-permute-start.34 = (bf16[80,3072]{1,0:T(8,128)(2,1)S(1)}, bf16[80,3072]{1,0:T(8,128)(2,1)S(1)}, u32[]{:S(2)}, u32[]{:S(2)}) collective-permute-start(bf16[80,3072]{1,0:T(8,128)(2,1)S(1)} %get-tuple-element.51), channel_id=1, source_target_pairs={{0,8},{4,12},{8,16},{12,20},{16,24},{20,28},{24,0},{28,4},{32,40},... | collective-permute-start | bytes 1474568 | tf_op jit(solution)/shard_map/ppermute | solution.py:30
  182.6 15.3 %collective-permute-start.39 = (bf16[80,3072]{1,0:T(8,128)(2,1)S(1)}, bf16[80,3072]{1,0:T(8,128)(2,1)S(1)}, u32[]{:S(2)}, u32[]{:S(2)}) collective-permute-start(bf16[80,3072]{1,0:T(8,128)(2,1)S(1)} %get-tuple-element.57), channel_id=1, source_target_pairs={{0,8},{4,12},{8,16},{12,20},{16,24},{20,28},{24,0},{28,4},{32,40},... | collective-permute-start | bytes 1474568 | tf_op jit(solution)/shard_map/ppermute | solution.py:30
  182.7 34.3 %collective-permute-start.38 = (bf16[80,3072]{1,0:T(8,128)(2,1)S(1)}, bf16[80,3072]{1,0:T(8,128)(2,1)S(1)}, u32[]{:S(2)}, u32[]{:S(2)}) collective-permute-start(bf16[80,3072]{1,0:T(8,128)(2,1)S(1)} %get-tuple-element.55), channel_id=1, source_target_pairs={{0,24},{4,28},{8,0},{12,4},{16,8},{20,12},{24,16},{28,20},{32,56},... | collective-permute-start | bytes 1474568 | tf_op jit(solution)/shard_map/ppermute | solution.py:30
  185.9 13.3 %collective-permute-start.44 = (bf16[80,3072]{1,0:T(8,128)(2,1)S(1)}, bf16[80,3072]{1,0:T(8,128)(2,1)S(1)}, u32[]{:S(2)}, u32[]{:S(2)}) collective-permute-start(bf16[80,3072]{1,0:T(8,128)(2,1)S(1)} %get-tuple-element.61), channel_id=1, source_target_pairs={{0,96},{4,100},{8,104},{12,108},{16,112},{20,116},{24,120},{28,124... | collective-permute-start | bytes 1474568 | tf_op jit(solution)/shard_map/ppermute | solution.py:30
  187.2 33.4 %collective-permute-start.43 = (bf16[80,3072]{1,0:T(8,128)(2,1)S(1)}, bf16[80,3072]{1,0:T(8,128)(2,1)S(1)}, u32[]{:S(2)}, u32[]{:S(2)}) collective-permute-start(bf16[80,3072]{1,0:T(8,128)(2,1)S(1)} %get-tuple-element.59), channel_id=1, source_target_pairs={{0,32},{4,36},{8,40},{12,44},{16,48},{20,52},{24,56},{28,60},{32,6... | collective-permute-start | bytes 1474568 | tf_op jit(solution)/shard_map/ppermute | solution.py:30
  197.9 10.0 %collective-permute-start.48 = (bf16[80,3072]{1,0:T(8,128)(2,1)S(1)}, bf16[80,3072]{1,0:T(8,128)(2,1)S(1)}, u32[]{:S(2)}, u32[]{:S(2)}) collective-permute-start(bf16[80,3072]{1,0:T(8,128)(2,1)S(1)} %get-tuple-element.65), channel_id=1, source_target_pairs={{0,32},{4,36},{8,40},{12,44},{16,48},{20,52},{24,56},{28,60},{32,6... | collective-permute-start | bytes 1474568 | tf_op jit(solution)/shard_map/ppermute | solution.py:30
  199.2 27.5 %collective-permute-start.47 = (bf16[80,3072]{1,0:T(8,128)(2,1)S(1)}, bf16[80,3072]{1,0:T(8,128)(2,1)S(1)}, u32[]{:S(2)}, u32[]{:S(2)}) collective-permute-start(bf16[80,3072]{1,0:T(8,128)(2,1)S(1)} %get-tuple-element.63), channel_id=1, source_target_pairs={{0,96},{4,100},{8,104},{12,108},{16,112},{20,116},{24,120},{28,124... | collective-permute-start | bytes 1474568 | tf_op jit(solution)/shard_map/ppermute | solution.py:30
  208.0 8.8 %collective-permute-start.36 = (bf16[80,3072]{1,0:T(8,128)(2,1)S(1)}, bf16[80,3072]{1,0:T(8,128)(2,1)S(1)}, u32[]{:S(2)}, u32[]{:S(2)}) collective-permute-start(bf16[80,3072]{1,0:T(8,128)(2,1)S(1)} %add_convert_fusion.7), channel_id=1, source_target_pairs={{0,24},{4,28},{8,0},{12,4},{16,8},{20,12},{24,16},{28,20},{32,56},... | collective-permute-start | bytes 1474568 | tf_op jit(solution)/shard_map/ppermute | solution.py:30
  208.1 11.0 %collective-permute-start.40 = (bf16[80,3072]{1,0:T(8,128)(2,1)S(1)}, bf16[80,3072]{1,0:T(8,128)(2,1)S(1)}, u32[]{:S(2)}, u32[]{:S(2)}) collective-permute-start(bf16[80,3072]{1,0:T(8,128)(2,1)S(1)} %add_convert_fusion.5), channel_id=1, source_target_pairs={{0,8},{4,12},{8,16},{12,20},{16,24},{20,28},{24,0},{28,4},{32,40},... | collective-permute-start | bytes 1474568 | tf_op jit(solution)/shard_map/ppermute | solution.py:30
  216.8 8.8 %collective-permute-start.45 = (bf16[80,3072]{1,0:T(8,128)(2,1)S(1)}, bf16[80,3072]{1,0:T(8,128)(2,1)S(1)}, u32[]{:S(2)}, u32[]{:S(2)}) collective-permute-start(bf16[80,3072]{1,0:T(8,128)(2,1)S(1)} %add_convert_fusion.3), channel_id=1, source_target_pairs={{0,96},{4,100},{8,104},{12,108},{16,112},{20,116},{24,120},{28,124... | collective-permute-start | bytes 1474568 | tf_op jit(solution)/shard_map/ppermute | solution.py:30
  217.0 14.2 %collective-permute-start.49 = (bf16[80,3072]{1,0:T(8,128)(2,1)S(1)}, bf16[80,3072]{1,0:T(8,128)(2,1)S(1)}, u32[]{:S(2)}, u32[]{:S(2)}) collective-permute-start(bf16[80,3072]{1,0:T(8,128)(2,1)S(1)} %add_convert_fusion.1), channel_id=1, source_target_pairs={{0,32},{4,36},{8,40},{12,44},{16,48},{20,52},{24,56},{28,60},{32,6... | collective-permute-start | bytes 1474568 | tf_op jit(solution)/shard_map/ppermute | solution.py:30
  219.1 12.9 %collective-permute-start.37 = (bf16[40,3072]{1,0:T(8,128)(2,1)S(1)}, bf16[40,3072]{1,0:T(8,128)(2,1)S(1)}, u32[]{:S(2)}, u32[]{:S(2)}) collective-permute-start(bf16[40,3072]{1,0:T(8,128)(2,1)S(1)} %slice.99), channel_id=1, source_target_pairs={{0,96},{4,100},{8,104},{12,108},{16,112},{20,116},{24,120},{28,124... | collective-permute-start | bytes 737288 | tf_op jit(solution)/shard_map/ppermute | solution.py:30
  220.6 13.4 %collective-permute-start.41 = (bf16[40,3072]{1,0:T(8,128)(2,1)S(1)}, bf16[40,3072]{1,0:T(8,128)(2,1)S(1)}, u32[]{:S(2)}, u32[]{:S(2)}) collective-permute-start(bf16[40,3072]{1,0:T(8,128)(2,1)S(1)} %get-tuple-element.68), channel_id=1, source_target_pairs={{0,64},{4,68},{8,72},{12,76},{16,80},{20,84},{24,88},{28,92},{32,9... | collective-permute-start | bytes 737288 | tf_op jit(solution)/shard_map/ppermute | solution.py:30
  225.6 8.3 %collective-permute-start.42 = (bf16[40,3072]{1,0:T(8,128)(2,1)S(1)}, bf16[40,3072]{1,0:T(8,128)(2,1)S(1)}, u32[]{:S(2)}, u32[]{:S(2)}) collective-permute-start(bf16[40,3072]{1,0:T(8,128)(2,1)S(1)} %get-tuple-element.69), channel_id=1, source_target_pairs={{0,32},{4,36},{8,40},{12,44},{16,48},{20,52},{24,56},{28,60},{32,6... | collective-permute-start | bytes 737288 | tf_op jit(solution)/shard_map/ppermute | solution.py:30
  226.8 7.3 %collective-permute-start.46 = (bf16[40,3072]{1,0:T(8,128)(2,1)S(1)}, bf16[40,3072]{1,0:T(8,128)(2,1)S(1)}, u32[]{:S(2)}, u32[]{:S(2)}) collective-permute-start(bf16[40,3072]{1,0:T(8,128)(2,1)S(1)} %slice.105), channel_id=1, source_target_pairs={{0,24},{4,28},{8,0},{12,4},{16,8},{20,12},{24,16},{28,20},{32,56},... | collective-permute-start | bytes 737288 | tf_op jit(solution)/shard_map/ppermute | solution.py:30
  231.5 15.1 %copy-start.3 = (f32[128,2]{0,1:T(2,128)S(1)}, f32[128,2]{0,1:T(2,128)}, u32[]{:S(2)}) copy-start(f32[128,2]{0,1:T(2,128)} %param.22) | copy-start | bytes 3076
  231.5 7.9 %collective-permute-start.50 = (bf16[40,3072]{1,0:T(8,128)(2,1)S(1)}, bf16[40,3072]{1,0:T(8,128)(2,1)S(1)}, u32[]{:S(2)}, u32[]{:S(2)}) collective-permute-start(bf16[40,3072]{1,0:T(8,128)(2,1)S(1)} %get-tuple-element.70), channel_id=1, source_target_pairs={{0,16},{4,20},{8,24},{12,28},{16,0},{20,4},{24,8},{28,12},{32,48},... | collective-permute-start | bytes 737288 | tf_op jit(solution)/shard_map/ppermute | solution.py:30
  232.0 10.0 %collective-permute-start.51 = (bf16[40,3072]{1,0:T(8,128)(2,1)S(1)}, bf16[40,3072]{1,0:T(8,128)(2,1)S(1)}, u32[]{:S(2)}, u32[]{:S(2)}) collective-permute-start(bf16[40,3072]{1,0:T(8,128)(2,1)S(1)} %get-tuple-element.71), channel_id=1, source_target_pairs={{0,8},{4,12},{8,16},{12,20},{16,24},{20,28},{24,0},{28,4},{32,40},... | collective-permute-start | bytes 737288 | tf_op jit(solution)/shard_map/ppermute | solution.py:30
  242.9 11.6 %all-to-all-start.1 = ((bf16[4,40,1536]{2,1,0:T(8,128)(2,1)}), bf16[4,40,1536]{2,1,0:T(8,128)(2,1)S(1)}, u32[]{:S(2)}, u32[]{:S(2)}) async-start(bf16[4,40,1536]{2,1,0:T(8,128)(2,1)} %pad_maximum_fusion.2), calls=%async_computation.1 | async-start | bytes 983040 | tf_op jit(solution)/shard_map/all_to_all | solution.py:511

commit v2 on v1

--- a/solution.py
+++ b/solution.py
@@ -41,7 +41,7 @@
 
 
 def attention_kernel(
-    rank_ref, order_ref, q_hbm, own_ref, other_ref, docs_hbm, weight_hbm, *rest
+    place_ref, q_hbm, own_ref, other_ref, docs_hbm, weight_hbm, *rest
 ):
     *outs, q_ref, docs_ref, kv_ref, bias_ref, attended_ref, weight_ref, sems = rest
     tokens = q_ref.shape[0]
@@ -49,7 +49,7 @@
     quarter = weight_ref.shape[2]
 
     def fetch(d):
-        at = ((rank_ref[1] + SIDE - d) % SIDE) * quarter
+        at = ((place_ref[1] + SIDE - d) % SIDE) * quarter
         return pltpu.make_async_copy(
             weight_hbm.at[:, pl.ds(pl.multiple_of(at, HD), quarter)], weight_ref.at[d], sems.at[d]
         )
@@ -61,18 +61,18 @@
     for d in range(SIDE):
         fetch(d).start()
 
-    rank = rank_ref[0]
+    rank = place_ref[0]
     core = rank % 2
     z = (rank // 2) % SIDE
     y = rank // (2 * SIDE)
-    placed = order_ref[rank]
+    placed = place_ref[2 + rank]
     first_block = placed - (WINDOW - 1)
 
     def place_from(source, slot_core):
         def place(in_half, carry):
             slot_y = (y + SIDE - in_half % SIDE) % SIDE
             slot_z = (z + SIDE - in_half // SIDE) % SIDE
-            at = order_ref[(slot_y * SIDE + slot_z) * 2 + slot_core] - first_block
+            at = place_ref[2 + (slot_y * SIDE + slot_z) * 2 + slot_core] - first_block
 
             @pl.when((at >= 0) & (at < WINDOW))
             def _():
@@ -110,8 +110,8 @@
     lax.fori_loop(0, WINDOW, mask, 0)
     q_copy.wait()
 
-    def head(h, carry):
-        at = pl.ds(pl.multiple_of(h * HD, HD), HD)
+    def head(h):
+        at = slice(h * HD, (h + 1) * HD)
         scores = lax.dot_general(
             q_ref[:, at], kv_ref[:, :HD], (((1,), (1,)), ((), ())), preferred_element_type=jnp.float32
         )
@@ -122,9 +122,9 @@
             weights.astype(jnp.bfloat16), kv_ref[:, HD:], preferred_element_type=jnp.float32
         )
         attended_ref[:, at] = (mix / total).astype(jnp.bfloat16)
-        return carry
-
-    lax.fori_loop(0, heads, head, 0)
+
+    for h in range(heads):
+        head(h)
     for d in range(SIDE):
         fetch(d).wait()
         part = jnp.dot(attended_ref[...], weight_ref[d], preferred_element_type=jnp.float32)
@@ -133,7 +133,7 @@
         outs[2 * d + 1][...] = part[tokens // 2 :]
 
 
-def attend_and_project(ranks, order, queries, own, other, docs, out_weight):
+def attend_and_project(place, queries, own, other, docs, out_weight):
     tokens, inner = queries.shape
     quarter = out_weight.shape[1] // SIDE
     smem = pl.BlockSpec(memory_space=pltpu.SMEM)
@@ -143,7 +143,7 @@
     outs = pl.pallas_call(
         attention_kernel,
         out_shape=[jax.ShapeDtypeStruct((tokens // 2, quarter), jnp.bfloat16)] * (2 * SIDE),
-        in_specs=[smem, smem, far, vmem, vmem, far, far],
+        in_specs=[smem, far, vmem, vmem, far, far],
         out_specs=[vmem] * (2 * SIDE),
         scratch_shapes=[
             pltpu.VMEM(queries.shape, queries.dtype),
@@ -156,12 +156,11 @@
         ],
         compiler_params=pltpu.CompilerParams(vmem_limit_bytes=20 * 1024 * 1024),
         name="attention",
-    )(ranks, order, queries, own, other, docs, out_weight)
+    )(place, queries, own, other, docs, out_weight)
     return [(outs[2 * d], outs[2 * d + 1]) for d in range(SIDE)]
 
 
 TILE = 256
-OWN_LIMIT = 12
 
 
 def tiles(width, body):
@@ -218,34 +217,32 @@
 
 
 def own_kernel(*refs):
-    pieces, lifts, downs = refs[:4], refs[4:8], refs[8:10]
-    own_ref, weight_ref, down_ref, lift_sems, down_sems = refs[10:]
-    units = downs[0].shape[0]
-
-    def lift_copy(source, n):
+    pieces, lifts, (own_ref, weight_ref, sems) = refs[:4], refs[4:8], refs[8:]
+
+    def fetch(source, n):
         cols = pl.ds(pl.multiple_of(n * TILE, TILE), TILE)
-        return pltpu.make_async_copy(source, weight_ref.at[:, cols], lift_sems.at[n])
-
-    down_copies = [
-        pltpu.make_async_copy(ref, down_ref.at[i * units : (i + 1) * units, :], down_sems.at[i])
-        for i, ref in enumerate(downs)
-    ]
+        return pltpu.make_async_copy(source, weight_ref.at[:, cols], sems.at[n])
+
     for n, ref in enumerate(lifts):
-        lift_copy(ref, n).start()
-    for copy in down_copies:
-        copy.start()
+        fetch(ref, n).start()
     lift_groups(
         [(0, 0, pieces[0], pieces[1]), (1, 0, pieces[2], pieces[3])],
         weight_ref,
         own_ref,
-        lambda n: lift_copy(lifts[0], n).wait(),
-    )
-    for copy in down_copies:
-        copy.wait()
+        lambda n: fetch(lifts[0], n).wait(),
+    )
 
 
 def early_kernel(*refs):
-    pieces, own_ref, weight_ref, (sums_ref, hidden_a, hidden_b) = refs[:8], refs[8], refs[9], refs[10:]
+    pieces, own_ref, weight_ref, downs = refs[:8], refs[8], refs[9], refs[10:12]
+    sums_ref, hidden_a, hidden_b, down_ref, sems = refs[12:]
+    units = downs[0].shape[0]
+    copies = [
+        pltpu.make_async_copy(ref, down_ref.at[i * units : (i + 1) * units, :], sems.at[i])
+        for i, ref in enumerate(downs)
+    ]
+    for copy in copies:
+        copy.start()
     groups = []
     for lane in range(2):
         for k in range(len(SIDES)):
@@ -262,6 +259,8 @@
         )
 
     each_side(outer)
+    for copy in copies:
+        copy.wait()
 
 
 def lower_groups(hidden_refs, down_ref, outs):
@@ -316,7 +315,7 @@
     return [pltpu.with_memory_space_constraint(a, pltpu.HBM) for a in arrays]
 
 
-def in_vmem(kernel, out_shapes, operands, scratch=(), aliases=None, hbm=(), limit=12):
+def in_vmem(kernel, out_shapes, operands, scratch=(), aliases=None, hbm=()):
     vmem = pl.BlockSpec(memory_space=pltpu.VMEM)
     far = pl.BlockSpec(memory_space=pltpu.HBM)
     return pl.pallas_call(
@@ -326,7 +325,7 @@
         out_specs=[vmem] * len(out_shapes),
         scratch_shapes=list(scratch),
         input_output_aliases=aliases or {},
-        compiler_params=pltpu.CompilerParams(vmem_limit_bytes=limit * 1024 * 1024),
+        compiler_params=pltpu.CompilerParams(vmem_limit_bytes=12 * 1024 * 1024),
     )(*operands)
 
 
@@ -337,23 +336,28 @@
     both = 2 * units
     hidden = jax.ShapeDtypeStruct((SIDE * rows, units), jnp.float32)
     part = jax.ShapeDtypeStruct(piece.shape, jnp.bfloat16)
-    own_sums, weight, down = in_vmem(
+    own_sums, weight = in_vmem(
         own_kernel,
         [
             jax.ShapeDtypeStruct((2, rows, both), jnp.float32),
             jax.ShapeDtypeStruct((lifts[0].shape[0], both), piece.dtype),
+        ],
+        [*a_groups[0], *b_groups[0], *in_hbm(lifts)],
+        [pltpu.SemaphoreType.DMA((len(lifts),))],
+        hbm=range(4, 8),
+    )
+    sides = [p for groups in (a_groups, b_groups) for d in SIDES for p in groups[d]]
+    sums, early_a, early_b, down = in_vmem(
+        early_kernel,
+        [
+            jax.ShapeDtypeStruct((2, len(SIDES) * rows, both), jnp.float32),
+            hidden,
+            hidden,
             jax.ShapeDtypeStruct((units, downs[0].shape[1]), piece.dtype),
         ],
-        [*a_groups[0], *b_groups[0], *in_hbm(lifts), *in_hbm(downs)],
-        [pltpu.SemaphoreType.DMA((len(lifts),)), pltpu.SemaphoreType.DMA((len(downs),))],
-        hbm=range(4, 10),
-        limit=OWN_LIMIT,
-    )
-    sides = [p for groups in (a_groups, b_groups) for d in SIDES for p in groups[d]]
-    sums, early_a, early_b = in_vmem(
-        early_kernel,
-        [jax.ShapeDtypeStruct((2, len(SIDES) * rows, both), jnp.float32), hidden, hidden],
-        [*sides, own_sums, weight],
+        [*sides, own_sums, weight, *in_hbm(downs)],
+        [pltpu.SemaphoreType.DMA((len(downs),))],
+        hbm=(10, 11),
     )
     operands = [*a_groups[LAST], *b_groups[LAST], weight, own_sums, sums, down, early_a, early_b]
     hidden_a, hidden_b, *first = in_vmem(
@@ -444,8 +448,7 @@
     kv_other = shifted(kv_own, 0, 0, 1)
 
     projected = attend_and_project(
-        jnp.stack([cp_rank, ep_rank]).astype(jnp.int32),
-        block_order,
+        jnp.concatenate([jnp.stack([cp_rank, ep_rank]).astype(jnp.int32), block_order]),
         queries,
         kv_own,
         kv_other,

time: 256 us -> 256 us (level)
  waiting for transfers between devices: 125 us -> 135 us
  starting transfers between devices: 87.5 us -> 80.4 us
    ppermute x46, waiting for transfers between devices: 103 us -> 113 us  [shifted(): return lax.ppermute(array, 'cp', pairs)]
    ppermute x46, starting transfers between devices: 70.1 us -> 63.2 us  [shifted(): return lax.ppermute(array, 'cp', pairs)]
  transfers between devices with their start and end apart: 54 -> 54, of which waited for: 30 -> 30; matrix products, arithmetic and copies ran while one was open for 2% -> 2% of each run, Pallas kernels for 7% -> 6%
where the time goes in v2:
time: 256 us
  waiting for transfers between devices  135 us (53%)
  starting transfers between devices  80.4 us (31%)
  Pallas kernels  29.1 us (11%)
  other arithmetic  5.53 us (2%)
  local copies, waits for them, and re-layouts  2.96 us (1%)
    ppermute x46, waiting for transfers between devices, shifted(): return lax.ppermute(array, 'cp', pairs)  113 us
    ppermute x46, starting transfers between devices, shifted(): return lax.ppermute(array, 'cp', pairs)  63.2 us
    pallas_call x4, Pallas kernels, in_vmem(): pl.pallas_call(kernel, out_shape=out_shapes, in_specs=[far if i in hbm el...  22.5 us
    ppermute x6, starting transfers between devices, along(): lax.ppermute(array, 'ep', [(i, (i + step) % SIDE) for i in range(SIDE)])  9.47 us
    all_to_all x1, waiting for transfers between devices, local(): back = lax.all_to_all(back, 'ep', split_axis=0, concat_axis=0, tiled=True)  7.64 us
    all_to_all x1, waiting for transfers between devices, local(): lax.all_to_all(rows.reshape(SIDE, CAP, quarter), 'ep', split_axis=0, conc...  7.52 us
    ppermute x6, waiting for transfers between devices, along(): lax.ppermute(array, 'ep', [(i, (i + step) % SIDE) for i in range(SIDE)])  6.65 us
    pallas_call x1, Pallas kernels, attend_and_project(): pl.pallas_call(attention_kernel, out_shape=[jax.ShapeDtypeStruct((tokens...  6.59 us
  transfers between devices with their start and end apart: 54, of which 30 were waited for; matrix products, arithmetic and copies ran while one was open for 2% of the time, Pallas kernels for 6%

profile of v2, /device:TPU:0, one launch (start us, length us, event | category | flops | bytes accessed | tf_op | source)
XLA Modules:
  0.0 256.0 jit_solution(13397908090853280073)
XLA Ops:
  2.2 1.8 collective-permute-start
  3.9 2.9 %collective-permute-start.1 = (bf16[128,256]{1,0:T(8,128)(2,1)S(1)}, bf16[128,256]{1,0:T(8,128)(2,1)S(1)}, u32[]{:S(2)}, u32[]{:S(2)}) collective-permute-start(bf16[128,256]{1,0:T(8,128)(2,1)S(1)} %get-tuple-element.80), channel_id=1, source_target_pairs={{0,64},{4,68},{8,72},{12,76},{16,80},{20,84},{24,88},{28,92},{32,9... | collective-permute-start | bytes 196616 | tf_op jit(solution)/shard_map/ppermute | solution.py:30
  6.8 1.3 collective-permute-start.2
  8.2 1.9 collective-permute-done.1
  11.1 2.0 collective-permute-start.3
  13.1 3.6 %collective-permute-start.4 = (bf16[512,256]{1,0:T(8,128)(2,1)S(1)}, bf16[512,256]{1,0:T(8,128)(2,1)S(1)}, u32[]{:S(2)}, u32[]{:S(2)}) collective-permute-start(bf16[512,256]{1,0:T(8,128)(2,1)S(1)} %pad_maximum_fusion.4), channel_id=1, source_target_pairs={{0,16},{4,20},{8,24},{12,28},{16,0},{20,4},{24,8},{28,12},{32,48},... | collective-permute-start | bytes 786440 | tf_op jit(solution)/shard_map/ppermute | solution.py:30
  17.7 3.8 %collective-permute-done.3 = bf16[512,256]{1,0:T(8,128)(2,1)S(1)} collective-permute-done((bf16[512,256]{1,0:T(8,128)(2,1)S(1)}, bf16[512,256]{1,0:T(8,128)(2,1)S(1)}, u32[]{:S(2)}, u32[]{:S(2)}) %collective-permute-start.3) | collective-permute-done | bytes 262176 | tf_op jit(solution)/shard_map/ppermute | solution.py:30
  21.5 5.4 %collective-permute-done.4 = bf16[512,256]{1,0:T(8,128)(2,1)S(1)} collective-permute-done((bf16[512,256]{1,0:T(8,128)(2,1)S(1)}, bf16[512,256]{1,0:T(8,128)(2,1)S(1)}, u32[]{:S(2)}, u32[]{:S(2)}) %collective-permute-start.4) | collective-permute-done | bytes 262176 | tf_op jit(solution)/shard_map/ppermute | solution.py:30
  28.6 1.1 collective-permute-done.6.other_ref
  29.7 6.6 %attention.1 = (bf16[64,1536]{1,0:T(8,128)(2,1)S(1)}, bf16[64,1536]{1,0:T(8,128)(2,1)S(1)}, bf16[64,1536]{1,0:T(8,128)(2,1)S(1)}, bf16[64,1536]{1,0:T(8,128)(2,1...) custom-call(s32[34]{0:T(128)S(1)} %pad_add_fusion.place_ref, ...), custom_call_target="tpu_custom_call" | custom-call | tf_op jit(solution)/shard_map/attention/pallas_call | solution.py:143
  36.3 1.6 collective-permute-start.11
  38.2 1.8 collective-permute-start.8
  40.0 1.5 collective-permute-start.10
  42.0 2.9 %collective-permute-done.11 = bf16[64,1536]{1,0:T(8,128)(2,1)S(1)} collective-permute-done((bf16[64,1536]{1,0:T(8,128)(2,1)}, bf16[64,1536]{1,0:T(8,128)(2,1)S(1)}, u32[]{:S(2)}, u32[]{:S(2)}) %collective-permute-start.11) | collective-permute-done | bytes 196640 | tf_op jit(solution)/shard_map/ppermute | solution.py:35
  46.0 3.0 %collective-permute-start.9 = (bf16[64,1536]{1,0:T(8,128)(2,1)S(1)}, bf16[64,1536]{1,0:T(8,128)(2,1)S(1)}, u32[]{:S(2)}, u32[]{:S(2)}) collective-permute-start(bf16[64,1536]{1,0:T(8,128)(2,1)S(1)} %add_convert_fusion.13), channel_id=1, source_target_pairs={{0,3},{1,0},{2,1},{3,2},{4,7},{5,4},{6,5},{7,6},{8,11},{9,8},{10,9... | collective-permute-start | bytes 589832 | tf_op jit(solution)/shard_map/ppermute | solution.py:35
  50.2 3.0 %collective-permute-done.12 = bf16[64,1536]{1,0:T(8,128)(2,1)S(1)} collective-permute-done((bf16[64,1536]{1,0:T(8,128)(2,1)S(1)}, bf16[64,1536]{1,0:T(8,128)(2,1)S(1)}, u32[]{:S(2)}, u32[]{:S(2)}) %collective-permute-start.12) | collective-permute-done | bytes 196640 | tf_op jit(solution)/shard_map/ppermute | solution.py:35
  53.3 1.2 add_convert_fusion.12
  55.7 4.2 %all-to-all-start = ((bf16[4,40,1536]{2,1,0:T(8,128)(2,1)}), bf16[4,40,1536]{2,1,0:T(8,128)(2,1)S(1)}, u32[]{:S(2)}, u32[]{:S(2)}) async-start(bf16[4,40,1536]{2,1,0:T(8,128)(2,1)} %bitcast.9), calls=%async_computation | async-start | bytes 983040 | tf_op jit(solution)/shard_map/all_to_all | solution.py:484
  60.4 7.5 %all-to-all-done = bf16[4,40,1536]{2,1,0:T(8,128)(2,1)S(1)} async-done(((bf16[4,40,1536]{2,1,0:T(8,128)(2,1)}), bf16[4,40,1536]{2,1,0:T(8,128)(2,1)S(1)}, u32[]{:S(2)}, u32[]{:S(2)}) %all-to-all-start) | async-done | bytes 491552 | tf_op jit(solution)/shard_map/all_to_all | solution.py:484
  68.4 2.3 collective-permute-start.23
  70.7 1.7 collective-permute-start.24
  72.4 3.8 %collective-permute-done.23 = bf16[40,3072]{1,0:T(8,128)(2,1)S(1)} collective-permute-done((bf16[40,3072]{1,0:T(8,128)(2,1)S(1)}, bf16[40,3072]{1,0:T(8,128)(2,1)S(1)}, u32[]{:S(2)}, u32[]{:S(2)}) %collective-permute-start.23) | collective-permute-done | bytes 245792 | tf_op jit(solution)/shard_map/ppermute | solution.py:30
  76.2 3.0 %collective-permute-start.20 = (bf16[40,3072]{1,0:T(8,128)(2,1)S(1)}, bf16[40,3072]{1,0:T(8,128)(2,1)S(1)}, u32[]{:S(2)}, u32[]{:S(2)}) collective-permute-start(bf16[40,3072]{1,0:T(8,128)(2,1)S(1)} %pad_maximum_fusion.6), channel_id=1, source_target_pairs={{0,8},{4,12},{8,16},{12,20},{16,24},{20,28},{24,0},{28,4},{32,40},... | collective-permute-start | bytes 737288 | tf_op jit(solution)/shard_map/ppermute | solution.py:30
  79.9 1.5 collective-permute-start.16
  81.4 2.7 %collective-permute-done.20 = bf16[40,3072]{1,0:T(8,128)(2,1)S(1)} collective-permute-done((bf16[40,3072]{1,0:T(8,128)(2,1)S(1)}, bf16[40,3072]{1,0:T(8,128)(2,1)S(1)}, u32[]{:S(2)}, u32[]{:S(2)}) %collective-permute-start.20) | collective-permute-done | bytes 245792 | tf_op jit(solution)/shard_map/ppermute | solution.py:30
  84.2 2.4 collective-permute-start.17
  86.5 1.1 collective-permute-done.16
  87.7 1.8 collective-permute-start.13
  89.5 3.0 %collective-permute-done.17 = bf16[40,3072]{1,0:T(8,128)(2,1)S(1)} collective-permute-done((bf16[40,3072]{1,0:T(8,128)(2,1)S(1)}, bf16[40,3072]{1,0:T(8,128)(2,1)S(1)}, u32[]{:S(2)}, u32[]{:S(2)}) %collective-permute-start.17) | collective-permute-done | bytes 245792 | tf_op jit(solution)/shard_map/ppermute | solution.py:30
  92.5 1.7 collective-permute-start.25
  94.1 3.2 %collective-permute-done.13 = bf16[40,3072]{1,0:T(8,128)(2,1)S(1)} collective-permute-done((bf16[40,3072]{1,0:T(8,128)(2,1)S(1)}, bf16[40,3072]{1,0:T(8,128)(2,1)S(1)}, u32[]{:S(2)}, u32[]{:S(2)}) %collective-permute-start.13) | collective-permute-done | bytes 245792 | tf_op jit(solution)/shard_map/ppermute | solution.py:30
  98.2 3.8 %collective-permute-done.25.refs_7_ = bf16[80,3072]{1,0:T(8,128)(2,1)S(1)} collective-permute-done((bf16[80,3072]{1,0:T(8,128)(2,1)S(1)}, bf16[80,3072]{1,0:T(8,128)(2,1)S(1)}, u32[]{:S(2)}, u32[]{:S(2)}) %collective-permute-start.25) | collective-permute-done | bytes 491552 | tf_op jit(solution)/shard_map/ppermute | solution.py:30
  102.8 9.1 %collective-permute-done.31.refs_5_ = bf16[80,3072]{1,0:T(8,128)(2,1)S(1)} collective-permute-done((bf16[80,3072]{1,0:T(8,128)(2,1)S(1)}, bf16[80,3072]{1,0:T(8,128)(2,1)S(1)}, u32[]{:S(2)}, u32[]{:S(2)}) %collective-permute-start.31) | collective-permute-done | bytes 491552 | tf_op jit(solution)/shard_map/ppermute | solution.py:30
  111.9 1.6 collective-permute-start.32
  113.5 3.6 %collective-permute-done.21.refs_4_ = bf16[80,3072]{1,0:T(8,128)(2,1)S(1)} collective-permute-done((bf16[80,3072]{1,0:T(8,128)(2,1)S(1)}, bf16[80,3072]{1,0:T(8,128)(2,1)S(1)}, u32[]{:S(2)}, u32[]{:S(2)}) %collective-permute-start.21) | collective-permute-done | bytes 491552 | tf_op jit(solution)/shard_map/ppermute | solution.py:30
  117.2 4.0 %collective-permute-start.18 = (bf16[80,3072]{1,0:T(8,128)(2,1)S(1)}, bf16[80,3072]{1,0:T(8,128)(2,1)S(1)}, u32[]{:S(2)}, u32[]{:S(2)}) collective-permute-start(bf16[80,3072]{1,0:T(8,128)(2,1)S(1)} %constant_dynamic-update-slice_fusion.10.refs_1_), channel_id=1, source_target_pairs={{0,24},{4,28},{8,0},{12,4},{16,8},{20,12},{24,16},{28,20},{32,56},... | collective-permute-start | bytes 1474568 | tf_op jit(solution)/shard_map/ppermute | solution.py:30
  121.3 9.6 %collective-permute-done.18.refs_3_ = bf16[80,3072]{1,0:T(8,128)(2,1)S(1)} collective-permute-done((bf16[80,3072]{1,0:T(8,128)(2,1)S(1)}, bf16[80,3072]{1,0:T(8,128)(2,1)S(1)}, u32[]{:S(2)}, u32[]{:S(2)}) %collective-permute-start.18) | collective-permute-done | bytes 491552 | tf_op jit(solution)/shard_map/ppermute | solution.py:30
  130.9 1.7 collective-permute-start.14
  132.7 2.3 collective-permute-done.29.refs_1_
  134.9 9.3 %collective-permute-done.14.refs_0_ = bf16[80,3072]{1,0:T(8,128)(2,1)S(1)} collective-permute-done((bf16[80,3072]{1,0:T(8,128)(2,1)S(1)}, bf16[80,3072]{1,0:T(8,128)(2,1)S(1)}, u32[]{:S(2)}, u32[]{:S(2)}) %collective-permute-start.14) | collective-permute-done | bytes 491552 | tf_op jit(solution)/shard_map/ppermute | solution.py:30
  144.2 2.0 collective-permute-start.26
  146.8 1.6 collective-permute-start.15
  148.4 5.4 %shard_map.140 = (f32[2,160,1024]{2,1,0:T(8,128)S(1)}, bf16[6144,1024]{1,0:T(8,128)(2,1)S(1)}) custom-call(bf16[80,3072]{1,0:T(8,128)(2,1)S(1)} %pad_maximum_fusion.refs_0_, bf16[80,3072]{1,0:T(8,128)(2,1)S(1)} %constant_dynamic-update-slice_fusion.10.refs_1_, bf16[80,3072]{1,0:T(8,128)(2,1)S(1)} %pad_maximum_fusion.1.refs_2_, ...), custom_call_target="tpu_custom_call" | custom-call | tf_op jit(solution)/shard_map/pallas_call | solution.py:321
  153.8 5.2 %shard_map.141 = (f32[2,320,1024]{2,1,0:T(8,128)S(1)}, f32[640,512]{1,0:T(8,128)S(1)}, f32[640,512]{1,0:T(8,128)S(1)}, bf16[512,6144]{1,0:T(8,128)(2,1)S(1)}) custom-call(bf16[80,3072]{1,0:T(8,128)(2,1)S(1)} %collective-permute-done.14.refs_0_, bf16[80,3072]{1,0:T(8,128)(2,1)S(1)} %collective-permute-done.29.refs_1_, ...), custom_call_target="tpu_custom_call" | custom-call | tf_op jit(solution)/shard_map/pallas_call | solution.py:321
  159.0 6.4 %shard_map.142 = (f32[640,512]{1,0:T(8,128)S(1)}, f32[640,512]{1,0:T(8,128)S(1)}, bf16[80,3072]{1,0:T(8,128)(2,1)S(1)}, bf16[80,3072]{1,0:T(8,128)(2,1)S(1)}, bf...) custom-call(bf16[80,3072]{1,0:T(8,128)(2,1)S(1)} %collective-permute-done.1, ...), custom_call_target="tpu_custom_call", output_to_operand_aliasing={{0}: (8, {}), {1}: (9, {})} | custom-call | tf_op jit(solution)/shard_map/pallas_call | solution.py:321
  165.4 1.7 collective-permute-start.35
  167.1 5.5 %shard_map.143 = (bf16[80,3072]{1,0:T(8,128)(2,1)S(1)}, bf16[80,3072]{1,0:T(8,128)(2,1)S(1)}, bf16[80,3072]{1,0:T(8,128)(2,1)S(1)}, bf16[80,3072]{1,0:T(8,128)(2...) custom-call(f32[640,512]{1,0:T(8,128)S(1)} %get-tuple-element.48.hid, ...), custom_call_target="tpu_custom_call" | custom-call | tf_op jit(solution)/shard_map/pallas_call | solution.py:321
  173.3 3.0 %collective-permute-start.38 = (bf16[80,3072]{1,0:T(8,128)(2,1)S(1)}, bf16[80,3072]{1,0:T(8,128)(2,1)S(1)}, u32[]{:S(2)}, u32[]{:S(2)}) collective-permute-start(bf16[80,3072]{1,0:T(8,128)(2,1)S(1)} %get-tuple-element.55), channel_id=1, source_target_pairs={{0,24},{4,28},{8,0},{12,4},{16,8},{20,12},{24,16},{28,20},{32,56},... | collective-permute-start | bytes 1474568 | tf_op jit(solution)/shard_map/ppermute | solution.py:30
  176.3 3.2 %collective-permute-start.44 = (bf16[80,3072]{1,0:T(8,128)(2,1)S(1)}, bf16[80,3072]{1,0:T(8,128)(2,1)S(1)}, u32[]{:S(2)}, u32[]{:S(2)}) collective-permute-start(bf16[80,3072]{1,0:T(8,128)(2,1)S(1)} %get-tuple-element.61), channel_id=1, source_target_pairs={{0,96},{4,100},{8,104},{12,108},{16,112},{20,116},{24,120},{28,124... | collective-permute-start | bytes 1474568 | tf_op jit(solution)/shard_map/ppermute | solution.py:30
  179.6 15.1 %collective-permute-done.39 = bf16[80,3072]{1,0:T(8,128)(2,1)S(1)} collective-permute-done((bf16[80,3072]{1,0:T(8,128)(2,1)S(1)}, bf16[80,3072]{1,0:T(8,128)(2,1)S(1)}, u32[]{:S(2)}, u32[]{:S(2)}) %collective-permute-start.39) | collective-permute-done | bytes 491552 | tf_op jit(solution)/shard_map/ppermute | solution.py:30
  194.9 3.3 %collective-permute-start.47 = (bf16[80,3072]{1,0:T(8,128)(2,1)S(1)}, bf16[80,3072]{1,0:T(8,128)(2,1)S(1)}, u32[]{:S(2)}, u32[]{:S(2)}) collective-permute-start(bf16[80,3072]{1,0:T(8,128)(2,1)S(1)} %get-tuple-element.63), channel_id=1, source_target_pairs={{0,96},{4,100},{8,104},{12,108},{16,112},{20,116},{24,120},{28,124... | collective-permute-start | bytes 1474568 | tf_op jit(solution)/shard_map/ppermute | solution.py:30
  198.3 7.0 %collective-permute-done.48 = bf16[80,3072]{1,0:T(8,128)(2,1)S(1)} collective-permute-done((bf16[80,3072]{1,0:T(8,128)(2,1)S(1)}, bf16[80,3072]{1,0:T(8,128)(2,1)S(1)}, u32[]{:S(2)}, u32[]{:S(2)}) %collective-permute-start.48) | collective-permute-done | bytes 491552 | tf_op jit(solution)/shard_map/ppermute | solution.py:30
  205.4 2.1 collective-permute-start.40
  207.5 6.6 %collective-permute-done.36 = bf16[80,3072]{1,0:T(8,128)(2,1)S(1)} collective-permute-done((bf16[80,3072]{1,0:T(8,128)(2,1)S(1)}, bf16[80,3072]{1,0:T(8,128)(2,1)S(1)}, u32[]{:S(2)}, u32[]{:S(2)}) %collective-permute-start.36) | collective-permute-done | bytes 491552 | tf_op jit(solution)/shard_map/ppermute | solution.py:30
  214.1 1.3 collective-permute-start.45
  216.5 2.6 collective-permute-start.37
  219.3 7.4 %collective-permute-done.45 = bf16[80,3072]{1,0:T(8,128)(2,1)S(1)} collective-permute-done((bf16[80,3072]{1,0:T(8,128)(2,1)S(1)}, bf16[80,3072]{1,0:T(8,128)(2,1)S(1)}, u32[]{:S(2)}, u32[]{:S(2)}) %collective-permute-start.45) | collective-permute-done | bytes 491552 | tf_op jit(solution)/shard_map/ppermute | solution.py:30
  227.0 1.6 collective-permute-start.46
  228.6 3.1 %collective-permute-done.49 = bf16[80,3072]{1,0:T(8,128)(2,1)S(1)} collective-permute-done((bf16[80,3072]{1,0:T(8,128)(2,1)S(1)}, bf16[80,3072]{1,0:T(8,128)(2,1)S(1)}, u32[]{:S(2)}, u32[]{:S(2)}) %collective-permute-start.49) | collective-permute-done | bytes 491552 | tf_op jit(solution)/shard_map/ppermute | solution.py:30
  232.3 2.0 collective-permute-start.51
  234.5 5.3 %collective-permute-done.50 = bf16[40,3072]{1,0:T(8,128)(2,1)S(1)} collective-permute-done((bf16[40,3072]{1,0:T(8,128)(2,1)S(1)}, bf16[40,3072]{1,0:T(8,128)(2,1)S(1)}, u32[]{:S(2)}, u32[]{:S(2)}) %collective-permute-start.50) | collective-permute-done | bytes 245792 | tf_op jit(solution)/shard_map/ppermute | solution.py:30
  239.8 2.5 collective-permute-done.51
  243.3 3.5 %all-to-all-start.1 = ((bf16[4,40,1536]{2,1,0:T(8,128)(2,1)}), bf16[4,40,1536]{2,1,0:T(8,128)(2,1)S(1)}, u32[]{:S(2)}, u32[]{:S(2)}) async-start(bf16[4,40,1536]{2,1,0:T(8,128)(2,1)} %pad_maximum_fusion.2), calls=%async_computation.1 | async-start | bytes 983040 | tf_op jit(solution)/shard_map/all_to_all | solution.py:514
  247.0 7.6 %all-to-all-done.1 = bf16[4,40,1536]{2,1,0:T(8,128)(2,1)S(1)} async-done(((bf16[4,40,1536]{2,1,0:T(8,128)(2,1)}), bf16[4,40,1536]{2,1,0:T(8,128)(2,1)S(1)}, u32[]{:S(2)}, u32[]{:S(2)}) %all-to-all-start.1) | async-done | bytes 491552 | tf_op jit(solution)/shard_map/all_to_all | solution.py:514
  (114 shorter events, 19.5 us)
Async XLA Ops:
  2.2 6.0 %collective-permute-start = (bf16[128,256]{1,0:T(8,128)(2,1)S(1)}, bf16[128,256]{1,0:T(8,128)(2,1)S(1)}, u32[]{:S(2)}, u32[]{:S(2)}) collective-permute-start(bf16[128,256]{1,0:T(8,128)(2,1)S(1)} %get-tuple-element.80), channel_id=1, source_target_pairs={{0,32},{4,36},{8,40},{12,44},{16,48},{20,52},{24,56},{28,60},{32,6... | collective-permute-start | bytes 196616 | tf_op jit(solution)/shard_map/ppermute | solution.py:30
  3.9 6.1 %collective-permute-start.1 = (bf16[128,256]{1,0:T(8,128)(2,1)S(1)}, bf16[128,256]{1,0:T(8,128)(2,1)S(1)}, u32[]{:S(2)}, u32[]{:S(2)}) collective-permute-start(bf16[128,256]{1,0:T(8,128)(2,1)S(1)} %get-tuple-element.80), channel_id=1, source_target_pairs={{0,64},{4,68},{8,72},{12,76},{16,80},{20,84},{24,88},{28,92},{32,9... | collective-permute-start | bytes 196616 | tf_op jit(solution)/shard_map/ppermute | solution.py:30
  6.8 4.3 %collective-permute-start.2 = (bf16[128,256]{1,0:T(8,128)(2,1)S(1)}, bf16[128,256]{1,0:T(8,128)(2,1)S(1)}, u32[]{:S(2)}, u32[]{:S(2)}) collective-permute-start(bf16[128,256]{1,0:T(8,128)(2,1)S(1)} %get-tuple-element.80), channel_id=1, source_target_pairs={{0,96},{4,100},{8,104},{12,108},{16,112},{20,116},{24,120},{28,124... | collective-permute-start | bytes 196616 | tf_op jit(solution)/shard_map/ppermute | solution.py:30
  11.1 10.4 %collective-permute-start.3 = (bf16[512,256]{1,0:T(8,128)(2,1)S(1)}, bf16[512,256]{1,0:T(8,128)(2,1)S(1)}, u32[]{:S(2)}, u32[]{:S(2)}) collective-permute-start(bf16[512,256]{1,0:T(8,128)(2,1)S(1)} %pad_maximum_fusion.4), channel_id=1, source_target_pairs={{0,8},{4,12},{8,16},{12,20},{16,24},{20,28},{24,0},{28,4},{32,40},... | collective-permute-start | bytes 786440 | tf_op jit(solution)/shard_map/ppermute | solution.py:30
  13.1 13.8 %collective-permute-start.4 = (bf16[512,256]{1,0:T(8,128)(2,1)S(1)}, bf16[512,256]{1,0:T(8,128)(2,1)S(1)}, u32[]{:S(2)}, u32[]{:S(2)}) collective-permute-start(bf16[512,256]{1,0:T(8,128)(2,1)S(1)} %pad_maximum_fusion.4), channel_id=1, source_target_pairs={{0,16},{4,20},{8,24},{12,28},{16,0},{20,4},{24,8},{28,12},{32,48},... | collective-permute-start | bytes 786440 | tf_op jit(solution)/shard_map/ppermute | solution.py:30
  16.7 10.2 %collective-permute-start.5 = (bf16[512,256]{1,0:T(8,128)(2,1)S(1)}, bf16[512,256]{1,0:T(8,128)(2,1)S(1)}, u32[]{:S(2)}, u32[]{:S(2)}) collective-permute-start(bf16[512,256]{1,0:T(8,128)(2,1)S(1)} %pad_maximum_fusion.4), channel_id=1, source_target_pairs={{0,24},{4,28},{8,0},{12,4},{16,8},{20,12},{24,16},{28,20},{32,56},... | collective-permute-start | bytes 786440 | tf_op jit(solution)/shard_map/ppermute | solution.py:30
  27.0 2.7 %collective-permute-start.6 = (bf16[2048,256]{1,0:T(8,128)(2,1)S(1)}, bf16[2048,256]{1,0:T(8,128)(2,1)S(1)}, u32[]{:S(2)}, u32[]{:S(2)}) collective-permute-start(bf16[2048,256]{1,0:T(8,128)(2,1)S(1)} %constant_dynamic-update-slice_fusion.2.own_ref), channel_id=1, source_target_pairs={{0,4},{4,0},{8,12},{12,8},{16,20},{20,16},{24,28},{28,24},{32,36},... | collective-permute-start | bytes 3145736 | tf_op jit(solution)/shard_map/ppermute | solution.py:30
  36.3 8.6 %collective-permute-start.11 = (bf16[64,1536]{1,0:T(8,128)(2,1)}, bf16[64,1536]{1,0:T(8,128)(2,1)S(1)}, u32[]{:S(2)}, u32[]{:S(2)}) collective-permute-start(bf16[64,1536]{1,0:T(8,128)(2,1)} %get-tuple-element.41), channel_id=1, source_target_pairs={{0,1},{1,2},{2,3},{3,0},{4,5},{5,6},{6,7},{7,4},{8,9},{9,10},{10,1... | collective-permute-start | bytes 589832 | tf_op jit(solution)/shard_map/ppermute | solution.py:35
  37.9 22.5 %copy-start.1 = (f32[6144]{0:T(1024)S(1)}, f32[6144]{0:T(1024)}, u32[]{:S(2)}) copy-start(f32[6144]{0:T(1024)} %param.18) | copy-start | bytes 73732
  38.2 7.8 %collective-permute-start.8 = (bf16[64,1536]{1,0:T(8,128)(2,1)S(1)}, bf16[64,1536]{1,0:T(8,128)(2,1)S(1)}, u32[]{:S(2)}, u32[]{:S(2)}) collective-permute-start(bf16[64,1536]{1,0:T(8,128)(2,1)S(1)} %get-tuple-element.37), channel_id=1, source_target_pairs={{0,3},{1,0},{2,1},{3,2},{4,7},{5,4},{6,5},{7,6},{8,11},{9,8},{10,9... | collective-permute-start | bytes 589832 | tf_op jit(solution)/shard_map/ppermute | solution.py:35
  40.0 10.2 %collective-permute-start.10 = (bf16[64,1536]{1,0:T(8,128)(2,1)S(1)}, bf16[64,1536]{1,0:T(8,128)(2,1)S(1)}, u32[]{:S(2)}, u32[]{:S(2)}) collective-permute-start(bf16[64,1536]{1,0:T(8,128)(2,1)S(1)} %get-tuple-element.39), channel_id=1, source_target_pairs={{0,3},{1,0},{2,1},{3,2},{4,7},{5,4},{6,5},{7,6},{8,11},{9,8},{10,9... | collective-permute-start | bytes 589832 | tf_op jit(solution)/shard_map/ppermute | solution.py:35
  41.5 8.7 %collective-permute-start.7 = (bf16[64,1536]{1,0:T(8,128)(2,1)S(1)}, bf16[64,1536]{1,0:T(8,128)(2,1)S(1)}, u32[]{:S(2)}, u32[]{:S(2)}) collective-permute-start(bf16[64,1536]{1,0:T(8,128)(2,1)S(1)} %get-tuple-element.35), channel_id=1, source_target_pairs={{0,1},{1,2},{2,3},{3,0},{4,5},{5,6},{6,7},{7,4},{8,9},{9,10},{10,1... | collective-permute-start | bytes 589832 | tf_op jit(solution)/shard_map/ppermute | solution.py:35
  44.9 8.2 %collective-permute-start.12 = (bf16[64,1536]{1,0:T(8,128)(2,1)S(1)}, bf16[64,1536]{1,0:T(8,128)(2,1)S(1)}, u32[]{:S(2)}, u32[]{:S(2)}) collective-permute-start(bf16[64,1536]{1,0:T(8,128)(2,1)S(1)} %add_convert_fusion.11), channel_id=1, source_target_pairs={{0,1},{1,2},{2,3},{3,0},{4,5},{5,6},{6,7},{7,4},{8,9},{9,10},{10,1... | collective-permute-start | bytes 589832 | tf_op jit(solution)/shard_map/ppermute | solution.py:35
  46.0 7.3 %collective-permute-start.9 = (bf16[64,1536]{1,0:T(8,128)(2,1)S(1)}, bf16[64,1536]{1,0:T(8,128)(2,1)S(1)}, u32[]{:S(2)}, u32[]{:S(2)}) collective-permute-start(bf16[64,1536]{1,0:T(8,128)(2,1)S(1)} %add_convert_fusion.13), channel_id=1, source_target_pairs={{0,3},{1,0},{2,1},{3,2},{4,7},{5,4},{6,5},{7,6},{8,11},{9,8},{10,9... | collective-permute-start | bytes 589832 | tf_op jit(solution)/shard_map/ppermute | solution.py:35
  54.6 34.9 %copy-start = (bf16[128,1536]{1,0:T(8,128)(2,1)}, bf16[128,1536]{1,0:T(8,128)(2,1)S(1)}, u32[]{:S(2)}) copy-start(bf16[128,1536]{1,0:T(8,128)(2,1)S(1)} %pad_maximum_fusion.3) | copy-start | bytes 1179652
  55.7 12.3 %all-to-all-start = ((bf16[4,40,1536]{2,1,0:T(8,128)(2,1)}), bf16[4,40,1536]{2,1,0:T(8,128)(2,1)S(1)}, u32[]{:S(2)}, u32[]{:S(2)}) async-start(bf16[4,40,1536]{2,1,0:T(8,128)(2,1)} %bitcast.9), calls=%async_computation | async-start | bytes 983040 | tf_op jit(solution)/shard_map/all_to_all | solution.py:484
  59.9 86.4 %collective-permute-start.27 = (bf16[6144,256]{1,0:T(8,128)(2,1)}, bf16[6144,256]{1,0:T(8,128)(2,1)}, u32[]{:S(2)}, u32[]{:S(2)}) collective-permute-start(bf16[6144,256]{1,0:T(8,128)(2,1)} %bitcast.49), channel_id=1, source_target_pairs={{0,4},{4,0},{8,12},{12,8},{16,20},{20,16},{24,28},{28,24},{32,36},... | collective-permute-start | bytes 9437192 | tf_op jit(solution)/shard_map/ppermute | solution.py:30
  59.9 86.9 %collective-permute-start.28 = (bf16[6144,256]{1,0:T(8,128)(2,1)}, bf16[6144,256]{1,0:T(8,128)(2,1)}, u32[]{:S(2)}, u32[]{:S(2)}) collective-permute-start(bf16[6144,256]{1,0:T(8,128)(2,1)} %bitcast.51), channel_id=1, source_target_pairs={{0,4},{4,0},{8,12},{12,8},{16,20},{20,16},{24,28},{28,24},{32,36},... | collective-permute-start | bytes 9437192 | tf_op jit(solution)/shard_map/ppermute | solution.py:30
  60.4 93.4 %collective-permute-start.33 = (bf16[256,6144]{1,0:T(8,128)(2,1)}, bf16[256,6144]{1,0:T(8,128)(2,1)}, u32[]{:S(2)}, u32[]{:S(2)}) collective-permute-start(bf16[256,6144]{1,0:T(8,128)(2,1)} %bitcast.53), channel_id=1, source_target_pairs={{0,4},{4,0},{8,12},{12,8},{16,20},{20,16},{24,28},{28,24},{32,36},... | collective-permute-start | bytes 9437192 | tf_op jit(solution)/shard_map/ppermute | solution.py:30
  68.4 7.8 %collective-permute-start.23 = (bf16[40,3072]{1,0:T(8,128)(2,1)S(1)}, bf16[40,3072]{1,0:T(8,128)(2,1)S(1)}, u32[]{:S(2)}, u32[]{:S(2)}) collective-permute-start(bf16[40,3072]{1,0:T(8,128)(2,1)S(1)} %pad_maximum_fusion.6), channel_id=1, source_target_pairs={{0,16},{4,20},{8,24},{12,28},{16,0},{20,4},{24,8},{28,12},{32,48},... | collective-permute-start | bytes 737288 | tf_op jit(solution)/shard_map/ppermute | solution.py:30
  70.7 9.2 %collective-permute-start.24 = (bf16[40,3072]{1,0:T(8,128)(2,1)S(1)}, bf16[40,3072]{1,0:T(8,128)(2,1)S(1)}, u32[]{:S(2)}, u32[]{:S(2)}) collective-permute-start(bf16[40,3072]{1,0:T(8,128)(2,1)S(1)} %pad_maximum_fusion.6), channel_id=1, source_target_pairs={{0,24},{4,28},{8,0},{12,4},{16,8},{20,12},{24,16},{28,20},{32,56},... | collective-permute-start | bytes 737288 | tf_op jit(solution)/shard_map/ppermute | solution.py:30
  76.2 8.0 %collective-permute-start.20 = (bf16[40,3072]{1,0:T(8,128)(2,1)S(1)}, bf16[40,3072]{1,0:T(8,128)(2,1)S(1)}, u32[]{:S(2)}, u32[]{:S(2)}) collective-permute-start(bf16[40,3072]{1,0:T(8,128)(2,1)S(1)} %pad_maximum_fusion.6), channel_id=1, source_target_pairs={{0,8},{4,12},{8,16},{12,20},{16,24},{20,28},{24,0},{28,4},{32,40},... | collective-permute-start | bytes 737288 | tf_op jit(solution)/shard_map/ppermute | solution.py:30
  79.9 7.7 %collective-permute-start.16 = (bf16[40,3072]{1,0:T(8,128)(2,1)S(1)}, bf16[40,3072]{1,0:T(8,128)(2,1)S(1)}, u32[]{:S(2)}, u32[]{:S(2)}) collective-permute-start(bf16[40,3072]{1,0:T(8,128)(2,1)S(1)} %pad_maximum_fusion.5), channel_id=1, source_target_pairs={{0,64},{4,68},{8,72},{12,76},{16,80},{20,84},{24,88},{28,92},{32,9... | collective-permute-start | bytes 737288 | tf_op jit(solution)/shard_map/ppermute | solution.py:30
  84.2 8.3 %collective-permute-start.17 = (bf16[40,3072]{1,0:T(8,128)(2,1)S(1)}, bf16[40,3072]{1,0:T(8,128)(2,1)S(1)}, u32[]{:S(2)}, u32[]{:S(2)}) collective-permute-start(bf16[40,3072]{1,0:T(8,128)(2,1)S(1)} %pad_maximum_fusion.5), channel_id=1, source_target_pairs={{0,96},{4,100},{8,104},{12,108},{16,112},{20,116},{24,120},{28,124... | collective-permute-start | bytes 737288 | tf_op jit(solution)/shard_map/ppermute | solution.py:30
  87.7 9.7 %collective-permute-start.13 = (bf16[40,3072]{1,0:T(8,128)(2,1)S(1)}, bf16[40,3072]{1,0:T(8,128)(2,1)S(1)}, u32[]{:S(2)}, u32[]{:S(2)}) collective-permute-start(bf16[40,3072]{1,0:T(8,128)(2,1)S(1)} %pad_maximum_fusion.5), channel_id=1, source_target_pairs={{0,32},{4,36},{8,40},{12,44},{16,48},{20,52},{24,56},{28,60},{32,6... | collective-permute-start | bytes 737288 | tf_op jit(solution)/shard_map/ppermute | solution.py:30
  92.5 9.5 %collective-permute-start.25 = (bf16[80,3072]{1,0:T(8,128)(2,1)S(1)}, bf16[80,3072]{1,0:T(8,128)(2,1)S(1)}, u32[]{:S(2)}, u32[]{:S(2)}) collective-permute-start(bf16[80,3072]{1,0:T(8,128)(2,1)S(1)} %constant_dynamic-update-slice_fusion.12.refs_3_), channel_id=1, source_target_pairs={{0,96},{4,100},{8,104},{12,108},{16,112},{20,116},{24,120},{28,124... | collective-permute-start | bytes 1474568 | tf_op jit(solution)/shard_map/ppermute | solution.py:30
  97.3 14.6 %collective-permute-start.31 = (bf16[80,3072]{1,0:T(8,128)(2,1)S(1)}, bf16[80,3072]{1,0:T(8,128)(2,1)S(1)}, u32[]{:S(2)}, u32[]{:S(2)}) collective-permute-start(bf16[80,3072]{1,0:T(8,128)(2,1)S(1)} %constant_dynamic-update-slice_fusion.12.refs_3_), channel_id=1, source_target_pairs={{0,32},{4,36},{8,40},{12,44},{16,48},{20,52},{24,56},{28,60},{32,6... | collective-permute-start | bytes 1474568 | tf_op jit(solution)/shard_map/ppermute | solution.py:30
  102.0 15.2 %collective-permute-start.21 = (bf16[80,3072]{1,0:T(8,128)(2,1)S(1)}, bf16[80,3072]{1,0:T(8,128)(2,1)S(1)}, u32[]{:S(2)}, u32[]{:S(2)}) collective-permute-start(bf16[80,3072]{1,0:T(8,128)(2,1)S(1)} %pad_maximum_fusion.1.refs_2_), channel_id=1, source_target_pairs={{0,32},{4,36},{8,40},{12,44},{16,48},{20,52},{24,56},{28,60},{32,6... | collective-permute-start | bytes 1474568 | tf_op jit(solution)/shard_map/ppermute | solution.py:30
  111.9 9.3 %collective-permute-start.32 = (bf16[80,3072]{1,0:T(8,128)(2,1)S(1)}, bf16[80,3072]{1,0:T(8,128)(2,1)S(1)}, u32[]{:S(2)}, u32[]{:S(2)}) collective-permute-start(bf16[80,3072]{1,0:T(8,128)(2,1)S(1)} %pad_maximum_fusion.1.refs_2_), channel_id=1, source_target_pairs={{0,96},{4,100},{8,104},{12,108},{16,112},{20,116},{24,120},{28,124... | collective-permute-start | bytes 1474568 | tf_op jit(solution)/shard_map/ppermute | solution.py:30
  117.2 13.8 %collective-permute-start.18 = (bf16[80,3072]{1,0:T(8,128)(2,1)S(1)}, bf16[80,3072]{1,0:T(8,128)(2,1)S(1)}, u32[]{:S(2)}, u32[]{:S(2)}) collective-permute-start(bf16[80,3072]{1,0:T(8,128)(2,1)S(1)} %constant_dynamic-update-slice_fusion.10.refs_1_), channel_id=1, source_target_pairs={{0,24},{4,28},{8,0},{12,4},{16,8},{20,12},{24,16},{28,20},{32,56},... | collective-permute-start | bytes 1474568 | tf_op jit(solution)/shard_map/ppermute | solution.py:30
  121.2 13.7 %collective-permute-start.29 = (bf16[80,3072]{1,0:T(8,128)(2,1)S(1)}, bf16[80,3072]{1,0:T(8,128)(2,1)S(1)}, u32[]{:S(2)}, u32[]{:S(2)}) collective-permute-start(bf16[80,3072]{1,0:T(8,128)(2,1)S(1)} %constant_dynamic-update-slice_fusion.10.refs_1_), channel_id=1, source_target_pairs={{0,8},{4,12},{8,16},{12,20},{16,24},{20,28},{24,0},{28,4},{32,40},... | collective-permute-start | bytes 1474568 | tf_op jit(solution)/shard_map/ppermute | solution.py:30
  130.9 13.3 %collective-permute-start.14 = (bf16[80,3072]{1,0:T(8,128)(2,1)S(1)}, bf16[80,3072]{1,0:T(8,128)(2,1)S(1)}, u32[]{:S(2)}, u32[]{:S(2)}) collective-permute-start(bf16[80,3072]{1,0:T(8,128)(2,1)S(1)} %pad_maximum_fusion.refs_0_), channel_id=1, source_target_pairs={{0,8},{4,12},{8,16},{12,20},{16,24},{20,28},{24,0},{28,4},{32,40},... | collective-permute-start | bytes 1474568 | tf_op jit(solution)/shard_map/ppermute | solution.py:30
  134.9 11.3 %collective-permute-start.30 = (bf16[80,3072]{1,0:T(8,128)(2,1)S(1)}, bf16[80,3072]{1,0:T(8,128)(2,1)S(1)}, u32[]{:S(2)}, u32[]{:S(2)}) collective-permute-start(bf16[80,3072]{1,0:T(8,128)(2,1)S(1)} %pad_maximum_fusion.refs_0_), channel_id=1, source_target_pairs={{0,24},{4,28},{8,0},{12,4},{16,8},{20,12},{24,16},{28,20},{32,56},... | collective-permute-start | bytes 1474568 | tf_op jit(solution)/shard_map/ppermute | solution.py:30
  144.2 14.8 %collective-permute-start.26 = (bf16[80,3072]{1,0:T(8,128)(2,1)S(1)}, bf16[80,3072]{1,0:T(8,128)(2,1)S(1)}, u32[]{:S(2)}, u32[]{:S(2)}) collective-permute-start(bf16[80,3072]{1,0:T(8,128)(2,1)S(1)} %collective-permute-done.25.refs_7_), channel_id=1, source_target_pairs={{0,96},{4,100},{8,104},{12,108},{16,112},{20,116},{24,120},{28,124... | collective-permute-start | bytes 1474568 | tf_op jit(solution)/shard_map/ppermute | solution.py:30
  146.3 12.8 %collective-permute-start.22 = (bf16[80,3072]{1,0:T(8,128)(2,1)S(1)}, bf16[80,3072]{1,0:T(8,128)(2,1)S(1)}, u32[]{:S(2)}, u32[]{:S(2)}) collective-permute-start(bf16[80,3072]{1,0:T(8,128)(2,1)S(1)} %collective-permute-done.21.refs_4_), channel_id=1, source_target_pairs={{0,32},{4,36},{8,40},{12,44},{16,48},{20,52},{24,56},{28,60},{32,6... | collective-permute-start | bytes 1474568 | tf_op jit(solution)/shard_map/ppermute | solution.py:30
  146.3 12.8 %collective-permute-start.19 = (bf16[80,3072]{1,0:T(8,128)(2,1)S(1)}, bf16[80,3072]{1,0:T(8,128)(2,1)S(1)}, u32[]{:S(2)}, u32[]{:S(2)}) collective-permute-start(bf16[80,3072]{1,0:T(8,128)(2,1)S(1)} %collective-permute-done.18.refs_3_), channel_id=1, source_target_pairs={{0,24},{4,28},{8,0},{12,4},{16,8},{20,12},{24,16},{28,20},{32,56},... | collective-permute-start | bytes 1474568 | tf_op jit(solution)/shard_map/ppermute | solution.py:30
  146.8 12.3 %collective-permute-start.15 = (bf16[80,3072]{1,0:T(8,128)(2,1)S(1)}, bf16[80,3072]{1,0:T(8,128)(2,1)S(1)}, u32[]{:S(2)}, u32[]{:S(2)}) collective-permute-start(bf16[80,3072]{1,0:T(8,128)(2,1)S(1)} %collective-permute-done.14.refs_0_), channel_id=1, source_target_pairs={{0,8},{4,12},{8,16},{12,20},{16,24},{20,28},{24,0},{28,4},{32,40},... | collective-permute-start | bytes 1474568 | tf_op jit(solution)/shard_map/ppermute | solution.py:30
  165.4 14.1 %collective-permute-start.35 = (bf16[80,3072]{1,0:T(8,128)(2,1)S(1)}, bf16[80,3072]{1,0:T(8,128)(2,1)S(1)}, u32[]{:S(2)}, u32[]{:S(2)}) collective-permute-start(bf16[80,3072]{1,0:T(8,128)(2,1)S(1)} %get-tuple-element.53), channel_id=1, source_target_pairs={{0,24},{4,28},{8,0},{12,4},{16,8},{20,12},{24,16},{28,20},{32,56},... | collective-permute-start | bytes 1474568 | tf_op jit(solution)/shard_map/ppermute | solution.py:30
  172.7 32.8 %collective-permute-start.34 = (bf16[80,3072]{1,0:T(8,128)(2,1)S(1)}, bf16[80,3072]{1,0:T(8,128)(2,1)S(1)}, u32[]{:S(2)}, u32[]{:S(2)}) collective-permute-start(bf16[80,3072]{1,0:T(8,128)(2,1)S(1)} %get-tuple-element.51), channel_id=1, source_target_pairs={{0,8},{4,12},{8,16},{12,20},{16,24},{20,28},{24,0},{28,4},{32,40},... | collective-permute-start | bytes 1474568 | tf_op jit(solution)/shard_map/ppermute | solution.py:30
  173.1 21.6 %collective-permute-start.39 = (bf16[80,3072]{1,0:T(8,128)(2,1)S(1)}, bf16[80,3072]{1,0:T(8,128)(2,1)S(1)}, u32[]{:S(2)}, u32[]{:S(2)}) collective-permute-start(bf16[80,3072]{1,0:T(8,128)(2,1)S(1)} %get-tuple-element.57), channel_id=1, source_target_pairs={{0,8},{4,12},{8,16},{12,20},{16,24},{20,28},{24,0},{28,4},{32,40},... | collective-permute-start | bytes 1474568 | tf_op jit(solution)/shard_map/ppermute | solution.py:30
  173.3 42.4 %collective-permute-start.38 = (bf16[80,3072]{1,0:T(8,128)(2,1)S(1)}, bf16[80,3072]{1,0:T(8,128)(2,1)S(1)}, u32[]{:S(2)}, u32[]{:S(2)}) collective-permute-start(bf16[80,3072]{1,0:T(8,128)(2,1)S(1)} %get-tuple-element.55), channel_id=1, source_target_pairs={{0,24},{4,28},{8,0},{12,4},{16,8},{20,12},{24,16},{28,20},{32,56},... | collective-permute-start | bytes 1474568 | tf_op jit(solution)/shard_map/ppermute | solution.py:30
  176.3 18.5 %collective-permute-start.44 = (bf16[80,3072]{1,0:T(8,128)(2,1)S(1)}, bf16[80,3072]{1,0:T(8,128)(2,1)S(1)}, u32[]{:S(2)}, u32[]{:S(2)}) collective-permute-start(bf16[80,3072]{1,0:T(8,128)(2,1)S(1)} %get-tuple-element.61), channel_id=1, source_target_pairs={{0,96},{4,100},{8,104},{12,108},{16,112},{20,116},{24,120},{28,124... | collective-permute-start | bytes 1474568 | tf_op jit(solution)/shard_map/ppermute | solution.py:30
  179.5 39.7 %collective-permute-start.43 = (bf16[80,3072]{1,0:T(8,128)(2,1)S(1)}, bf16[80,3072]{1,0:T(8,128)(2,1)S(1)}, u32[]{:S(2)}, u32[]{:S(2)}) collective-permute-start(bf16[80,3072]{1,0:T(8,128)(2,1)S(1)} %get-tuple-element.59), channel_id=1, source_target_pairs={{0,32},{4,36},{8,40},{12,44},{16,48},{20,52},{24,56},{28,60},{32,6... | collective-permute-start | bytes 1474568 | tf_op jit(solution)/shard_map/ppermute | solution.py:30
  194.7 10.6 %collective-permute-start.48 = (bf16[80,3072]{1,0:T(8,128)(2,1)S(1)}, bf16[80,3072]{1,0:T(8,128)(2,1)S(1)}, u32[]{:S(2)}, u32[]{:S(2)}) collective-permute-start(bf16[80,3072]{1,0:T(8,128)(2,1)S(1)} %get-tuple-element.65), channel_id=1, source_target_pairs={{0,32},{4,36},{8,40},{12,44},{16,48},{20,52},{24,56},{28,60},{32,6... | collective-permute-start | bytes 1474568 | tf_op jit(solution)/shard_map/ppermute | solution.py:30
  194.9 32.1 %collective-permute-start.47 = (bf16[80,3072]{1,0:T(8,128)(2,1)S(1)}, bf16[80,3072]{1,0:T(8,128)(2,1)S(1)}, u32[]{:S(2)}, u32[]{:S(2)}) collective-permute-start(bf16[80,3072]{1,0:T(8,128)(2,1)S(1)} %get-tuple-element.63), channel_id=1, source_target_pairs={{0,96},{4,100},{8,104},{12,108},{16,112},{20,116},{24,120},{28,124... | collective-permute-start | bytes 1474568 | tf_op jit(solution)/shard_map/ppermute | solution.py:30
  205.3 8.8 %collective-permute-start.36 = (bf16[80,3072]{1,0:T(8,128)(2,1)S(1)}, bf16[80,3072]{1,0:T(8,128)(2,1)S(1)}, u32[]{:S(2)}, u32[]{:S(2)}) collective-permute-start(bf16[80,3072]{1,0:T(8,128)(2,1)S(1)} %add_convert_fusion.7), channel_id=1, source_target_pairs={{0,24},{4,28},{8,0},{12,4},{16,8},{20,12},{24,16},{28,20},{32,56},... | collective-permute-start | bytes 1474568 | tf_op jit(solution)/shard_map/ppermute | solution.py:30
  205.4 11.0 %collective-permute-start.40 = (bf16[80,3072]{1,0:T(8,128)(2,1)S(1)}, bf16[80,3072]{1,0:T(8,128)(2,1)S(1)}, u32[]{:S(2)}, u32[]{:S(2)}) collective-permute-start(bf16[80,3072]{1,0:T(8,128)(2,1)S(1)} %add_convert_fusion.5), channel_id=1, source_target_pairs={{0,8},{4,12},{8,16},{12,20},{16,24},{20,28},{24,0},{28,4},{32,40},... | collective-permute-start | bytes 1474568 | tf_op jit(solution)/shard_map/ppermute | solution.py:30
  214.1 12.6 %collective-permute-start.45 = (bf16[80,3072]{1,0:T(8,128)(2,1)S(1)}, bf16[80,3072]{1,0:T(8,128)(2,1)S(1)}, u32[]{:S(2)}, u32[]{:S(2)}) collective-permute-start(bf16[80,3072]{1,0:T(8,128)(2,1)S(1)} %add_convert_fusion.3), channel_id=1, source_target_pairs={{0,96},{4,100},{8,104},{12,108},{16,112},{20,116},{24,120},{28,124... | collective-permute-start | bytes 1474568 | tf_op jit(solution)/shard_map/ppermute | solution.py:30
  215.7 16.0 %collective-permute-start.49 = (bf16[80,3072]{1,0:T(8,128)(2,1)S(1)}, bf16[80,3072]{1,0:T(8,128)(2,1)S(1)}, u32[]{:S(2)}, u32[]{:S(2)}) collective-permute-start(bf16[80,3072]{1,0:T(8,128)(2,1)S(1)} %add_convert_fusion.1), channel_id=1, source_target_pairs={{0,32},{4,36},{8,40},{12,44},{16,48},{20,52},{24,56},{28,60},{32,6... | collective-permute-start | bytes 1474568 | tf_op jit(solution)/shard_map/ppermute | solution.py:30
  216.5 15.8 %collective-permute-start.37 = (bf16[40,3072]{1,0:T(8,128)(2,1)S(1)}, bf16[40,3072]{1,0:T(8,128)(2,1)S(1)}, u32[]{:S(2)}, u32[]{:S(2)}) collective-permute-start(bf16[40,3072]{1,0:T(8,128)(2,1)S(1)} %slice.99), channel_id=1, source_target_pairs={{0,96},{4,100},{8,104},{12,108},{16,112},{20,116},{24,120},{28,124... | collective-permute-start | bytes 737288 | tf_op jit(solution)/shard_map/ppermute | solution.py:30
  219.2 15.1 %collective-permute-start.41 = (bf16[40,3072]{1,0:T(8,128)(2,1)S(1)}, bf16[40,3072]{1,0:T(8,128)(2,1)S(1)}, u32[]{:S(2)}, u32[]{:S(2)}) collective-permute-start(bf16[40,3072]{1,0:T(8,128)(2,1)S(1)} %get-tuple-element.68), channel_id=1, source_target_pairs={{0,64},{4,68},{8,72},{12,76},{16,80},{20,84},{24,88},{28,92},{32,9... | collective-permute-start | bytes 737288 | tf_op jit(solution)/shard_map/ppermute | solution.py:30
  226.8 7.6 %collective-permute-start.42 = (bf16[40,3072]{1,0:T(8,128)(2,1)S(1)}, bf16[40,3072]{1,0:T(8,128)(2,1)S(1)}, u32[]{:S(2)}, u32[]{:S(2)}) collective-permute-start(bf16[40,3072]{1,0:T(8,128)(2,1)S(1)} %get-tuple-element.69), channel_id=1, source_target_pairs={{0,32},{4,36},{8,40},{12,44},{16,48},{20,52},{24,56},{28,60},{32,6... | collective-permute-start | bytes 737288 | tf_op jit(solution)/shard_map/ppermute | solution.py:30
  227.0 7.5 %collective-permute-start.46 = (bf16[40,3072]{1,0:T(8,128)(2,1)S(1)}, bf16[40,3072]{1,0:T(8,128)(2,1)S(1)}, u32[]{:S(2)}, u32[]{:S(2)}) collective-permute-start(bf16[40,3072]{1,0:T(8,128)(2,1)S(1)} %slice.105), channel_id=1, source_target_pairs={{0,24},{4,28},{8,0},{12,4},{16,8},{20,12},{24,16},{28,20},{32,56},... | collective-permute-start | bytes 737288 | tf_op jit(solution)/shard_map/ppermute | solution.py:30
  231.8 15.0 %copy-start.2 = (f32[128,2]{0,1:T(2,128)S(1)}, f32[128,2]{0,1:T(2,128)}, u32[]{:S(2)}) copy-start(f32[128,2]{0,1:T(2,128)} %param.22) | copy-start | bytes 3076
  231.9 7.9 %collective-permute-start.50 = (bf16[40,3072]{1,0:T(8,128)(2,1)S(1)}, bf16[40,3072]{1,0:T(8,128)(2,1)S(1)}, u32[]{:S(2)}, u32[]{:S(2)}) collective-permute-start(bf16[40,3072]{1,0:T(8,128)(2,1)S(1)} %get-tuple-element.70), channel_id=1, source_target_pairs={{0,16},{4,20},{8,24},{12,28},{16,0},{20,4},{24,8},{28,12},{32,48},... | collective-permute-start | bytes 737288 | tf_op jit(solution)/shard_map/ppermute | solution.py:30
  232.3 10.0 %collective-permute-start.51 = (bf16[40,3072]{1,0:T(8,128)(2,1)S(1)}, bf16[40,3072]{1,0:T(8,128)(2,1)S(1)}, u32[]{:S(2)}, u32[]{:S(2)}) collective-permute-start(bf16[40,3072]{1,0:T(8,128)(2,1)S(1)} %get-tuple-element.71), channel_id=1, source_target_pairs={{0,8},{4,12},{8,16},{12,20},{16,24},{20,28},{24,0},{28,4},{32,40},... | collective-permute-start | bytes 737288 | tf_op jit(solution)/shard_map/ppermute | solution.py:30
  243.3 11.3 %all-to-all-start.1 = ((bf16[4,40,1536]{2,1,0:T(8,128)(2,1)}), bf16[4,40,1536]{2,1,0:T(8,128)(2,1)S(1)}, u32[]{:S(2)}, u32[]{:S(2)}) async-start(bf16[4,40,1536]{2,1,0:T(8,128)(2,1)} %pad_maximum_fusion.2), calls=%async_computation.1 | async-start | bytes 983040 | tf_op jit(solution)/shard_map/all_to_all | solution.py:514

commit v3 on v2

--- a/solution.py
+++ b/solution.py
@@ -278,17 +278,21 @@
     tiles(half, body)
 
 
+def late_kernel(near, far, weight_ref, late_ref):
+    lift_groups([(0, 0, near, far)], weight_ref, late_ref)
+
+
 def last_kernel(
-    a_near, a_far, b_near, b_far, weight_ref, own_ref, sums_ref, down_ref, early_a, early_b,
+    late_a, b_near, b_far, weight_ref, own_ref, sums_ref, down_ref, early_a, early_b,
     hidden_a, hidden_b, a_out_near, a_out_far, b_out_near, b_out_far, late_ref,
 ):
-    lift_groups([(0, 0, a_near, a_far), (1, 0, b_near, b_far)], weight_ref, late_ref)
-    combine(late_ref, 0, late_ref, 0, LAST, LAST, hidden_a, hidden_b)
-    combine(late_ref, 0, own_ref, 0, LAST, 0, hidden_a, hidden_b)
+    lift_groups([(1, 0, b_near, b_far)], weight_ref, late_ref)
+    combine(late_a, 0, late_ref, 0, LAST, LAST, hidden_a, hidden_b)
+    combine(late_a, 0, own_ref, 0, LAST, 0, hidden_a, hidden_b)
     combine(own_ref, 0, late_ref, 0, 0, LAST, hidden_a, hidden_b)
 
     def crossing(k, d):
-        combine(late_ref, 0, sums_ref, k, LAST, d, hidden_a, hidden_b)
+        combine(late_a, 0, sums_ref, k, LAST, d, hidden_a, hidden_b)
         combine(sums_ref, k, late_ref, 0, d, LAST, hidden_a, hidden_b)
 
     each_side(crossing)
@@ -359,7 +363,10 @@
         [pltpu.SemaphoreType.DMA((len(downs),))],
         hbm=(10, 11),
     )
-    operands = [*a_groups[LAST], *b_groups[LAST], weight, own_sums, sums, down, early_a, early_b]
+    (late_a,) = in_vmem(
+        late_kernel, [jax.ShapeDtypeStruct((1, rows, both), jnp.float32)], [*a_groups[LAST], weight]
+    )
+    operands = [late_a, *b_groups[LAST], weight, own_sums, sums, down, early_a, early_b]
     hidden_a, hidden_b, *first = in_vmem(
         last_kernel,
         [hidden, hidden] + [part] * 4,

time: 256 us -> 257 us (level)
    pallas_call x4 -> x5, Pallas kernels: 22.5 us -> 23.2 us  [in_vmem(): pl.pallas_call(kernel, out_shape=out_shapes, in_specs=[far if i in hbm el...]
  transfers between devices with their start and end apart: 54 -> 54, of which waited for: 30 -> 30; matrix products, arithmetic and copies ran while one was open for 2% -> 2% of each run, Pallas kernels for 6% -> 7%
where the time goes in v3:
time: 257 us; the launch traced here: 256 us
  waiting for transfers between devices  134 us (52%)
  starting transfers between devices  80.5 us (31%)
  Pallas kernels  29.8 us (12%)
  other arithmetic  5.53 us (2%)
  local copies, waits for them, and re-layouts  2.96 us (1%)
    ppermute x46, waiting for transfers between devices, shifted(): return lax.ppermute(array, 'cp', pairs)  112 us
    ppermute x46, starting transfers between devices, shifted(): return lax.ppermute(array, 'cp', pairs)  63.3 us
    pallas_call x5, Pallas kernels, in_vmem(): pl.pallas_call(kernel, out_shape=out_shapes, in_specs=[far if i in hbm el...  23.2 us
    ppermute x6, starting transfers between devices, along(): lax.ppermute(array, 'ep', [(i, (i + step) % SIDE) for i in range(SIDE)])  9.47 us
    all_to_all x1, waiting for transfers between devices, local(): back = lax.all_to_all(back, 'ep', split_axis=0, concat_axis=0, tiled=True)  7.64 us
    all_to_all x1, waiting for transfers between devices, local(): lax.all_to_all(rows.reshape(SIDE, CAP, quarter), 'ep', split_axis=0, conc...  7.52 us
    ppermute x6, waiting for transfers between devices, along(): lax.ppermute(array, 'ep', [(i, (i + step) % SIDE) for i in range(SIDE)])  6.65 us
    pallas_call x1, Pallas kernels, attend_and_project(): pl.pallas_call(attention_kernel, out_shape=[jax.ShapeDtypeStruct((tokens...  6.59 us
  transfers between devices with their start and end apart: 54, of which 30 were waited for; matrix products, arithmetic and copies ran while one was open for 2% of the time, Pallas kernels for 7%

profile of v3, /device:TPU:0, one launch (start us, length us, event | category | flops | bytes accessed | tf_op | source)
XLA Modules:
  0.0 256.3 jit_solution(13618043610205085267)
XLA Ops:
  2.2 1.8 collective-permute-start
  3.9 2.9 %collective-permute-start.1 = (bf16[128,256]{1,0:T(8,128)(2,1)S(1)}, bf16[128,256]{1,0:T(8,128)(2,1)S(1)}, u32[]{:S(2)}, u32[]{:S(2)}) collective-permute-start(bf16[128,256]{1,0:T(8,128)(2,1)S(1)} %get-tuple-element.80), channel_id=1, source_target_pairs={{0,64},{4,68},{8,72},{12,76},{16,80},{20,84},{24,88},{28,92},{32,9... | collective-permute-start | bytes 196616 | tf_op jit(solution)/shard_map/ppermute | solution.py:30
  6.8 1.3 collective-permute-start.2
  8.2 1.9 collective-permute-done.1
  11.1 2.0 collective-permute-start.3
  13.1 3.6 %collective-permute-start.4 = (bf16[512,256]{1,0:T(8,128)(2,1)S(1)}, bf16[512,256]{1,0:T(8,128)(2,1)S(1)}, u32[]{:S(2)}, u32[]{:S(2)}) collective-permute-start(bf16[512,256]{1,0:T(8,128)(2,1)S(1)} %pad_maximum_fusion.4), channel_id=1, source_target_pairs={{0,16},{4,20},{8,24},{12,28},{16,0},{20,4},{24,8},{28,12},{32,48},... | collective-permute-start | bytes 786440 | tf_op jit(solution)/shard_map/ppermute | solution.py:30
  17.7 3.8 %collective-permute-done.3 = bf16[512,256]{1,0:T(8,128)(2,1)S(1)} collective-permute-done((bf16[512,256]{1,0:T(8,128)(2,1)S(1)}, bf16[512,256]{1,0:T(8,128)(2,1)S(1)}, u32[]{:S(2)}, u32[]{:S(2)}) %collective-permute-start.3) | collective-permute-done | bytes 262176 | tf_op jit(solution)/shard_map/ppermute | solution.py:30
  21.5 5.4 %collective-permute-done.4 = bf16[512,256]{1,0:T(8,128)(2,1)S(1)} collective-permute-done((bf16[512,256]{1,0:T(8,128)(2,1)S(1)}, bf16[512,256]{1,0:T(8,128)(2,1)S(1)}, u32[]{:S(2)}, u32[]{:S(2)}) %collective-permute-start.4) | collective-permute-done | bytes 262176 | tf_op jit(solution)/shard_map/ppermute | solution.py:30
  28.6 1.1 collective-permute-done.6.other_ref
  29.7 6.6 %attention.1 = (bf16[64,1536]{1,0:T(8,128)(2,1)S(1)}, bf16[64,1536]{1,0:T(8,128)(2,1)S(1)}, bf16[64,1536]{1,0:T(8,128)(2,1)S(1)}, bf16[64,1536]{1,0:T(8,128)(2,1...) custom-call(s32[34]{0:T(128)S(1)} %pad_add_fusion.place_ref, ...), custom_call_target="tpu_custom_call" | custom-call | tf_op jit(solution)/shard_map/attention/pallas_call | solution.py:143
  36.3 1.6 collective-permute-start.11
  38.2 1.8 collective-permute-start.8
  40.0 1.5 collective-permute-start.10
  42.0 2.9 %collective-permute-done.11 = bf16[64,1536]{1,0:T(8,128)(2,1)S(1)} collective-permute-done((bf16[64,1536]{1,0:T(8,128)(2,1)}, bf16[64,1536]{1,0:T(8,128)(2,1)S(1)}, u32[]{:S(2)}, u32[]{:S(2)}) %collective-permute-start.11) | collective-permute-done | bytes 196640 | tf_op jit(solution)/shard_map/ppermute | solution.py:35
  46.0 3.0 %collective-permute-start.9 = (bf16[64,1536]{1,0:T(8,128)(2,1)S(1)}, bf16[64,1536]{1,0:T(8,128)(2,1)S(1)}, u32[]{:S(2)}, u32[]{:S(2)}) collective-permute-start(bf16[64,1536]{1,0:T(8,128)(2,1)S(1)} %add_convert_fusion.13), channel_id=1, source_target_pairs={{0,3},{1,0},{2,1},{3,2},{4,7},{5,4},{6,5},{7,6},{8,11},{9,8},{10,9... | collective-permute-start | bytes 589832 | tf_op jit(solution)/shard_map/ppermute | solution.py:35
  50.2 3.0 %collective-permute-done.12 = bf16[64,1536]{1,0:T(8,128)(2,1)S(1)} collective-permute-done((bf16[64,1536]{1,0:T(8,128)(2,1)S(1)}, bf16[64,1536]{1,0:T(8,128)(2,1)S(1)}, u32[]{:S(2)}, u32[]{:S(2)}) %collective-permute-start.12) | collective-permute-done | bytes 196640 | tf_op jit(solution)/shard_map/ppermute | solution.py:35
  53.3 1.2 add_convert_fusion.12
  55.7 4.2 %all-to-all-start = ((bf16[4,40,1536]{2,1,0:T(8,128)(2,1)}), bf16[4,40,1536]{2,1,0:T(8,128)(2,1)S(1)}, u32[]{:S(2)}, u32[]{:S(2)}) async-start(bf16[4,40,1536]{2,1,0:T(8,128)(2,1)} %bitcast.9), calls=%async_computation | async-start | bytes 983040 | tf_op jit(solution)/shard_map/all_to_all | solution.py:491
  60.4 7.5 %all-to-all-done = bf16[4,40,1536]{2,1,0:T(8,128)(2,1)S(1)} async-done(((bf16[4,40,1536]{2,1,0:T(8,128)(2,1)}), bf16[4,40,1536]{2,1,0:T(8,128)(2,1)S(1)}, u32[]{:S(2)}, u32[]{:S(2)}) %all-to-all-start) | async-done | bytes 491552 | tf_op jit(solution)/shard_map/all_to_all | solution.py:491
  68.4 2.3 collective-permute-start.21
  70.7 1.7 collective-permute-start.22
  72.4 3.8 %collective-permute-done.21 = bf16[40,3072]{1,0:T(8,128)(2,1)S(1)} collective-permute-done((bf16[40,3072]{1,0:T(8,128)(2,1)S(1)}, bf16[40,3072]{1,0:T(8,128)(2,1)S(1)}, u32[]{:S(2)}, u32[]{:S(2)}) %collective-permute-start.21) | collective-permute-done | bytes 245792 | tf_op jit(solution)/shard_map/ppermute | solution.py:30
  76.2 3.0 %collective-permute-start.20 = (bf16[40,3072]{1,0:T(8,128)(2,1)S(1)}, bf16[40,3072]{1,0:T(8,128)(2,1)S(1)}, u32[]{:S(2)}, u32[]{:S(2)}) collective-permute-start(bf16[40,3072]{1,0:T(8,128)(2,1)S(1)} %pad_maximum_fusion.6), channel_id=1, source_target_pairs={{0,8},{4,12},{8,16},{12,20},{16,24},{20,28},{24,0},{28,4},{32,40},... | collective-permute-start | bytes 737288 | tf_op jit(solution)/shard_map/ppermute | solution.py:30
  79.9 1.5 collective-permute-start.16
  81.4 2.7 %collective-permute-done.20 = bf16[40,3072]{1,0:T(8,128)(2,1)S(1)} collective-permute-done((bf16[40,3072]{1,0:T(8,128)(2,1)S(1)}, bf16[40,3072]{1,0:T(8,128)(2,1)S(1)}, u32[]{:S(2)}, u32[]{:S(2)}) %collective-permute-start.20) | collective-permute-done | bytes 245792 | tf_op jit(solution)/shard_map/ppermute | solution.py:30
  84.2 2.4 collective-permute-start.17
  87.7 1.8 collective-permute-start.13
  89.5 3.0 %collective-permute-done.17 = bf16[40,3072]{1,0:T(8,128)(2,1)S(1)} collective-permute-done((bf16[40,3072]{1,0:T(8,128)(2,1)S(1)}, bf16[40,3072]{1,0:T(8,128)(2,1)S(1)}, u32[]{:S(2)}, u32[]{:S(2)}) %collective-permute-start.17) | collective-permute-done | bytes 245792 | tf_op jit(solution)/shard_map/ppermute | solution.py:30
  92.5 1.7 collective-permute-start.27
  94.1 3.2 %collective-permute-done.13 = bf16[40,3072]{1,0:T(8,128)(2,1)S(1)} collective-permute-done((bf16[40,3072]{1,0:T(8,128)(2,1)S(1)}, bf16[40,3072]{1,0:T(8,128)(2,1)S(1)}, u32[]{:S(2)}, u32[]{:S(2)}) %collective-permute-start.13) | collective-permute-done | bytes 245792 | tf_op jit(solution)/shard_map/ppermute | solution.py:30
  98.2 3.8 %collective-permute-done.27.refs_7_ = bf16[80,3072]{1,0:T(8,128)(2,1)S(1)} collective-permute-done((bf16[80,3072]{1,0:T(8,128)(2,1)S(1)}, bf16[80,3072]{1,0:T(8,128)(2,1)S(1)}, u32[]{:S(2)}, u32[]{:S(2)}) %collective-permute-start.27) | collective-permute-done | bytes 491552 | tf_op jit(solution)/shard_map/ppermute | solution.py:30
  102.8 9.1 %collective-permute-done.31.refs_5_ = bf16[80,3072]{1,0:T(8,128)(2,1)S(1)} collective-permute-done((bf16[80,3072]{1,0:T(8,128)(2,1)S(1)}, bf16[80,3072]{1,0:T(8,128)(2,1)S(1)}, u32[]{:S(2)}, u32[]{:S(2)}) %collective-permute-start.31) | collective-permute-done | bytes 491552 | tf_op jit(solution)/shard_map/ppermute | solution.py:30
  111.9 1.6 collective-permute-start.32
  113.5 3.6 %collective-permute-done.25.refs_4_ = bf16[80,3072]{1,0:T(8,128)(2,1)S(1)} collective-permute-done((bf16[80,3072]{1,0:T(8,128)(2,1)S(1)}, bf16[80,3072]{1,0:T(8,128)(2,1)S(1)}, u32[]{:S(2)}, u32[]{:S(2)}) %collective-permute-start.25) | collective-permute-done | bytes 491552 | tf_op jit(solution)/shard_map/ppermute | solution.py:30
  117.2 4.0 %collective-permute-start.18 = (bf16[80,3072]{1,0:T(8,128)(2,1)S(1)}, bf16[80,3072]{1,0:T(8,128)(2,1)S(1)}, u32[]{:S(2)}, u32[]{:S(2)}) collective-permute-start(bf16[80,3072]{1,0:T(8,128)(2,1)S(1)} %constant_dynamic-update-slice_fusion.10.refs_1_), channel_id=1, source_target_pairs={{0,24},{4,28},{8,0},{12,4},{16,8},{20,12},{24,16},{28,20},{32,56},... | collective-permute-start | bytes 1474568 | tf_op jit(solution)/shard_map/ppermute | solution.py:30
  121.3 9.6 %collective-permute-done.18.refs_3_ = bf16[80,3072]{1,0:T(8,128)(2,1)S(1)} collective-permute-done((bf16[80,3072]{1,0:T(8,128)(2,1)S(1)}, bf16[80,3072]{1,0:T(8,128)(2,1)S(1)}, u32[]{:S(2)}, u32[]{:S(2)}) %collective-permute-start.18) | collective-permute-done | bytes 491552 | tf_op jit(solution)/shard_map/ppermute | solution.py:30
  130.9 1.7 collective-permute-start.14
  132.7 2.3 collective-permute-done.29.refs_1_
  134.9 9.3 %collective-permute-done.14.refs_0_ = bf16[80,3072]{1,0:T(8,128)(2,1)S(1)} collective-permute-done((bf16[80,3072]{1,0:T(8,128)(2,1)S(1)}, bf16[80,3072]{1,0:T(8,128)(2,1)S(1)}, u32[]{:S(2)}, u32[]{:S(2)}) %collective-permute-start.14) | collective-permute-done | bytes 491552 | tf_op jit(solution)/shard_map/ppermute | solution.py:30
  144.7 1.6 collective-permute-start.15
  146.3 2.0 collective-permute-start.28
  148.3 5.4 %shard_map.140 = (f32[2,160,1024]{2,1,0:T(8,128)S(1)}, bf16[6144,1024]{1,0:T(8,128)(2,1)S(1)}) custom-call(bf16[80,3072]{1,0:T(8,128)(2,1)S(1)} %pad_maximum_fusion.refs_0_, bf16[80,3072]{1,0:T(8,128)(2,1)S(1)} %constant_dynamic-update-slice_fusion.10.refs_1_, bf16[80,3072]{1,0:T(8,128)(2,1)S(1)} %pad_maximum_fusion.1.refs_2_, ...), custom_call_target="tpu_custom_call" | custom-call | tf_op jit(solution)/shard_map/pallas_call | solution.py:325
  153.7 5.2 %shard_map.142 = (f32[2,320,1024]{2,1,0:T(8,128)S(1)}, f32[640,512]{1,0:T(8,128)S(1)}, f32[640,512]{1,0:T(8,128)S(1)}, bf16[512,6144]{1,0:T(8,128)(2,1)S(1)}) custom-call(bf16[80,3072]{1,0:T(8,128)(2,1)S(1)} %collective-permute-done.14.refs_0_, bf16[80,3072]{1,0:T(8,128)(2,1)S(1)} %collective-permute-done.29.refs_1_, ...), custom_call_target="tpu_custom_call" | custom-call | tf_op jit(solution)/shard_map/pallas_call | solution.py:325
  159.0 1.8 shard_map.141.late_a
  160.8 5.3 %shard_map.143 = (f32[640,512]{1,0:T(8,128)S(1)}, f32[640,512]{1,0:T(8,128)S(1)}, bf16[80,3072]{1,0:T(8,128)(2,1)S(1)}, bf16[80,3072]{1,0:T(8,128)(2,1)S(1)}, bf...) custom-call(f32[1,160,1024]{2,1,0:T(8,128)S(1)} %shard_map.141.late_a, ...), custom_call_target="tpu_custom_call", output_to_operand_aliasing={{0}: (7, {}), {1}: (8, {})} | custom-call | tf_op jit(solution)/shard_map/pallas_call | solution.py:325
  166.1 1.7 collective-permute-start.35
  167.8 5.5 %shard_map.144 = (bf16[80,3072]{1,0:T(8,128)(2,1)S(1)}, bf16[80,3072]{1,0:T(8,128)(2,1)S(1)}, bf16[80,3072]{1,0:T(8,128)(2,1)S(1)}, bf16[80,3072]{1,0:T(8,128)(2...) custom-call(f32[640,512]{1,0:T(8,128)S(1)} %get-tuple-element.48.hid, ...), custom_call_target="tpu_custom_call" | custom-call | tf_op jit(solution)/shard_map/pallas_call | solution.py:325
  174.8 2.2 collective-permute-start.38
  177.0 3.2 %collective-permute-start.44 = (bf16[80,3072]{1,0:T(8,128)(2,1)S(1)}, bf16[80,3072]{1,0:T(8,128)(2,1)S(1)}, u32[]{:S(2)}, u32[]{:S(2)}) collective-permute-start(bf16[80,3072]{1,0:T(8,128)(2,1)S(1)} %get-tuple-element.61), channel_id=1, source_target_pairs={{0,96},{4,100},{8,104},{12,108},{16,112},{20,116},{24,120},{28,124... | collective-permute-start | bytes 1474568 | tf_op jit(solution)/shard_map/ppermute | solution.py:30
  180.3 14.9 %collective-permute-done.39 = bf16[80,3072]{1,0:T(8,128)(2,1)S(1)} collective-permute-done((bf16[80,3072]{1,0:T(8,128)(2,1)S(1)}, bf16[80,3072]{1,0:T(8,128)(2,1)S(1)}, u32[]{:S(2)}, u32[]{:S(2)}) %collective-permute-start.39) | collective-permute-done | bytes 491552 | tf_op jit(solution)/shard_map/ppermute | solution.py:30
  195.4 3.3 %collective-permute-start.47 = (bf16[80,3072]{1,0:T(8,128)(2,1)S(1)}, bf16[80,3072]{1,0:T(8,128)(2,1)S(1)}, u32[]{:S(2)}, u32[]{:S(2)}) collective-permute-start(bf16[80,3072]{1,0:T(8,128)(2,1)S(1)} %get-tuple-element.63), channel_id=1, source_target_pairs={{0,96},{4,100},{8,104},{12,108},{16,112},{20,116},{24,120},{28,124... | collective-permute-start | bytes 1474568 | tf_op jit(solution)/shard_map/ppermute | solution.py:30
  198.8 6.9 %collective-permute-done.48 = bf16[80,3072]{1,0:T(8,128)(2,1)S(1)} collective-permute-done((bf16[80,3072]{1,0:T(8,128)(2,1)S(1)}, bf16[80,3072]{1,0:T(8,128)(2,1)S(1)}, u32[]{:S(2)}, u32[]{:S(2)}) %collective-permute-start.48) | collective-permute-done | bytes 491552 | tf_op jit(solution)/shard_map/ppermute | solution.py:30
  205.9 2.1 collective-permute-start.40
  208.0 6.6 %collective-permute-done.36 = bf16[80,3072]{1,0:T(8,128)(2,1)S(1)} collective-permute-done((bf16[80,3072]{1,0:T(8,128)(2,1)S(1)}, bf16[80,3072]{1,0:T(8,128)(2,1)S(1)}, u32[]{:S(2)}, u32[]{:S(2)}) %collective-permute-start.36) | collective-permute-done | bytes 491552 | tf_op jit(solution)/shard_map/ppermute | solution.py:30
  214.6 1.5 collective-permute-start.45
  216.9 2.7 %collective-permute-start.37 = (bf16[40,3072]{1,0:T(8,128)(2,1)S(1)}, bf16[40,3072]{1,0:T(8,128)(2,1)S(1)}, u32[]{:S(2)}, u32[]{:S(2)}) collective-permute-start(bf16[40,3072]{1,0:T(8,128)(2,1)S(1)} %slice.99), channel_id=1, source_target_pairs={{0,96},{4,100},{8,104},{12,108},{16,112},{20,116},{24,120},{28,124... | collective-permute-start | bytes 737288 | tf_op jit(solution)/shard_map/ppermute | solution.py:30
  219.9 7.2 %collective-permute-done.45 = bf16[80,3072]{1,0:T(8,128)(2,1)S(1)} collective-permute-done((bf16[80,3072]{1,0:T(8,128)(2,1)S(1)}, bf16[80,3072]{1,0:T(8,128)(2,1)S(1)}, u32[]{:S(2)}, u32[]{:S(2)}) %collective-permute-start.45) | collective-permute-done | bytes 491552 | tf_op jit(solution)/shard_map/ppermute | solution.py:30
  227.3 1.6 collective-permute-start.46
  228.9 3.3 %collective-permute-done.49 = bf16[80,3072]{1,0:T(8,128)(2,1)S(1)} collective-permute-done((bf16[80,3072]{1,0:T(8,128)(2,1)S(1)}, bf16[80,3072]{1,0:T(8,128)(2,1)S(1)}, u32[]{:S(2)}, u32[]{:S(2)}) %collective-permute-start.49) | collective-permute-done | bytes 491552 | tf_op jit(solution)/shard_map/ppermute | solution.py:30
  232.5 2.3 collective-permute-start.51
  235.0 5.3 %collective-permute-done.50 = bf16[40,3072]{1,0:T(8,128)(2,1)S(1)} collective-permute-done((bf16[40,3072]{1,0:T(8,128)(2,1)S(1)}, bf16[40,3072]{1,0:T(8,128)(2,1)S(1)}, u32[]{:S(2)}, u32[]{:S(2)}) %collective-permute-start.50) | collective-permute-done | bytes 245792 | tf_op jit(solution)/shard_map/ppermute | solution.py:30
  240.3 2.3 collective-permute-done.51
  243.6 3.5 %all-to-all-start.1 = ((bf16[4,40,1536]{2,1,0:T(8,128)(2,1)}), bf16[4,40,1536]{2,1,0:T(8,128)(2,1)S(1)}, u32[]{:S(2)}, u32[]{:S(2)}) async-start(bf16[4,40,1536]{2,1,0:T(8,128)(2,1)} %pad_maximum_fusion.2), calls=%async_computation.1 | async-start | bytes 983040 | tf_op jit(solution)/shard_map/all_to_all | solution.py:521
  247.3 7.6 %all-to-all-done.1 = bf16[4,40,1536]{2,1,0:T(8,128)(2,1)S(1)} async-done(((bf16[4,40,1536]{2,1,0:T(8,128)(2,1)}), bf16[4,40,1536]{2,1,0:T(8,128)(2,1)S(1)}, u32[]{:S(2)}, u32[]{:S(2)}) %all-to-all-start.1) | async-done | bytes 491552 | tf_op jit(solution)/shard_map/all_to_all | solution.py:521
  (115 shorter events, 20.9 us)
Async XLA Ops:
  2.2 6.0 %collective-permute-start = (bf16[128,256]{1,0:T(8,128)(2,1)S(1)}, bf16[128,256]{1,0:T(8,128)(2,1)S(1)}, u32[]{:S(2)}, u32[]{:S(2)}) collective-permute-start(bf16[128,256]{1,0:T(8,128)(2,1)S(1)} %get-tuple-element.80), channel_id=1, source_target_pairs={{0,32},{4,36},{8,40},{12,44},{16,48},{20,52},{24,56},{28,60},{32,6... | collective-permute-start | bytes 196616 | tf_op jit(solution)/shard_map/ppermute | solution.py:30
  3.9 6.1 %collective-permute-start.1 = (bf16[128,256]{1,0:T(8,128)(2,1)S(1)}, bf16[128,256]{1,0:T(8,128)(2,1)S(1)}, u32[]{:S(2)}, u32[]{:S(2)}) collective-permute-start(bf16[128,256]{1,0:T(8,128)(2,1)S(1)} %get-tuple-element.80), channel_id=1, source_target_pairs={{0,64},{4,68},{8,72},{12,76},{16,80},{20,84},{24,88},{28,92},{32,9... | collective-permute-start | bytes 196616 | tf_op jit(solution)/shard_map/ppermute | solution.py:30
  6.8 4.3 %collective-permute-start.2 = (bf16[128,256]{1,0:T(8,128)(2,1)S(1)}, bf16[128,256]{1,0:T(8,128)(2,1)S(1)}, u32[]{:S(2)}, u32[]{:S(2)}) collective-permute-start(bf16[128,256]{1,0:T(8,128)(2,1)S(1)} %get-tuple-element.80), channel_id=1, source_target_pairs={{0,96},{4,100},{8,104},{12,108},{16,112},{20,116},{24,120},{28,124... | collective-permute-start | bytes 196616 | tf_op jit(solution)/shard_map/ppermute | solution.py:30
  11.1 10.4 %collective-permute-start.3 = (bf16[512,256]{1,0:T(8,128)(2,1)S(1)}, bf16[512,256]{1,0:T(8,128)(2,1)S(1)}, u32[]{:S(2)}, u32[]{:S(2)}) collective-permute-start(bf16[512,256]{1,0:T(8,128)(2,1)S(1)} %pad_maximum_fusion.4), channel_id=1, source_target_pairs={{0,8},{4,12},{8,16},{12,20},{16,24},{20,28},{24,0},{28,4},{32,40},... | collective-permute-start | bytes 786440 | tf_op jit(solution)/shard_map/ppermute | solution.py:30
  13.1 13.8 %collective-permute-start.4 = (bf16[512,256]{1,0:T(8,128)(2,1)S(1)}, bf16[512,256]{1,0:T(8,128)(2,1)S(1)}, u32[]{:S(2)}, u32[]{:S(2)}) collective-permute-start(bf16[512,256]{1,0:T(8,128)(2,1)S(1)} %pad_maximum_fusion.4), channel_id=1, source_target_pairs={{0,16},{4,20},{8,24},{12,28},{16,0},{20,4},{24,8},{28,12},{32,48},... | collective-permute-start | bytes 786440 | tf_op jit(solution)/shard_map/ppermute | solution.py:30
  16.7 10.2 %collective-permute-start.5 = (bf16[512,256]{1,0:T(8,128)(2,1)S(1)}, bf16[512,256]{1,0:T(8,128)(2,1)S(1)}, u32[]{:S(2)}, u32[]{:S(2)}) collective-permute-start(bf16[512,256]{1,0:T(8,128)(2,1)S(1)} %pad_maximum_fusion.4), channel_id=1, source_target_pairs={{0,24},{4,28},{8,0},{12,4},{16,8},{20,12},{24,16},{28,20},{32,56},... | collective-permute-start | bytes 786440 | tf_op jit(solution)/shard_map/ppermute | solution.py:30
  27.0 2.7 %collective-permute-start.6 = (bf16[2048,256]{1,0:T(8,128)(2,1)S(1)}, bf16[2048,256]{1,0:T(8,128)(2,1)S(1)}, u32[]{:S(2)}, u32[]{:S(2)}) collective-permute-start(bf16[2048,256]{1,0:T(8,128)(2,1)S(1)} %constant_dynamic-update-slice_fusion.2.own_ref), channel_id=1, source_target_pairs={{0,4},{4,0},{8,12},{12,8},{16,20},{20,16},{24,28},{28,24},{32,36},... | collective-permute-start | bytes 3145736 | tf_op jit(solution)/shard_map/ppermute | solution.py:30
  36.3 8.6 %collective-permute-start.11 = (bf16[64,1536]{1,0:T(8,128)(2,1)}, bf16[64,1536]{1,0:T(8,128)(2,1)S(1)}, u32[]{:S(2)}, u32[]{:S(2)}) collective-permute-start(bf16[64,1536]{1,0:T(8,128)(2,1)} %get-tuple-element.41), channel_id=1, source_target_pairs={{0,1},{1,2},{2,3},{3,0},{4,5},{5,6},{6,7},{7,4},{8,9},{9,10},{10,1... | collective-permute-start | bytes 589832 | tf_op jit(solution)/shard_map/ppermute | solution.py:35
  37.9 22.5 %copy-start.1 = (f32[6144]{0:T(1024)S(1)}, f32[6144]{0:T(1024)}, u32[]{:S(2)}) copy-start(f32[6144]{0:T(1024)} %param.18) | copy-start | bytes 73732
  38.2 7.8 %collective-permute-start.8 = (bf16[64,1536]{1,0:T(8,128)(2,1)S(1)}, bf16[64,1536]{1,0:T(8,128)(2,1)S(1)}, u32[]{:S(2)}, u32[]{:S(2)}) collective-permute-start(bf16[64,1536]{1,0:T(8,128)(2,1)S(1)} %get-tuple-element.37), channel_id=1, source_target_pairs={{0,3},{1,0},{2,1},{3,2},{4,7},{5,4},{6,5},{7,6},{8,11},{9,8},{10,9... | collective-permute-start | bytes 589832 | tf_op jit(solution)/shard_map/ppermute | solution.py:35
  40.0 10.2 %collective-permute-start.10 = (bf16[64,1536]{1,0:T(8,128)(2,1)S(1)}, bf16[64,1536]{1,0:T(8,128)(2,1)S(1)}, u32[]{:S(2)}, u32[]{:S(2)}) collective-permute-start(bf16[64,1536]{1,0:T(8,128)(2,1)S(1)} %get-tuple-element.39), channel_id=1, source_target_pairs={{0,3},{1,0},{2,1},{3,2},{4,7},{5,4},{6,5},{7,6},{8,11},{9,8},{10,9... | collective-permute-start | bytes 589832 | tf_op jit(solution)/shard_map/ppermute | solution.py:35
  41.5 8.7 %collective-permute-start.7 = (bf16[64,1536]{1,0:T(8,128)(2,1)S(1)}, bf16[64,1536]{1,0:T(8,128)(2,1)S(1)}, u32[]{:S(2)}, u32[]{:S(2)}) collective-permute-start(bf16[64,1536]{1,0:T(8,128)(2,1)S(1)} %get-tuple-element.35), channel_id=1, source_target_pairs={{0,1},{1,2},{2,3},{3,0},{4,5},{5,6},{6,7},{7,4},{8,9},{9,10},{10,1... | collective-permute-start | bytes 589832 | tf_op jit(solution)/shard_map/ppermute | solution.py:35
  44.9 8.2 %collective-permute-start.12 = (bf16[64,1536]{1,0:T(8,128)(2,1)S(1)}, bf16[64,1536]{1,0:T(8,128)(2,1)S(1)}, u32[]{:S(2)}, u32[]{:S(2)}) collective-permute-start(bf16[64,1536]{1,0:T(8,128)(2,1)S(1)} %add_convert_fusion.11), channel_id=1, source_target_pairs={{0,1},{1,2},{2,3},{3,0},{4,5},{5,6},{6,7},{7,4},{8,9},{9,10},{10,1... | collective-permute-start | bytes 589832 | tf_op jit(solution)/shard_map/ppermute | solution.py:35
  46.0 7.3 %collective-permute-start.9 = (bf16[64,1536]{1,0:T(8,128)(2,1)S(1)}, bf16[64,1536]{1,0:T(8,128)(2,1)S(1)}, u32[]{:S(2)}, u32[]{:S(2)}) collective-permute-start(bf16[64,1536]{1,0:T(8,128)(2,1)S(1)} %add_convert_fusion.13), channel_id=1, source_target_pairs={{0,3},{1,0},{2,1},{3,2},{4,7},{5,4},{6,5},{7,6},{8,11},{9,8},{10,9... | collective-permute-start | bytes 589832 | tf_op jit(solution)/shard_map/ppermute | solution.py:35
  54.6 34.9 %copy-start = (bf16[128,1536]{1,0:T(8,128)(2,1)}, bf16[128,1536]{1,0:T(8,128)(2,1)S(1)}, u32[]{:S(2)}) copy-start(bf16[128,1536]{1,0:T(8,128)(2,1)S(1)} %pad_maximum_fusion.3) | copy-start | bytes 1179652
  55.7 12.3 %all-to-all-start = ((bf16[4,40,1536]{2,1,0:T(8,128)(2,1)}), bf16[4,40,1536]{2,1,0:T(8,128)(2,1)S(1)}, u32[]{:S(2)}, u32[]{:S(2)}) async-start(bf16[4,40,1536]{2,1,0:T(8,128)(2,1)} %bitcast.9), calls=%async_computation | async-start | bytes 983040 | tf_op jit(solution)/shard_map/all_to_all | solution.py:491
  59.9 86.4 %collective-permute-start.23 = (bf16[6144,256]{1,0:T(8,128)(2,1)}, bf16[6144,256]{1,0:T(8,128)(2,1)}, u32[]{:S(2)}, u32[]{:S(2)}) collective-permute-start(bf16[6144,256]{1,0:T(8,128)(2,1)} %bitcast.49), channel_id=1, source_target_pairs={{0,4},{4,0},{8,12},{12,8},{16,20},{20,16},{24,28},{28,24},{32,36},... | collective-permute-start | bytes 9437192 | tf_op jit(solution)/shard_map/ppermute | solution.py:30
  59.9 88.4 %collective-permute-start.24 = (bf16[6144,256]{1,0:T(8,128)(2,1)}, bf16[6144,256]{1,0:T(8,128)(2,1)}, u32[]{:S(2)}, u32[]{:S(2)}) collective-permute-start(bf16[6144,256]{1,0:T(8,128)(2,1)} %bitcast.51), channel_id=1, source_target_pairs={{0,4},{4,0},{8,12},{12,8},{16,20},{20,16},{24,28},{28,24},{32,36},... | collective-permute-start | bytes 9437192 | tf_op jit(solution)/shard_map/ppermute | solution.py:30
  60.4 93.3 %collective-permute-start.33 = (bf16[256,6144]{1,0:T(8,128)(2,1)}, bf16[256,6144]{1,0:T(8,128)(2,1)}, u32[]{:S(2)}, u32[]{:S(2)}) collective-permute-start(bf16[256,6144]{1,0:T(8,128)(2,1)} %bitcast.53), channel_id=1, source_target_pairs={{0,4},{4,0},{8,12},{12,8},{16,20},{20,16},{24,28},{28,24},{32,36},... | collective-permute-start | bytes 9437192 | tf_op jit(solution)/shard_map/ppermute | solution.py:30
  68.4 7.8 %collective-permute-start.21 = (bf16[40,3072]{1,0:T(8,128)(2,1)S(1)}, bf16[40,3072]{1,0:T(8,128)(2,1)S(1)}, u32[]{:S(2)}, u32[]{:S(2)}) collective-permute-start(bf16[40,3072]{1,0:T(8,128)(2,1)S(1)} %pad_maximum_fusion.6), channel_id=1, source_target_pairs={{0,16},{4,20},{8,24},{12,28},{16,0},{20,4},{24,8},{28,12},{32,48},... | collective-permute-start | bytes 737288 | tf_op jit(solution)/shard_map/ppermute | solution.py:30
  70.7 9.2 %collective-permute-start.22 = (bf16[40,3072]{1,0:T(8,128)(2,1)S(1)}, bf16[40,3072]{1,0:T(8,128)(2,1)S(1)}, u32[]{:S(2)}, u32[]{:S(2)}) collective-permute-start(bf16[40,3072]{1,0:T(8,128)(2,1)S(1)} %pad_maximum_fusion.6), channel_id=1, source_target_pairs={{0,24},{4,28},{8,0},{12,4},{16,8},{20,12},{24,16},{28,20},{32,56},... | collective-permute-start | bytes 737288 | tf_op jit(solution)/shard_map/ppermute | solution.py:30
  76.2 8.0 %collective-permute-start.20 = (bf16[40,3072]{1,0:T(8,128)(2,1)S(1)}, bf16[40,3072]{1,0:T(8,128)(2,1)S(1)}, u32[]{:S(2)}, u32[]{:S(2)}) collective-permute-start(bf16[40,3072]{1,0:T(8,128)(2,1)S(1)} %pad_maximum_fusion.6), channel_id=1, source_target_pairs={{0,8},{4,12},{8,16},{12,20},{16,24},{20,28},{24,0},{28,4},{32,40},... | collective-permute-start | bytes 737288 | tf_op jit(solution)/shard_map/ppermute | solution.py:30
  79.9 7.7 %collective-permute-start.16 = (bf16[40,3072]{1,0:T(8,128)(2,1)S(1)}, bf16[40,3072]{1,0:T(8,128)(2,1)S(1)}, u32[]{:S(2)}, u32[]{:S(2)}) collective-permute-start(bf16[40,3072]{1,0:T(8,128)(2,1)S(1)} %pad_maximum_fusion.5), channel_id=1, source_target_pairs={{0,64},{4,68},{8,72},{12,76},{16,80},{20,84},{24,88},{28,92},{32,9... | collective-permute-start | bytes 737288 | tf_op jit(solution)/shard_map/ppermute | solution.py:30
  84.2 8.3 %collective-permute-start.17 = (bf16[40,3072]{1,0:T(8,128)(2,1)S(1)}, bf16[40,3072]{1,0:T(8,128)(2,1)S(1)}, u32[]{:S(2)}, u32[]{:S(2)}) collective-permute-start(bf16[40,3072]{1,0:T(8,128)(2,1)S(1)} %pad_maximum_fusion.5), channel_id=1, source_target_pairs={{0,96},{4,100},{8,104},{12,108},{16,112},{20,116},{24,120},{28,124... | collective-permute-start | bytes 737288 | tf_op jit(solution)/shard_map/ppermute | solution.py:30
  87.7 9.7 %collective-permute-start.13 = (bf16[40,3072]{1,0:T(8,128)(2,1)S(1)}, bf16[40,3072]{1,0:T(8,128)(2,1)S(1)}, u32[]{:S(2)}, u32[]{:S(2)}) collective-permute-start(bf16[40,3072]{1,0:T(8,128)(2,1)S(1)} %pad_maximum_fusion.5), channel_id=1, source_target_pairs={{0,32},{4,36},{8,40},{12,44},{16,48},{20,52},{24,56},{28,60},{32,6... | collective-permute-start | bytes 737288 | tf_op jit(solution)/shard_map/ppermute | solution.py:30
  92.5 9.5 %collective-permute-start.27 = (bf16[80,3072]{1,0:T(8,128)(2,1)S(1)}, bf16[80,3072]{1,0:T(8,128)(2,1)S(1)}, u32[]{:S(2)}, u32[]{:S(2)}) collective-permute-start(bf16[80,3072]{1,0:T(8,128)(2,1)S(1)} %constant_dynamic-update-slice_fusion.12.refs_3_), channel_id=1, source_target_pairs={{0,96},{4,100},{8,104},{12,108},{16,112},{20,116},{24,120},{28,124... | collective-permute-start | bytes 1474568 | tf_op jit(solution)/shard_map/ppermute | solution.py:30
  97.3 14.6 %collective-permute-start.31 = (bf16[80,3072]{1,0:T(8,128)(2,1)S(1)}, bf16[80,3072]{1,0:T(8,128)(2,1)S(1)}, u32[]{:S(2)}, u32[]{:S(2)}) collective-permute-start(bf16[80,3072]{1,0:T(8,128)(2,1)S(1)} %constant_dynamic-update-slice_fusion.12.refs_3_), channel_id=1, source_target_pairs={{0,32},{4,36},{8,40},{12,44},{16,48},{20,52},{24,56},{28,60},{32,6... | collective-permute-start | bytes 1474568 | tf_op jit(solution)/shard_map/ppermute | solution.py:30
  102.0 15.2 %collective-permute-start.25 = (bf16[80,3072]{1,0:T(8,128)(2,1)S(1)}, bf16[80,3072]{1,0:T(8,128)(2,1)S(1)}, u32[]{:S(2)}, u32[]{:S(2)}) collective-permute-start(bf16[80,3072]{1,0:T(8,128)(2,1)S(1)} %pad_maximum_fusion.1.refs_2_), channel_id=1, source_target_pairs={{0,32},{4,36},{8,40},{12,44},{16,48},{20,52},{24,56},{28,60},{32,6... | collective-permute-start | bytes 1474568 | tf_op jit(solution)/shard_map/ppermute | solution.py:30
  111.9 9.3 %collective-permute-start.32 = (bf16[80,3072]{1,0:T(8,128)(2,1)S(1)}, bf16[80,3072]{1,0:T(8,128)(2,1)S(1)}, u32[]{:S(2)}, u32[]{:S(2)}) collective-permute-start(bf16[80,3072]{1,0:T(8,128)(2,1)S(1)} %pad_maximum_fusion.1.refs_2_), channel_id=1, source_target_pairs={{0,96},{4,100},{8,104},{12,108},{16,112},{20,116},{24,120},{28,124... | collective-permute-start | bytes 1474568 | tf_op jit(solution)/shard_map/ppermute | solution.py:30
  117.2 13.8 %collective-permute-start.18 = (bf16[80,3072]{1,0:T(8,128)(2,1)S(1)}, bf16[80,3072]{1,0:T(8,128)(2,1)S(1)}, u32[]{:S(2)}, u32[]{:S(2)}) collective-permute-start(bf16[80,3072]{1,0:T(8,128)(2,1)S(1)} %constant_dynamic-update-slice_fusion.10.refs_1_), channel_id=1, source_target_pairs={{0,24},{4,28},{8,0},{12,4},{16,8},{20,12},{24,16},{28,20},{32,56},... | collective-permute-start | bytes 1474568 | tf_op jit(solution)/shard_map/ppermute | solution.py:30
  121.2 13.7 %collective-permute-start.29 = (bf16[80,3072]{1,0:T(8,128)(2,1)S(1)}, bf16[80,3072]{1,0:T(8,128)(2,1)S(1)}, u32[]{:S(2)}, u32[]{:S(2)}) collective-permute-start(bf16[80,3072]{1,0:T(8,128)(2,1)S(1)} %constant_dynamic-update-slice_fusion.10.refs_1_), channel_id=1, source_target_pairs={{0,8},{4,12},{8,16},{12,20},{16,24},{20,28},{24,0},{28,4},{32,40},... | collective-permute-start | bytes 1474568 | tf_op jit(solution)/shard_map/ppermute | solution.py:30
  130.9 13.3 %collective-permute-start.14 = (bf16[80,3072]{1,0:T(8,128)(2,1)S(1)}, bf16[80,3072]{1,0:T(8,128)(2,1)S(1)}, u32[]{:S(2)}, u32[]{:S(2)}) collective-permute-start(bf16[80,3072]{1,0:T(8,128)(2,1)S(1)} %pad_maximum_fusion.refs_0_), channel_id=1, source_target_pairs={{0,8},{4,12},{8,16},{12,20},{16,24},{20,28},{24,0},{28,4},{32,40},... | collective-permute-start | bytes 1474568 | tf_op jit(solution)/shard_map/ppermute | solution.py:30
  134.9 9.7 %collective-permute-start.30 = (bf16[80,3072]{1,0:T(8,128)(2,1)S(1)}, bf16[80,3072]{1,0:T(8,128)(2,1)S(1)}, u32[]{:S(2)}, u32[]{:S(2)}) collective-permute-start(bf16[80,3072]{1,0:T(8,128)(2,1)S(1)} %pad_maximum_fusion.refs_0_), channel_id=1, source_target_pairs={{0,24},{4,28},{8,0},{12,4},{16,8},{20,12},{24,16},{28,20},{32,56},... | collective-permute-start | bytes 1474568 | tf_op jit(solution)/shard_map/ppermute | solution.py:30
  144.2 14.7 %collective-permute-start.19 = (bf16[80,3072]{1,0:T(8,128)(2,1)S(1)}, bf16[80,3072]{1,0:T(8,128)(2,1)S(1)}, u32[]{:S(2)}, u32[]{:S(2)}) collective-permute-start(bf16[80,3072]{1,0:T(8,128)(2,1)S(1)} %collective-permute-done.18.refs_3_), channel_id=1, source_target_pairs={{0,24},{4,28},{8,0},{12,4},{16,8},{20,12},{24,16},{28,20},{32,56},... | collective-permute-start | bytes 1474568 | tf_op jit(solution)/shard_map/ppermute | solution.py:30
  144.7 14.3 %collective-permute-start.15 = (bf16[80,3072]{1,0:T(8,128)(2,1)S(1)}, bf16[80,3072]{1,0:T(8,128)(2,1)S(1)}, u32[]{:S(2)}, u32[]{:S(2)}) collective-permute-start(bf16[80,3072]{1,0:T(8,128)(2,1)S(1)} %collective-permute-done.14.refs_0_), channel_id=1, source_target_pairs={{0,8},{4,12},{8,16},{12,20},{16,24},{20,28},{24,0},{28,4},{32,40},... | collective-permute-start | bytes 1474568 | tf_op jit(solution)/shard_map/ppermute | solution.py:30
  146.3 14.5 %collective-permute-start.28 = (bf16[80,3072]{1,0:T(8,128)(2,1)S(1)}, bf16[80,3072]{1,0:T(8,128)(2,1)S(1)}, u32[]{:S(2)}, u32[]{:S(2)}) collective-permute-start(bf16[80,3072]{1,0:T(8,128)(2,1)S(1)} %collective-permute-done.27.refs_7_), channel_id=1, source_target_pairs={{0,96},{4,100},{8,104},{12,108},{16,112},{20,116},{24,120},{28,124... | collective-permute-start | bytes 1474568 | tf_op jit(solution)/shard_map/ppermute | solution.py:30
  148.3 12.5 %collective-permute-start.26 = (bf16[80,3072]{1,0:T(8,128)(2,1)S(1)}, bf16[80,3072]{1,0:T(8,128)(2,1)S(1)}, u32[]{:S(2)}, u32[]{:S(2)}) collective-permute-start(bf16[80,3072]{1,0:T(8,128)(2,1)S(1)} %collective-permute-done.25.refs_4_), channel_id=1, source_target_pairs={{0,32},{4,36},{8,40},{12,44},{16,48},{20,52},{24,56},{28,60},{32,6... | collective-permute-start | bytes 1474568 | tf_op jit(solution)/shard_map/ppermute | solution.py:30
  166.1 14.1 %collective-permute-start.35 = (bf16[80,3072]{1,0:T(8,128)(2,1)S(1)}, bf16[80,3072]{1,0:T(8,128)(2,1)S(1)}, u32[]{:S(2)}, u32[]{:S(2)}) collective-permute-start(bf16[80,3072]{1,0:T(8,128)(2,1)S(1)} %get-tuple-element.53), channel_id=1, source_target_pairs={{0,24},{4,28},{8,0},{12,4},{16,8},{20,12},{24,16},{28,20},{32,56},... | collective-permute-start | bytes 1474568 | tf_op jit(solution)/shard_map/ppermute | solution.py:30
  173.3 32.6 %collective-permute-start.34 = (bf16[80,3072]{1,0:T(8,128)(2,1)S(1)}, bf16[80,3072]{1,0:T(8,128)(2,1)S(1)}, u32[]{:S(2)}, u32[]{:S(2)}) collective-permute-start(bf16[80,3072]{1,0:T(8,128)(2,1)S(1)} %get-tuple-element.51), channel_id=1, source_target_pairs={{0,8},{4,12},{8,16},{12,20},{16,24},{20,28},{24,0},{28,4},{32,40},... | collective-permute-start | bytes 1474568 | tf_op jit(solution)/shard_map/ppermute | solution.py:30
  173.7 21.5 %collective-permute-start.39 = (bf16[80,3072]{1,0:T(8,128)(2,1)S(1)}, bf16[80,3072]{1,0:T(8,128)(2,1)S(1)}, u32[]{:S(2)}, u32[]{:S(2)}) collective-permute-start(bf16[80,3072]{1,0:T(8,128)(2,1)S(1)} %get-tuple-element.57), channel_id=1, source_target_pairs={{0,8},{4,12},{8,16},{12,20},{16,24},{20,28},{24,0},{28,4},{32,40},... | collective-permute-start | bytes 1474568 | tf_op jit(solution)/shard_map/ppermute | solution.py:30
  174.8 41.5 %collective-permute-start.38 = (bf16[80,3072]{1,0:T(8,128)(2,1)S(1)}, bf16[80,3072]{1,0:T(8,128)(2,1)S(1)}, u32[]{:S(2)}, u32[]{:S(2)}) collective-permute-start(bf16[80,3072]{1,0:T(8,128)(2,1)S(1)} %get-tuple-element.55), channel_id=1, source_target_pairs={{0,24},{4,28},{8,0},{12,4},{16,8},{20,12},{24,16},{28,20},{32,56},... | collective-permute-start | bytes 1474568 | tf_op jit(solution)/shard_map/ppermute | solution.py:30
  177.0 18.4 %collective-permute-start.44 = (bf16[80,3072]{1,0:T(8,128)(2,1)S(1)}, bf16[80,3072]{1,0:T(8,128)(2,1)S(1)}, u32[]{:S(2)}, u32[]{:S(2)}) collective-permute-start(bf16[80,3072]{1,0:T(8,128)(2,1)S(1)} %get-tuple-element.61), channel_id=1, source_target_pairs={{0,96},{4,100},{8,104},{12,108},{16,112},{20,116},{24,120},{28,124... | collective-permute-start | bytes 1474568 | tf_op jit(solution)/shard_map/ppermute | solution.py:30
  180.2 39.6 %collective-permute-start.43 = (bf16[80,3072]{1,0:T(8,128)(2,1)S(1)}, bf16[80,3072]{1,0:T(8,128)(2,1)S(1)}, u32[]{:S(2)}, u32[]{:S(2)}) collective-permute-start(bf16[80,3072]{1,0:T(8,128)(2,1)S(1)} %get-tuple-element.59), channel_id=1, source_target_pairs={{0,32},{4,36},{8,40},{12,44},{16,48},{20,52},{24,56},{28,60},{32,6... | collective-permute-start | bytes 1474568 | tf_op jit(solution)/shard_map/ppermute | solution.py:30
  195.3 10.5 %collective-permute-start.48 = (bf16[80,3072]{1,0:T(8,128)(2,1)S(1)}, bf16[80,3072]{1,0:T(8,128)(2,1)S(1)}, u32[]{:S(2)}, u32[]{:S(2)}) collective-permute-start(bf16[80,3072]{1,0:T(8,128)(2,1)S(1)} %get-tuple-element.65), channel_id=1, source_target_pairs={{0,32},{4,36},{8,40},{12,44},{16,48},{20,52},{24,56},{28,60},{32,6... | collective-permute-start | bytes 1474568 | tf_op jit(solution)/shard_map/ppermute | solution.py:30
  195.4 31.9 %collective-permute-start.47 = (bf16[80,3072]{1,0:T(8,128)(2,1)S(1)}, bf16[80,3072]{1,0:T(8,128)(2,1)S(1)}, u32[]{:S(2)}, u32[]{:S(2)}) collective-permute-start(bf16[80,3072]{1,0:T(8,128)(2,1)S(1)} %get-tuple-element.63), channel_id=1, source_target_pairs={{0,96},{4,100},{8,104},{12,108},{16,112},{20,116},{24,120},{28,124... | collective-permute-start | bytes 1474568 | tf_op jit(solution)/shard_map/ppermute | solution.py:30
  205.7 8.8 %collective-permute-start.36 = (bf16[80,3072]{1,0:T(8,128)(2,1)S(1)}, bf16[80,3072]{1,0:T(8,128)(2,1)S(1)}, u32[]{:S(2)}, u32[]{:S(2)}) collective-permute-start(bf16[80,3072]{1,0:T(8,128)(2,1)S(1)} %add_convert_fusion.7), channel_id=1, source_target_pairs={{0,24},{4,28},{8,0},{12,4},{16,8},{20,12},{24,16},{28,20},{32,56},... | collective-permute-start | bytes 1474568 | tf_op jit(solution)/shard_map/ppermute | solution.py:30
  205.9 11.0 %collective-permute-start.40 = (bf16[80,3072]{1,0:T(8,128)(2,1)S(1)}, bf16[80,3072]{1,0:T(8,128)(2,1)S(1)}, u32[]{:S(2)}, u32[]{:S(2)}) collective-permute-start(bf16[80,3072]{1,0:T(8,128)(2,1)S(1)} %add_convert_fusion.5), channel_id=1, source_target_pairs={{0,8},{4,12},{8,16},{12,20},{16,24},{20,28},{24,0},{28,4},{32,40},... | collective-permute-start | bytes 1474568 | tf_op jit(solution)/shard_map/ppermute | solution.py:30
  214.6 12.5 %collective-permute-start.45 = (bf16[80,3072]{1,0:T(8,128)(2,1)S(1)}, bf16[80,3072]{1,0:T(8,128)(2,1)S(1)}, u32[]{:S(2)}, u32[]{:S(2)}) collective-permute-start(bf16[80,3072]{1,0:T(8,128)(2,1)S(1)} %add_convert_fusion.3), channel_id=1, source_target_pairs={{0,96},{4,100},{8,104},{12,108},{16,112},{20,116},{24,120},{28,124... | collective-permute-start | bytes 1474568 | tf_op jit(solution)/shard_map/ppermute | solution.py:30
  216.3 15.9 %collective-permute-start.49 = (bf16[80,3072]{1,0:T(8,128)(2,1)S(1)}, bf16[80,3072]{1,0:T(8,128)(2,1)S(1)}, u32[]{:S(2)}, u32[]{:S(2)}) collective-permute-start(bf16[80,3072]{1,0:T(8,128)(2,1)S(1)} %add_convert_fusion.1), channel_id=1, source_target_pairs={{0,32},{4,36},{8,40},{12,44},{16,48},{20,52},{24,56},{28,60},{32,6... | collective-permute-start | bytes 1474568 | tf_op jit(solution)/shard_map/ppermute | solution.py:30
  216.9 15.6 %collective-permute-start.37 = (bf16[40,3072]{1,0:T(8,128)(2,1)S(1)}, bf16[40,3072]{1,0:T(8,128)(2,1)S(1)}, u32[]{:S(2)}, u32[]{:S(2)}) collective-permute-start(bf16[40,3072]{1,0:T(8,128)(2,1)S(1)} %slice.99), channel_id=1, source_target_pairs={{0,96},{4,100},{8,104},{12,108},{16,112},{20,116},{24,120},{28,124... | collective-permute-start | bytes 737288 | tf_op jit(solution)/shard_map/ppermute | solution.py:30
  219.8 15.0 %collective-permute-start.41 = (bf16[40,3072]{1,0:T(8,128)(2,1)S(1)}, bf16[40,3072]{1,0:T(8,128)(2,1)S(1)}, u32[]{:S(2)}, u32[]{:S(2)}) collective-permute-start(bf16[40,3072]{1,0:T(8,128)(2,1)S(1)} %get-tuple-element.68), channel_id=1, source_target_pairs={{0,64},{4,68},{8,72},{12,76},{16,80},{20,84},{24,88},{28,92},{32,9... | collective-permute-start | bytes 737288 | tf_op jit(solution)/shard_map/ppermute | solution.py:30
  227.1 7.7 %collective-permute-start.42 = (bf16[40,3072]{1,0:T(8,128)(2,1)S(1)}, bf16[40,3072]{1,0:T(8,128)(2,1)S(1)}, u32[]{:S(2)}, u32[]{:S(2)}) collective-permute-start(bf16[40,3072]{1,0:T(8,128)(2,1)S(1)} %get-tuple-element.69), channel_id=1, source_target_pairs={{0,32},{4,36},{8,40},{12,44},{16,48},{20,52},{24,56},{28,60},{32,6... | collective-permute-start | bytes 737288 | tf_op jit(solution)/shard_map/ppermute | solution.py:30
  227.3 7.7 %collective-permute-start.46 = (bf16[40,3072]{1,0:T(8,128)(2,1)S(1)}, bf16[40,3072]{1,0:T(8,128)(2,1)S(1)}, u32[]{:S(2)}, u32[]{:S(2)}) collective-permute-start(bf16[40,3072]{1,0:T(8,128)(2,1)S(1)} %slice.105), channel_id=1, source_target_pairs={{0,24},{4,28},{8,0},{12,4},{16,8},{20,12},{24,16},{28,20},{32,56},... | collective-permute-start | bytes 737288 | tf_op jit(solution)/shard_map/ppermute | solution.py:30
  232.3 14.8 %copy-start.2 = (f32[128,2]{0,1:T(2,128)S(1)}, f32[128,2]{0,1:T(2,128)}, u32[]{:S(2)}) copy-start(f32[128,2]{0,1:T(2,128)} %param.22) | copy-start | bytes 3076
  232.4 7.9 %collective-permute-start.50 = (bf16[40,3072]{1,0:T(8,128)(2,1)S(1)}, bf16[40,3072]{1,0:T(8,128)(2,1)S(1)}, u32[]{:S(2)}, u32[]{:S(2)}) collective-permute-start(bf16[40,3072]{1,0:T(8,128)(2,1)S(1)} %get-tuple-element.70), channel_id=1, source_target_pairs={{0,16},{4,20},{8,24},{12,28},{16,0},{20,4},{24,8},{28,12},{32,48},... | collective-permute-start | bytes 737288 | tf_op jit(solution)/shard_map/ppermute | solution.py:30
  232.5 10.1 %collective-permute-start.51 = (bf16[40,3072]{1,0:T(8,128)(2,1)S(1)}, bf16[40,3072]{1,0:T(8,128)(2,1)S(1)}, u32[]{:S(2)}, u32[]{:S(2)}) collective-permute-start(bf16[40,3072]{1,0:T(8,128)(2,1)S(1)} %get-tuple-element.71), channel_id=1, source_target_pairs={{0,8},{4,12},{8,16},{12,20},{16,24},{20,28},{24,0},{28,4},{32,40},... | collective-permute-start | bytes 737288 | tf_op jit(solution)/shard_map/ppermute | solution.py:30
  243.6 11.3 %all-to-all-start.1 = ((bf16[4,40,1536]{2,1,0:T(8,128)(2,1)}), bf16[4,40,1536]{2,1,0:T(8,128)(2,1)S(1)}, u32[]{:S(2)}, u32[]{:S(2)}) async-start(bf16[4,40,1536]{2,1,0:T(8,128)(2,1)} %pad_maximum_fusion.2), calls=%async_computation.1 | async-start | bytes 983040 | tf_op jit(solution)/shard_map/all_to_all | solution.py:521
